TPU v7x, 128 devices: a whole 4x4x4 slice. The times are simulated.
128 devices in a mesh: dp: 8 (over y, core), tensor: 16 (over x, z).
Axes of the slice: x: 4, y: 4, z: 4, core: 2. Of those that a mesh axis runs over, the one named last changes fastest.
Arguments:
- ref_hidden: bfloat16 [2304, 4608], P('dp', 'tensor'), may hold values from -6 to 6
- pol_hidden: bfloat16 [2304, 4608], P('dp', 'tensor'), may hold values from -6 to 6
- readout: bfloat16 [2304, 4608], P('dp', 'tensor'), may hold values from -0.019897461 to 0.019897461
- lengths: int32 [24], P('dp'), may hold values from 16 to 96, as said below
- pairing: int32 [24], replicated, may hold values from 0 to 23, each once
- pre_gain: float32 [4608], replicated, may hold values from 0.25 to 1.75
- post_gain: float32 [4608], replicated, may hold values from 0.25 to 1.75
- w_query: bfloat16 [4608, 4096], P('dp', 'tensor'), may hold values from -0.09375 to 0.09375
- w_key: bfloat16 [4608, 2048], P('dp', 'tensor'), may hold values from -3 to 3
- value_projection: bfloat16 [4608, 2048], P('dp', 'tensor'), may hold values from -0.09375 to 0.09375
- w_out: bfloat16 [4608, 4096], P('dp', 'tensor'), may hold values from -0.09375 to 0.09375
- a_query: bfloat16 [4608, 64], P('dp'), may hold values from -0.09375 to 0.09375
- a_value: bfloat16 [4608, 64], P('dp'), may hold values from -0.09375 to 0.09375
- query_second_factor: bfloat16 [64, 4096], P(None, 'tensor'), may hold values from -0.75 to 0.75
- value_second_factor: bfloat16 [64, 2048], P(None, 'tensor'), may hold values from -0.75 to 0.75
Outputs:
- policy_out: bfloat16 [2304, 4608], P('dp', 'tensor')
- reference_out: bfloat16 [2304, 4608], P('dp', 'tensor')
- dpo_loss: float32 [], replicated
- grad_hidden: bfloat16 [2304, 4608], P('dp', 'tensor')
- grad_a: float32 [4608, 128], P('dp')
- query_factor_gradient: float32 [64, 4096], P(None, 'tensor')
- value_factor_gradient: float32 [64, 2048], P(None, 'tensor')
Inputs may be any that keep to these rules, and one draw needn't show every extreme that they name: `lengths`: every sequence has at least one valid token and some sequence is full. `pairing`: entries 2k and 2k + 1 name the chosen and the rejected sequence of pair k; every sequence appears once.
All inputs are finite; a program needn't handle non-finite values.
Results may differ from a plain program's by a relative error of at most 0.0233.
The roundings to bfloat16 on the way count: a program that leaves them out, or rounds other values in their place, can miss the bound.
Values may be sent and summed in bfloat16 or wider, within the bound.
A program may use at most 128 MiB of HBM per device.

v0:
```python
import functools

import jax
import jax.numpy as jnp
from jax import lax
from jax.sharding import Mesh
from jax.sharding import PartitionSpec as P

MODEL_WIDTH = 4608
HQ = 32
HEAD_SIZE = 128
TENSOR = ("tensor_0", "tensor_1")
DP = ("dp_0", "dp_1")
DP_TENSOR = ("dp_0", "dp_1", "tensor_0", "tensor_1")


NORM_EPS = 1e-06
SOFT_CAP = 50.0
ADAPTER_SCALE = 0.5
DPO_BETA = 0.5
LOSS_SCALE = 256.0
ROPE_BASE = 10000.0


def one_axis_at_a_time(shard, axes):
    return functools.reduce(lax.psum, axes, shard)


def copy_for_each(shard, axis):
    count = lax.axis_size(axis)
    return lax.all_to_all(
        jnp.broadcast_to(shard[None], (count, *shard.shape)), axis, 0, 0, tiled=True
    )


def in_order(tiles, dim):
    shape = list(tiles.shape[1:])
    shape[dim] *= tiles.shape[0]
    return jnp.moveaxis(tiles, 0, dim).reshape(shape)


def collect(shard, axis, dim):
    tiles = copy_for_each(shard, axis)
    return in_order(tiles, dim)


def split_up(shard, dim, count):
    shape = shard.shape
    tiles = shard.reshape(*shape[:dim], count, shape[dim] // count, *shape[dim + 1 :])
    return jnp.moveaxis(tiles, dim, 0)


def summed_on_arrival(shard, axis, dim):
    tiles = split_up(shard, dim, lax.axis_size(axis))
    arrived = lax.all_to_all(tiles, axis, split_axis=0, concat_axis=0, tiled=True)
    return arrived.astype(jnp.float32).sum(axis=0)


def sent_together(arrays, axis, dim, along):
    ends, at = ([], 0)
    for a in arrays[:-1]:
        at += a.shape[along]
        ends.append(at)
    both = jnp.concatenate(arrays, axis=along)
    return tuple(jnp.split(lax.all_gather(both, axis, axis=dim, tiled=True), ends, axis=along))


def over_copies(shard, axis):
    return copy_for_each(shard, axis).astype(jnp.float32).sum(axis=0)


def query_scale():
    return float(MODEL_WIDTH // HQ) ** (-0.5)


def apply_rotation(value_rows, direction):
    length = value_rows.shape[1]
    head_depth = value_rows.shape[3]
    middle = head_depth // 2
    spacing = ROPE_BASE ** (-2.0 * jnp.arange(middle, dtype=jnp.float32) / head_depth)
    angles = jnp.arange(length, dtype=jnp.float32)[:, None] * spacing[None, :]
    cosine = jnp.cos(angles)[None, :, None, :]
    sine_part = direction * jnp.sin(angles)[None, :, None, :]
    leading = value_rows[..., :middle]
    trailing = value_rows[..., middle:]
    return jnp.concatenate(
        [leading * cosine - trailing * sine_part, trailing * cosine + leading * sine_part], axis=-1
    )


def allowed_mask(lengths, length):
    places = jnp.arange(length)
    causal = places[None, :] <= places[:, None]
    living = places[None, :] < lengths[:, None]
    return causal[None, None, None, :, :] & living[:, None, None, None, :]


def attend(query_rows, rotated_keys, value_rows, lengths):
    seqs_here, length, q_heads, head_depth = query_rows.shape
    kv_heads = rotated_keys.shape[2]
    grouped_heads = query_rows.reshape(seqs_here, length, kv_heads, q_heads // kv_heads, head_depth)
    scores = (
        jnp.einsum(
            "sqkgd,spkd->skgqp", grouped_heads, rotated_keys, preferred_element_type=jnp.float32
        )
        * query_scale()
    )
    capped = SOFT_CAP * jnp.tanh(scores / SOFT_CAP)
    allowed = allowed_mask(lengths, length)
    weights = jnp.where(allowed, jnp.exp(capped), 0.0)
    probabilities = weights / jnp.sum(weights, axis=-1, keepdims=True)
    probs_low = probabilities.astype(jnp.bfloat16)
    mixed_out = jnp.einsum(
        "skgqp,spkd->sqkgd", probs_low, value_rows, preferred_element_type=jnp.float32
    )
    return (
        mixed_out.astype(jnp.bfloat16).reshape(seqs_here, length, q_heads, head_depth),
        probs_low,
        probabilities,
        capped,
    )


def attend_back(grad_mixed, query_rows, rotated_keys, value_rows, probs_low, probabilities, capped):
    seqs_here, length, q_heads, head_depth = query_rows.shape
    kv_heads = rotated_keys.shape[2]
    shape_five = (seqs_here, length, kv_heads, q_heads // kv_heads, head_depth)
    grouped_heads = query_rows.reshape(shape_five)
    grad_grouped = grad_mixed.reshape(shape_five)
    grad_probs = jnp.einsum(
        "sqkgd,spkd->skgqp", grad_grouped, value_rows, preferred_element_type=jnp.float32
    )
    value_rows_gradient = jnp.einsum(
        "skgqp,sqkgd->spkd", probs_low, grad_grouped, preferred_element_type=jnp.float32
    )
    centered = grad_probs - jnp.sum(grad_probs * probabilities, axis=-1, keepdims=True)
    grad_scores = (
        probabilities * centered * (1.0 - (capped / SOFT_CAP) ** 2) * query_scale()
    ).astype(jnp.bfloat16)
    query_rows_gradient = jnp.einsum(
        "skgqp,spkd->sqkgd", grad_scores, rotated_keys, preferred_element_type=jnp.float32
    ).reshape(seqs_here, length, q_heads, head_depth)
    key_rows_gradient = jnp.einsum(
        "skgqp,sqkgd->spkd", grad_scores, grouped_heads, preferred_element_type=jnp.float32
    )
    return (query_rows_gradient, key_rows_gradient, value_rows_gradient)


def normalize(hidden, pre_gain, pre_local):
    narrow = hidden.astype(jnp.float32)
    squares = one_axis_at_a_time(jnp.sum(narrow * narrow, axis=1), TENSOR)
    pre_scale = lax.rsqrt(squares[:, None] / pre_gain.shape[0] + NORM_EPS)
    normed = collect((narrow * pre_scale * pre_local).astype(jnp.bfloat16), TENSOR, 1)
    return (normed, pre_scale)


def attention_layer(hidden, normed, weights, adapters, lengths, post_local):
    w_query, w_key, value_projection, w_out, a_query, a_value = weights
    tok_rows, full_width = normed.shape
    seqs_here = lengths.shape[0]
    length = tok_rows // seqs_here
    query_rows = jnp.dot(normed, w_query, preferred_element_type=jnp.float32)
    keys_before_rotation = jnp.dot(normed, w_key, preferred_element_type=jnp.float32)
    value_rows = jnp.dot(normed, value_projection, preferred_element_type=jnp.float32)
    low_rank_update = None
    if adapters is not None:
        query_second_factor, value_second_factor = adapters
        rank_size = query_second_factor.shape[0]
        low_rank_update = jnp.dot(
            normed, jnp.concatenate([a_query, a_value], axis=1), preferred_element_type=jnp.float32
        ).astype(jnp.bfloat16)
        query_rows = query_rows + ADAPTER_SCALE * jnp.dot(
            low_rank_update[:, :rank_size], query_second_factor, preferred_element_type=jnp.float32
        )
        value_rows = value_rows + ADAPTER_SCALE * jnp.dot(
            low_rank_update[:, rank_size:], value_second_factor, preferred_element_type=jnp.float32
        )
    q_heads = query_rows.shape[1] // HEAD_SIZE
    kv_heads = keys_before_rotation.shape[1] // HEAD_SIZE
    query_rows = apply_rotation(
        query_rows.reshape(seqs_here, length, q_heads, HEAD_SIZE), 1.0
    ).astype(jnp.bfloat16)
    rotated_keys = apply_rotation(
        keys_before_rotation.reshape(seqs_here, length, kv_heads, HEAD_SIZE), 1.0
    ).astype(jnp.bfloat16)
    value_rows = value_rows.reshape(seqs_here, length, kv_heads, HEAD_SIZE).astype(jnp.bfloat16)
    mixed_out, probs_low, probabilities, capped = attend(
        query_rows, rotated_keys, value_rows, lengths
    )
    head_terms = lax.dot_general(
        mixed_out.reshape(tok_rows, q_heads * HEAD_SIZE),
        w_out,
        (((1,), (1,)), ((), ())),
        preferred_element_type=jnp.float32,
    )
    summed = summed_on_arrival(head_terms.astype(jnp.bfloat16), TENSOR, 1)
    squares = one_axis_at_a_time(jnp.sum(summed * summed, axis=1), TENSOR)
    post_scale = lax.rsqrt(squares[:, None] / full_width + NORM_EPS)
    result = hidden.astype(jnp.float32) + summed * post_scale * post_local
    saved = (
        low_rank_update,
        query_rows,
        rotated_keys,
        value_rows,
        probs_low,
        probabilities,
        capped,
        summed,
        post_scale,
    )
    return (result, saved)


def body(
    ref_hidden,
    pol_hidden,
    readout,
    lengths,
    pairing,
    pre_gain,
    post_gain,
    w_query,
    w_key,
    value_projection,
    w_out,
    a_query,
    a_value,
    query_second_factor,
    value_second_factor,
):
    tok_rows, part_width = pol_hidden.shape
    seqs_here = lengths.shape[0]
    length = tok_rows // seqs_here
    tensor_rank = lax.axis_index(TENSOR)
    data_rank = lax.axis_index(DP)
    all_seqs = seqs_here * lax.axis_size(DP)
    full_width = part_width * lax.axis_size(TENSOR)
    pre_local = lax.dynamic_slice_in_dim(pre_gain, tensor_rank * part_width, part_width)
    post_local = lax.dynamic_slice_in_dim(post_gain, tensor_rank * part_width, part_width)
    weights = sent_together((w_query, w_key, value_projection, w_out, a_query, a_value), DP, 0, 1)
    w_query_all, w_key_all, w_value_all, w_out_all, a_query_all, a_value_all = weights
    ref_normed, ref_scale = normalize(ref_hidden, pre_gain, pre_local)
    ref_result, ref_saved = attention_layer(
        ref_hidden, ref_normed, weights, None, lengths, post_local
    )
    pol_normed, pol_scale = normalize(pol_hidden, pre_gain, pre_local)
    pol_result, pol_saved = attention_layer(
        pol_hidden,
        pol_normed,
        weights,
        (query_second_factor, value_second_factor),
        lengths,
        post_local,
    )
    readout_wide = readout.astype(jnp.float32)
    living = (jnp.arange(length)[None, :] < lengths[:, None]).astype(jnp.float32)

    def sequence_score(result):
        return jnp.sum(
            jnp.sum(result * readout_wide, axis=1).reshape(seqs_here, length) * living, axis=1
        )

    placed = jnp.zeros((2, all_seqs), jnp.float32)
    offset = data_rank * seqs_here
    placed = lax.dynamic_update_slice(
        placed,
        jnp.stack([sequence_score(ref_result), sequence_score(pol_result)]),
        (jnp.int32(0), offset),
    )
    scores = one_axis_at_a_time(placed, DP_TENSOR)
    ratios = scores[1] - scores[0]
    chooser = (pairing[:, None] == jnp.arange(all_seqs)[None, :]).astype(jnp.float32)
    picked = jnp.dot(chooser, ratios, precision=lax.Precision.HIGHEST).reshape(-1, 2)
    margins = DPO_BETA * (picked[:, 0] - picked[:, 1])
    dpo_loss = jnp.sum(jax.nn.softplus(-margins))
    pair_pull = DPO_BETA * LOSS_SCALE * jax.nn.sigmoid(-margins)
    signed = jnp.stack([-pair_pull, pair_pull], axis=1).reshape(-1)
    coefficients = jnp.dot(signed, chooser, precision=lax.Precision.HIGHEST)
    local_coef = lax.dynamic_slice_in_dim(coefficients, offset, seqs_here)
    grad_result = (local_coef[:, None] * living).reshape(tok_rows, 1) * readout_wide
    (
        low_rank_update,
        query_rows,
        rotated_keys,
        value_rows,
        probs_low,
        probabilities,
        capped,
        summed,
        post_scale,
    ) = pol_saved
    post_dot = one_axis_at_a_time(jnp.sum(summed * post_local * grad_result, axis=1), TENSOR)
    grad_summed = (
        post_scale * post_local * grad_result
        - summed * post_scale**3 * post_dot[:, None] / full_width
    )
    grad_wide = collect(grad_summed.astype(jnp.bfloat16), TENSOR, 1)
    grad_mixed = jnp.dot(grad_wide, w_out_all, preferred_element_type=jnp.float32).astype(
        jnp.bfloat16
    )
    q_heads = query_rows.shape[2]
    grad_q_rot, rotated_key_gradient, value_head_gradient = attend_back(
        grad_mixed.reshape(seqs_here, length, q_heads, HEAD_SIZE),
        query_rows,
        rotated_keys,
        value_rows,
        probs_low,
        probabilities,
        capped,
    )
    query_rows_gradient = (
        apply_rotation(grad_q_rot, -1.0).reshape(tok_rows, -1).astype(jnp.bfloat16)
    )
    key_rows_gradient = (
        apply_rotation(rotated_key_gradient, -1.0).reshape(tok_rows, -1).astype(jnp.bfloat16)
    )
    value_rows_gradient = value_head_gradient.reshape(tok_rows, -1).astype(jnp.bfloat16)
    rank_size = query_second_factor.shape[0]
    rows_contraction = (((0,), (0,)), ((), ()))
    contract_cols = (((1,), (1,)), ((), ()))
    query_adapter_term = ADAPTER_SCALE * lax.dot_general(
        low_rank_update[:, :rank_size],
        query_rows_gradient,
        rows_contraction,
        preferred_element_type=jnp.float32,
    )
    value_adapter_term = ADAPTER_SCALE * lax.dot_general(
        low_rank_update[:, rank_size:],
        value_rows_gradient,
        rows_contraction,
        preferred_element_type=jnp.float32,
    )
    query_factor_gradient, value_factor_gradient = (
        over_copies(query_adapter_term.astype(jnp.bfloat16), DP).astype(jnp.float32),
        over_copies(value_adapter_term.astype(jnp.bfloat16), DP).astype(jnp.float32),
    )
    adapter_grad = jnp.concatenate(
        [
            ADAPTER_SCALE
            * lax.dot_general(
                query_rows_gradient,
                query_second_factor,
                contract_cols,
                preferred_element_type=jnp.float32,
            ),
            ADAPTER_SCALE
            * lax.dot_general(
                value_rows_gradient,
                value_second_factor,
                contract_cols,
                preferred_element_type=jnp.float32,
            ),
        ],
        axis=1,
    ).astype(jnp.bfloat16)
    adapter_term = lax.dot_general(
        pol_normed, adapter_grad, rows_contraction, preferred_element_type=jnp.float32
    )
    adapter_part = summed_on_arrival(adapter_term.astype(jnp.bfloat16), DP, 0)
    grad_a = lax.psum(adapter_part.astype(jnp.bfloat16), TENSOR).astype(jnp.float32)
    a_both = jnp.concatenate([a_query_all, a_value_all], axis=1)
    input_terms = lax.dot_general(
        query_rows_gradient, w_query_all, contract_cols, preferred_element_type=jnp.float32
    )
    input_terms = input_terms + lax.dot_general(
        key_rows_gradient, w_key_all, contract_cols, preferred_element_type=jnp.float32
    )
    input_terms = input_terms + lax.dot_general(
        value_rows_gradient, w_value_all, contract_cols, preferred_element_type=jnp.float32
    )
    input_terms = input_terms + lax.dot_general(
        adapter_grad, a_both, contract_cols, preferred_element_type=jnp.float32
    )
    input_whole = lax.psum(input_terms.astype(jnp.bfloat16), TENSOR).astype(jnp.float32)
    grad_normed = lax.dynamic_slice_in_dim(input_whole, tensor_rank * part_width, part_width, 1)
    narrow = pol_hidden.astype(jnp.float32)
    pre_dot = one_axis_at_a_time(jnp.sum(narrow * pre_local * grad_normed, axis=1), TENSOR)
    grad_hidden = (
        grad_result
        + pol_scale * pre_local * grad_normed
        - narrow * pol_scale**3 * pre_dot[:, None] / full_width
    )
    return (
        pol_result.astype(jnp.bfloat16),
        ref_result.astype(jnp.bfloat16),
        dpo_loss,
        grad_hidden.astype(jnp.bfloat16),
        grad_a,
        query_factor_gradient,
        value_factor_gradient,
    )


def solution(mesh):
    torus = Mesh(mesh.devices.reshape(4, 2, 4, 4), ("dp_0", "dp_1", "tensor_0", "tensor_1"))
    placed = (
        P(DP, TENSOR),
        P(DP, TENSOR),
        P(DP, TENSOR),
        P(DP),
        P(),
        P(),
        P(),
        P(DP, TENSOR),
        P(DP, TENSOR),
        P(DP, TENSOR),
        P(DP, TENSOR),
        P(DP, None),
        P(DP, None),
        P(None, TENSOR),
        P(None, TENSOR),
    )
    return jax.shard_map(
        body,
        mesh=torus,
        in_specs=placed,
        out_specs=(
            P(DP, TENSOR),
            P(DP, TENSOR),
            P(),
            P(DP, TENSOR),
            P(DP, None),
            P(None, TENSOR),
            P(None, TENSOR),
        ),
        check_vma=False,
    )
```

profile of v0, /device:TPU:0, one launch (start us, length us, event | category | flops | bytes accessed | tf_op | source)
XLA Modules:
  0.0 563.7 jit_solution(11571863054451459790)
XLA Ops:
  9.4 3.2 concatenate.55
  13.6 10.6 %all-reduce.3 = (f32[288]{0:T(512)S(1)}, f32[288]{0:T(512)S(1)}) all-reduce(f32[288]{0:T(512)S(1)} %get-tuple-element.60, f32[288]{0:T(512)S(1)} %get-tuple-element.59), channel_id=1, replica_groups=mesh['dp_0'=4,'dp_1'=2,'tensor_0'=4,'tensor_1'=4] {'tensor_0'}, use_global_device_ids=true, to_apply=%region_1.0 | all-reduce | flops 576 | bytes 4608 | tf_op jit(solution)/shard_map/psum | solution.py:26
  24.2 11.7 %all-reduce.1 = (f32[288]{0:T(512)S(1)}, f32[288]{0:T(512)S(1)}) all-reduce(f32[288]{0:T(512)S(1)} %get-tuple-element.17, f32[288]{0:T(512)S(1)} %get-tuple-element.18), channel_id=1, replica_groups=mesh['dp_0'=4,'dp_1'=2,'tensor_0'=4,'tensor_1'=4] {'tensor_1'}, use_global_device_ids=true, to_apply=%region_2.0 | all-reduce | flops 576 | bytes 4608 | tf_op jit(solution)/shard_map/psum | solution.py:26
  37.0 43.5 %all_to_all.40 = bf16[16,288,288]{2,1,0:T(8,128)(2,1)} all-to-all(bf16[16,288,288]{2,1,0:T(8,128)(2,1)S(1)} %broadcast_in_dim.31), channel_id=1, replica_groups=mesh['dp_0'=4,'dp_1'=2,'tensor_0'=4,'tensor_1'=4] {'tensor_0','tensor_1'}, dimensions={0} | all-to-all | bytes 5308416 | tf_op jit(solution)/shard_map/all_to_all | solution.py:31
  80.6 2.1 broadcast_in_dim.24
  82.7 4.6 all-to-all-start
  89.0 5.1 copy.96
  94.2 6.7 %dot_general.122 = bf16[3,96,4608]{2,1,0:T(8,128)(2,1)} reshape(bf16[288,16,288]{2,1,0:T(8,128)(2,1)} %copy.96) | data formatting | bytes 5308416 | tf_op jit(solution)/shard_map/dot_general | solution.py:164
  100.8 6.6 %reshape.391 = bf16[3,96,4608,1]{2,1,0,3:T(8,128)(2,1)} reshape(bf16[288,16,288]{2,1,0:T(8,128)(2,1)} %copy.96) | data formatting | bytes 5308416 | tf_op jit(solution)/shard_map/dot_general | solution.py:164
  107.5 21.0 %all-to-all-done = bf16[16,288,288]{2,1,0:T(8,128)(2,1)} async-done(((bf16[16,288,288]{2,1,0:T(8,128)(2,1)}), bf16[16,288,288]{2,1,0:T(8,128)(2,1)}, u32[]{:S(2)}, u32[]{:S(2)}) %all-to-all-start) | async-done | bytes 2654240 | tf_op jit(solution)/shard_map/all_to_all | solution.py:31
  128.5 5.1 copy.87
  133.5 5.6 reshape.369
  139.1 7.2 %dot_general.114 = bf16[3,96,4608]{2,1,0:T(8,128)(2,1)} reshape(bf16[288,16,288]{2,1,0:T(8,128)(2,1)} %copy.87) | data formatting | bytes 5308416 | tf_op jit(solution)/shard_map/dot_general | solution.py:163
  146.3 3.2 slice_bitcast_fusion
  149.5 4.5 copy.119
  154.0 2.1 convolution_convert_fusion.5
  157.0 2.5 fusion.9
  161.9 3.5 fusion.1
  165.4 2.3 fusion.32
  167.7 2.1 fusion.29
  172.7 2.2 fusion.35
  175.6 2.5 convolution_convert_fusion.1
  178.2 5.9 %reshape.372 = bf16[288,16,288]{2,1,0:T(8,128)(2,1)} reshape(bf16[288,4608]{1,0:T(8,128)(2,1)S(1)} %convolution_convert_fusion.1) | data formatting | bytes 5308416 | tf_op jit(solution)/shard_map/reshape | solution.py:49
  184.0 4.5 copy.158
  188.6 9.0 %all-to-all-start.1 = ((bf16[16,288,288]{2,1,0:T(8,128)(2,1)}), bf16[16,288,288]{2,1,0:T(8,128)(2,1)}, u32[]{:S(2)}, u32[]{:S(2)}) async-start(bf16[16,288,288]{2,1,0:T(8,128)(2,1)} %bitcast.230), calls=%async_computation.1 | async-start | bytes 7077888 | tf_op jit(solution)/shard_map/all_to_all | solution.py:55
  197.6 2.6 fusion.136
  200.2 2.4 fusion.28
  202.8 2.5 convolution_convert_fusion
  205.3 5.9 %reshape.374 = bf16[288,16,288]{2,1,0:T(8,128)(2,1)} reshape(bf16[288,4608]{1,0:T(8,128)(2,1)S(1)} %convolution_convert_fusion) | data formatting | bytes 5308416 | tf_op jit(solution)/shard_map/reshape | solution.py:49
  211.2 4.6 copy.157
  215.8 25.3 %all-to-all-done.1 = bf16[16,288,288]{2,1,0:T(8,128)(2,1)} async-done(((bf16[16,288,288]{2,1,0:T(8,128)(2,1)}), bf16[16,288,288]{2,1,0:T(8,128)(2,1)}, u32[]{:S(2)}, u32[]{:S(2)}) %all-to-all-start.1) | async-done | bytes 2654240 | tf_op jit(solution)/shard_map/all_to_all | solution.py:55
  241.1 6.2 %all-to-all-start.3 = ((bf16[16,288,288]{2,1,0:T(8,128)(2,1)}), bf16[16,288,288]{2,1,0:T(8,128)(2,1)}, u32[]{:S(2)}, u32[]{:S(2)}) async-start(bf16[16,288,288]{2,1,0:T(8,128)(2,1)} %bitcast.229), calls=%async_computation.3 | async-start | bytes 7077888 | tf_op jit(solution)/shard_map/all_to_all | solution.py:55
  248.3 2.6 convert_reduce_fusion.1
  251.1 39.3 %all-to-all-done.3 = bf16[16,288,288]{2,1,0:T(8,128)(2,1)} async-done(((bf16[16,288,288]{2,1,0:T(8,128)(2,1)}), bf16[16,288,288]{2,1,0:T(8,128)(2,1)}, u32[]{:S(2)}, u32[]{:S(2)}) %all-to-all-start.3) | async-done | bytes 2654240 | tf_op jit(solution)/shard_map/all_to_all | solution.py:55
  290.4 2.6 convert_reduce_fusion
  293.1 9.2 %all-reduce.2 = (f32[288]{0:T(512)S(1)}, f32[288]{0:T(512)S(1)}) all-reduce(f32[288]{0:T(512)S(1)} %multiply_reduce_fusion.1, f32[288]{0:T(512)S(1)} %multiply_reduce_fusion), channel_id=1, replica_groups=mesh['dp_0'=4,'dp_1'=2,'tensor_0'=4,'tensor_1'=4] {'tensor_0'}, use_global_device_ids=true, to_apply=%region_6.7 | all-reduce | flops 576 | bytes 4608 | tf_op jit(solution)/shard_map/psum | solution.py:26
  302.3 9.1 %all-reduce = (f32[288]{0:T(512)S(1)}, f32[288]{0:T(512)S(1)}) all-reduce(f32[288]{0:T(512)S(1)} %get-tuple-element.15, f32[288]{0:T(512)S(1)} %get-tuple-element.16), channel_id=1, replica_groups=mesh['dp_0'=4,'dp_1'=2,'tensor_0'=4,'tensor_1'=4] {'tensor_1'}, use_global_device_ids=true, to_apply=%region_7.8 | all-reduce | flops 576 | bytes 4608 | tf_op jit(solution)/shard_map/psum | solution.py:26
  313.1 11.4 %psum.134 = f32[2,24]{1,0:T(2,128)S(1)} all-reduce(f32[2,24]{1,0:T(2,128)S(1)} %dynamic_update_slice.3), channel_id=1, replica_groups=mesh['dp_0'=4,'dp_1'=2,'tensor_0'=4,'tensor_1'=4] {'dp_0'}, use_global_device_ids=true, to_apply=%region_20.21 | all-reduce | flops 48 | bytes 384 | tf_op jit(solution)/shard_map/psum | solution.py:26
  324.5 2.5 psum.135
  326.9 9.0 %psum.136 = f32[2,24]{1,0:T(2,128)S(1)} all-reduce(f32[2,24]{1,0:T(2,128)S(1)} %psum.135), channel_id=1, replica_groups=mesh['dp_0'=4,'dp_1'=2,'tensor_0'=4,'tensor_1'=4] {'tensor_0'}, use_global_device_ids=true, to_apply=%region_22.23 | all-reduce | flops 48 | bytes 384 | tf_op jit(solution)/shard_map/psum | solution.py:26
  335.9 7.7 %psum.137 = f32[2,24]{1,0:T(2,128)S(1)} all-reduce(f32[2,24]{1,0:T(2,128)S(1)} %psum.136), channel_id=1, replica_groups=mesh['dp_0'=4,'dp_1'=2,'tensor_0'=4,'tensor_1'=4] {'tensor_1'}, use_global_device_ids=true, to_apply=%region_23.24 | all-reduce | flops 48 | bytes 384 | tf_op jit(solution)/shard_map/psum | solution.py:26
  344.8 8.5 %psum.138 = f32[288]{0:T(512)S(1)} all-reduce(f32[288]{0:T(512)S(1)} %fusion.63), channel_id=1, replica_groups=mesh['dp_0'=4,'dp_1'=2,'tensor_0'=4,'tensor_1'=4] {'tensor_0'}, use_global_device_ids=true, to_apply=%region_26.27 | all-reduce | flops 288 | bytes 2304 | tf_op jit(solution)/shard_map/psum | solution.py:26
  353.3 9.8 %psum.139 = f32[288]{0:T(512)S(1)} all-reduce(f32[288]{0:T(512)S(1)} %psum.138), channel_id=1, replica_groups=mesh['dp_0'=4,'dp_1'=2,'tensor_0'=4,'tensor_1'=4] {'tensor_1'}, use_global_device_ids=true, to_apply=%region_27.28 | all-reduce | flops 288 | bytes 2304 | tf_op jit(solution)/shard_map/psum | solution.py:26
  363.6 39.2 %all_to_all.41 = bf16[16,288,288]{2,1,0:T(8,128)(2,1)S(1)} all-to-all(bf16[16,288,288]{2,1,0:T(8,128)(2,1)S(1)} %broadcast_in_dim.33), channel_id=1, replica_groups=mesh['dp_0'=4,'dp_1'=2,'tensor_0'=4,'tensor_1'=4] {'tensor_0','tensor_1'}, dimensions={0} | all-to-all | bytes 5308416 | tf_op jit(solution)/shard_map/all_to_all | solution.py:31
  402.7 3.1 copy.103
  405.8 6.7 %reshape.378 = bf16[288,4608]{1,0:T(8,128)(2,1)} reshape(bf16[288,16,288]{2,1,0:T(8,128)(2,1)} %copy.103) | data formatting | bytes 5308416 | tf_op jit(solution)/shard_map/reshape | solution.py:39
  412.5 3.4 fusion.23
  418.3 2.2 convolution_convert_fusion.2
  420.5 3.6 all-to-all-start.5
  424.3 2.5 fusion.7
  426.8 2.2 convolution_add_fusion.2
  429.0 2.1 convolution_add_fusion.1
  431.1 3.8 fusion
  434.9 6.4 %all-to-all-done.5 = bf16[8,576,128]{2,1,0:T(8,128)(2,1)S(1)} async-done(((bf16[8,576,128]{2,1,0:T(8,128)(2,1)}), bf16[8,576,128]{2,1,0:T(8,128)(2,1)S(1)}, u32[]{:S(2)}, u32[]{:S(2)}) %all-to-all-start.5) | async-done | bytes 1179680 | tf_op jit(solution)/shard_map/all_to_all | solution.py:55
  443.2 3.4 all-to-all-start.7
  446.8 5.8 %all-to-all-done.7 = bf16[8,64,128]{2,1,0:T(8,128)(2,1)S(1)} async-done(((bf16[8,64,128]{2,1,0:T(8,128)(2,1)}), bf16[8,64,128]{2,1,0:T(8,128)(2,1)S(1)}, u32[]{:S(2)}, u32[]{:S(2)}) %all-to-all-start.7) | async-done | bytes 131104 | tf_op jit(solution)/shard_map/all_to_all | solution.py:31
  453.3 3.4 all-to-all-start.6
  458.0 6.2 %all-to-all-done.6 = bf16[8,64,256]{2,1,0:T(8,128)(2,1)S(1)} async-done(((bf16[8,64,256]{2,1,0:T(8,128)(2,1)}), bf16[8,64,256]{2,1,0:T(8,128)(2,1)S(1)}, u32[]{:S(2)}, u32[]{:S(2)}) %all-to-all-start.6) | async-done | bytes 262176 | tf_op jit(solution)/shard_map/all_to_all | solution.py:31
  464.8 68.0 %all-reduce.7.cloned.1.call-done = (bf16[288,4608]{1,0:T(8,128)(2,1)}, bf16[576,128]{1,0:T(8,128)(2,1)}) async-done(((bf16[288,4608]{1,0:T(8,128)(2,1)}, bf16[576,128]{1,0:T(8,128)(2,1)}), (bf16[288,4608]{1,0:T(8,128)(2,1)}, bf16[576,128]{1,0:T(8,128)(2,1)})) %all-reduce.7.cloned.1.call-update) | async-done | bytes 2801680 | tf_op jit(solution)/shard_map/psum | solution.py:374
  532.8 1.2 fusion.60
  534.1 10.0 %psum.141 = f32[288]{0:T(512)S(1)} all-reduce(f32[288]{0:T(512)S(1)} %fusion.60), channel_id=1, replica_groups=mesh['dp_0'=4,'dp_1'=2,'tensor_0'=4,'tensor_1'=4] {'tensor_0'}, use_global_device_ids=true, to_apply=%region_31.32 | all-reduce | flops 288 | bytes 2304 | tf_op jit(solution)/shard_map/psum | solution.py:26
  544.0 8.8 %psum.142 = f32[288]{0:T(512)S(1)} all-reduce(f32[288]{0:T(512)S(1)} %psum.141), channel_id=1, replica_groups=mesh['dp_0'=4,'dp_1'=2,'tensor_0'=4,'tensor_1'=4] {'tensor_1'}, use_global_device_ids=true, to_apply=%region_32.33 | all-reduce | flops 288 | bytes 2304 | tf_op jit(solution)/shard_map/psum | solution.py:26
  552.8 1.6 convert_element_type.190
  554.4 2.0 fusion.65
  (147 shorter events, 24.4 us)
Async XLA Ops:
  7.2 152.4 %copy-start = (bf16[64,256]{1,0:T(8,128)(2,1)S(1)}, bf16[64,256]{1,0:T(8,128)(2,1)}, u32[]{:S(2)}) copy-start(bf16[64,256]{1,0:T(8,128)(2,1)} %param.28) | copy-start | bytes 98308
  7.2 6.2 %copy-start.3 = (bf16[288,288]{1,0:T(8,128)(2,1)S(1)}, bf16[288,288]{1,0:T(8,128)(2,1)}, u32[]{:S(2)}) copy-start(bf16[288,288]{1,0:T(8,128)(2,1)} %param.16) | copy-start | bytes 497668
  7.2 6.2 %copy-start.8 = (bf16[288,288]{1,0:T(8,128)(2,1)S(1)}, bf16[288,288]{1,0:T(8,128)(2,1)}, u32[]{:S(2)}) copy-start(bf16[288,288]{1,0:T(8,128)(2,1)} %param.15) | copy-start | bytes 497668
  7.2 139.1 %all-gather.2.cloned.1.call-start = ((), (), s32[]{:S(2)}) async-start(), calls=%async_computation.8 | async-start | bytes 9289728 | tf_op jit(solution)/shard_map/all_gather | solution.py:65
  82.7 4.7 copy-start.31
  82.7 45.8 %all-to-all-start = ((bf16[16,288,288]{2,1,0:T(8,128)(2,1)}), bf16[16,288,288]{2,1,0:T(8,128)(2,1)}, u32[]{:S(2)}, u32[]{:S(2)}) async-start(bf16[16,288,288]{2,1,0:T(8,128)(2,1)} %broadcast_in_dim.24), calls=%async_computation | async-start | bytes 7077888 | tf_op jit(solution)/shard_map/all_to_all | solution.py:31
  139.1 33.6 %copy-start.1 = (bf16[288,4608]{1,0:T(8,128)(2,1)}, bf16[288,4608]{1,0:T(8,128)(2,1)S(1)}, u32[]{:S(2)}) copy-start(bf16[288,4608]{1,0:T(8,128)(2,1)S(1)} %reshape.369) | copy-start | bytes 7962628
  154.0 2.1 copy-start.26
  161.9 3.5 copy-start.5
  165.4 2.3 copy-start.7
  167.7 2.2 copy-start.14
  169.9 2.5 copy-start.23
  169.9 2.8 copy-start.25
  170.7 0.9 copy-start.17
  170.7 0.9 copy-start.19
  171.6 0.7 copy-start.9
  171.6 0.7 copy-start.11
  172.7 2.3 copy-start.15
  172.7 2.3 copy-start.29
  175.0 0.6 copy-start.34
  188.6 9.0 %copy-start.21 = (bf16[3,96,2,64]{3,1,2,0:T(8,128)(2,1)S(1)}, bf16[3,96,2,64]{3,1,2,0:T(8,128)(2,1)}, u32[]{:S(2)}) copy-start(bf16[3,96,2,64]{3,1,2,0:T(8,128)(2,1)} %get-tuple-element.30) | copy-start | bytes 221188
  188.6 9.1 %copy-start.22 = (bf16[3,96,2,64]{3,1,2,0:T(8,128)(2,1)S(1)}, bf16[3,96,2,64]{3,1,2,0:T(8,128)(2,1)}, u32[]{:S(2)}) copy-start(bf16[3,96,2,64]{3,1,2,0:T(8,128)(2,1)} %get-tuple-element.31) | copy-start | bytes 221188
  188.6 11.6 %copy-start.6 = (bf16[3,96,4608]{2,1,0:T(8,128)(2,1)S(1)}, bf16[3,96,4608]{2,1,0:T(8,128)(2,1)}, u32[]{:S(2)}) copy-start(bf16[3,96,4608]{2,1,0:T(8,128)(2,1)} %dot_general.122) | copy-start | bytes 7962628
  188.6 52.5 %all-to-all-start.1 = ((bf16[16,288,288]{2,1,0:T(8,128)(2,1)}), bf16[16,288,288]{2,1,0:T(8,128)(2,1)}, u32[]{:S(2)}, u32[]{:S(2)}) async-start(bf16[16,288,288]{2,1,0:T(8,128)(2,1)} %bitcast.230), calls=%async_computation.1 | async-start | bytes 7077888 | tf_op jit(solution)/shard_map/all_to_all | solution.py:55
  241.1 7.0 %copy-start.33 = (s32[24]{0:T(128)S(1)}, s32[24]{0:T(128)}, u32[]{:S(2)}) copy-start(s32[24]{0:T(128)} %param.19) | copy-start | bytes 292
  241.1 49.3 %all-to-all-start.3 = ((bf16[16,288,288]{2,1,0:T(8,128)(2,1)}), bf16[16,288,288]{2,1,0:T(8,128)(2,1)}, u32[]{:S(2)}, u32[]{:S(2)}) async-start(bf16[16,288,288]{2,1,0:T(8,128)(2,1)} %bitcast.229), calls=%async_computation.3 | async-start | bytes 7077888 | tf_op jit(solution)/shard_map/all_to_all | solution.py:55
  250.9 60.5 %copy-start.4 = (bf16[288,288]{1,0:T(8,128)(2,1)S(1)}, bf16[288,288]{1,0:T(8,128)(2,1)}, u32[]{:S(2)}) copy-start(bf16[288,288]{1,0:T(8,128)(2,1)} %param.17) | copy-start | bytes 497668
  251.1 61.6 %copy-start.32 = (s32[3]{0:T(128)S(1)}, s32[3]{0:T(128)}, u32[]{:S(2)}) copy-start(s32[3]{0:T(128)} %param.18) | copy-start | bytes 40
  412.5 3.5 copy-start.16
  412.5 3.5 copy-start.24
  412.5 3.5 copy-start.30
  412.5 3.8 copy-start.35
  415.8 0.9 copy-start.10
  415.8 1.0 copy-start.12
  415.9 1.2 copy-start.18
  415.9 1.2 copy-start.20
  416.0 1.4 copy-start.27
  416.0 1.6 copy-start.13
  416.5 1.8 copy-start.2
  420.5 20.8 %all-to-all-start.5 = ((bf16[8,576,128]{2,1,0:T(8,128)(2,1)}), bf16[8,576,128]{2,1,0:T(8,128)(2,1)S(1)}, u32[]{:S(2)}, u32[]{:S(2)}) async-start(bf16[8,576,128]{2,1,0:T(8,128)(2,1)} %bitcast.71), calls=%async_computation.5 | async-start | bytes 2359296 | tf_op jit(solution)/shard_map/all_to_all | solution.py:55
  424.1 108.7 %all-reduce.7.cloned.1.call-start = ((), (), s32[]{:S(2)}) async-start(), calls=%async_computation.9 | async-start | bytes 5603328 | tf_op jit(solution)/shard_map/psum | solution.py:374
  442.2 112.2 %copy-start.28 = (f32[288]{0:T(512)S(1)}, f32[288]{0:T(512)}, u32[]{:S(2)}) copy-start(f32[288]{0:T(512)} %get-tuple-element.44) | copy-start | bytes 3460
  443.2 9.4 %all-to-all-start.7 = ((bf16[8,64,128]{2,1,0:T(8,128)(2,1)}), bf16[8,64,128]{2,1,0:T(8,128)(2,1)S(1)}, u32[]{:S(2)}, u32[]{:S(2)}) async-start(bf16[8,64,128]{2,1,0:T(8,128)(2,1)} %broadcast_in_dim.35), calls=%async_computation.7 | async-start | bytes 262144 | tf_op jit(solution)/shard_map/all_to_all | solution.py:31
  453.3 10.9 %all-to-all-start.6 = ((bf16[8,64,256]{2,1,0:T(8,128)(2,1)}), bf16[8,64,256]{2,1,0:T(8,128)(2,1)S(1)}, u32[]{:S(2)}, u32[]{:S(2)}) async-start(bf16[8,64,256]{2,1,0:T(8,128)(2,1)} %broadcast_in_dim.34), calls=%async_computation.6 | async-start | bytes 524288 | tf_op jit(solution)/shard_map/all_to_all | solution.py:31
Sparse Core Ops, SparseCore 0:
  12.7 51.5 all-gather.1
  442.4 90.4 all-reduce.6
where the time goes:
time: 573 us; the launch traced here: 564 us
  blocking collectives  191 us (33%)
  waiting for transfers between devices  172 us (30%)
  local copies, waits for them, and re-layouts  89.4 us (16%)
  matrix products  45.7 us (8%)
  starting transfers between devices  30.3 us (5%)
  other arithmetic  20.1 us (4%)
  between operations  15.2 us (3%)
    psum x12, blocking collectives, one_axis_at_a_time(): return functools.reduce(lax.psum, axes, shard)  108 us
    all_to_all x2, blocking collectives, copy_for_each(): lax.all_to_all(jnp.broadcast_to(shard[None], (count, *shard.shape)), axis...  82.7 us
    all_to_all x3, waiting for transfers between devices, summed_on_arrival(): lax.all_to_all(tiles, axis, split_axis=0, concat_axis=0, tiled=True)  71 us
    psum x1, waiting for transfers between devices, body(): lax.psum(input_terms.astype(jnp.bfloat16), TENSOR).astype(jnp.float32)  68 us
    all_to_all x3, waiting for transfers between devices, copy_for_each(): lax.all_to_all(jnp.broadcast_to(shard[None], (count, *shard.shape)), axis...  33 us
    reshape x4, local copies, waits for them, and re-layouts, split_up(): shard.reshape(*shape[:dim], count, shape[dim] // count, *shape[dim + 1:])  20.9 us
    all_to_all x3, starting transfers between devices, summed_on_arrival(): lax.all_to_all(tiles, axis, split_axis=0, concat_axis=0, tiled=True)  18.8 us
    dot_general x2, local copies, waits for them, and re-layouts, attention_layer(): jnp.dot(normed, value_projection, preferred_element_type=jnp.float32)  13.3 us
  transfers between devices with their start and end apart: 8, of which 7 were waited for; matrix products, arithmetic and copies ran while one was open for 14% of the time, Pallas kernels for 0%

commit v1 on v0

v1 whole, which is shorter than its diff:
```python
import jax
import jax.numpy as jnp
import numpy as np
from jax import lax
from jax.experimental import pallas as pl
from jax.experimental.pallas import tpu as pltpu
from jax.sharding import Mesh
from jax.sharding import PartitionSpec as P

DP = ("dp_0", "dp_1")
TENSOR = ("tensor_0", "tensor_1")
MESH = pl.DeviceIdType.MESH

WIDTH = 4608
TOK = 288
LENGTH = 96
HEAD = 128
RANK = 64
NORM_EPS = 1e-06
SOFT_CAP = 50.0
ADAPTER_SCALE = 0.5
DPO_BETA = 0.5
LOSS_SCALE = 256.0
ROPE_BASE = 10000.0
QUERY_SCALE = float(WIDTH // 32) ** (-0.5)

GROUP = 80
SHARD = 2 * TOK + GROUP
MAIN = 4096
RINGS = ((0, 1), (0, -1), (1, 1), (1, -1))

F32 = jnp.float32
BF16 = jnp.bfloat16
NT = (((1,), (1,)), ((), ()))
TN = (((0,), (0,)), ((), ()))


def dot(a, b, dims=(((1,), (0,)), ((), ())), precision=None):
    return lax.dot_general(a, b, dims, preferred_element_type=F32, precision=precision)


def aligned(start, multiple):
    return start if isinstance(start, int) else pl.multiple_of(start, multiple)


def back(position, hops, direction):
    return lax.rem(position - hops * direction + 8, 4)


def chunks_of(rows):
    tiles = rows // 16
    sizes = [16 * (tiles // 4 + (1 if k < tiles % 4 else 0)) for k in range(4)]
    return sizes, [sum(sizes[:k]) for k in range(4)]


class Ring:
    def __init__(self, rows, send, recv):
        self.rows = rows
        self.sizes, self.starts = chunks_of(rows)
        self.send, self.recv = send, recv
        self.at = (lax.axis_index("tensor_0"), lax.axis_index("tensor_1"))

    def place(self, k, first, second):
        primary, way = RINGS[k]
        a = back(self.at[primary], first, way)
        b = back(self.at[1 - primary], second, way)
        px, pz = (a, b) if primary == 0 else (b, a)
        return aligned((4 * px + pz) * self.rows + self.starts[k], 16)

    def next_on(self, k, secondary):
        primary, way = RINGS[k]
        axis = 1 - primary if secondary else primary
        return {TENSOR[axis]: back(self.at[axis], -1, way)}

    def remote(self, source, target, k, number, device):
        return pltpu.make_async_remote_copy(
            src_ref=source,
            dst_ref=target,
            send_sem=self.send.at[k, number],
            recv_sem=self.recv.at[k, number],
            device_id=device,
            device_id_type=MESH,
        )


class Gather(Ring):
    def __init__(self, buffer, rows, send, recv):
        super().__init__(rows, send, recv)
        self.buffer = buffer

    def piece(self, k, j, s):
        return self.buffer.at[pl.ds(self.place(k, j, s), self.sizes[k]), :]

    def number(self, secondary, j, s):
        return 3 + 3 * j + s if secondary else j

    def copy(self, k, secondary, j, s):
        piece = self.piece(k, j, s)
        return self.remote(piece, piece, k, self.number(secondary, j, s), self.next_on(k, secondary))

    def start(self, secondary, j, s):
        for k in range(4):
            self.copy(k, secondary, j, s).start()

    def wait(self, k, secondary, j, s):
        piece = self.piece(k, j, s + 1) if secondary else self.piece(k, j + 1, s)
        self.remote(piece, piece, k, self.number(secondary, j, s), self.next_on(k, secondary)).wait_recv()

    def wave(self, w):
        if w == 0:
            self.start(False, 0, 0)
            self.start(True, 0, 0)
            return
        if w <= 3:
            for k in range(4):
                self.wait(k, False, w - 1, 0)
                if w < 3:
                    self.copy(k, False, w, 0).start()
                self.copy(k, True, w, 0).start()
        for s in range(3):
            j = w - 1 - s
            if 0 <= j <= 3:
                for k in range(4):
                    self.wait(k, True, j, s)
                    if s < 2:
                        self.copy(k, True, j, s + 1).start()

    def drain(self):
        for k in range(4):
            for j in range(3):
                self.copy(k, False, j, 0).wait_send()
            for j in range(4):
                for s in range(3):
                    self.copy(k, True, j, s).wait_send()


class Scatter(Ring):
    def __init__(self, partial, landing, rows, send, recv):
        super().__init__(rows, send, recv)
        self.partial, self.landing = partial, landing

    def piece(self, k, first, second):
        return self.partial.at[pl.ds(self.place(k, first, second), self.sizes[k]), :]

    def slot(self, k, number):
        return self.landing.at[pl.ds(15 * self.starts[k] + number * self.sizes[k], self.sizes[k]), :]

    def outer(self, k, j, s):
        number = 3 * j + s
        return self.remote(self.piece(k, j + 1, s + 1), self.slot(k, number), k, number, self.next_on(k, True))

    def inner(self, k, s):
        return self.remote(self.piece(k, s + 1, 0), self.slot(k, 12 + s), k, 12 + s, self.next_on(k, False))

    def add(self, k, number, first, second):
        piece, slot = self.piece(k, first, second), self.slot(k, number)
        piece[...] = (piece[...].astype(F32) + slot[...].astype(F32)).astype(BF16)

    def begin(self):
        for j in range(4):
            for k in range(4):
                self.outer(k, j, 0).start()

    def run(self, result):
        for s in range(3):
            self.turn(s, result)

    def turn(self, s, result):
        for j in range(4):
            for k in range(4):
                self.outer(k, j, s).wait_recv()
                self.add(k, 3 * j + s, j + 1, s + 2)
                if s < 2:
                    self.outer(k, j, s + 1).start()
                    continue
                if j == 0:
                    self.inner(k, 0).start()
                    continue
                self.inner(k, j - 1).wait_recv()
                if j < 3:
                    self.add(k, 12 + j - 1, j + 1, 0)
                    self.inner(k, j).start()
                else:
                    own = self.piece(k, 0, 0)[...].astype(F32) + self.slot(k, 14)[...].astype(F32)
                    result[pl.ds(self.starts[k], self.sizes[k]), :] = own

    def drain(self):
        for k in range(4):
            for j in range(4):
                for s in range(3):
                    self.outer(k, j, s).wait_send()
            for s in range(3):
                self.inner(k, s).wait_send()


class Weights:
    def __init__(self, w_in, w_back, y_send, y_recv, d_send, d_recv):
        self.w_in, self.w_back = w_in, w_back
        self.sems = (y_send, y_recv, d_send, d_recv)
        self.y, self.core = lax.axis_index("dp_0"), lax.axis_index("dp_1")

    def block(self, hops, half, part, core):
        way = 1 - 2 * half
        tile = 2 * (2 * back(self.y, hops, way) + core) + half
        ref = self.w_in if part < 2 else self.w_back
        if part % 2 == 0:
            return ref.at[pl.ds(aligned(256 * tile, 256), 256), :]
        return ref.at[pl.ds(aligned(MAIN + 32 * tile, 32), 32), :]

    def round(self, s, half, part, arriving=False):
        ref = self.block(s + 1 if arriving else s, half, part, self.core)
        return pltpu.make_async_remote_copy(
            src_ref=ref,
            dst_ref=ref,
            send_sem=self.sems[0].at[half, s, part],
            recv_sem=self.sems[1].at[half, s, part],
            device_id={"dp_0": back(self.y, -1, 1 - 2 * half)},
            device_id_type=MESH,
        )

    def across(self, i, half, part, arriving=False):
        ref = self.block(i, half, part, 1 - self.core if arriving else self.core)
        return pltpu.make_async_remote_copy(
            src_ref=ref,
            dst_ref=ref,
            send_sem=self.sems[2].at[half, i, part],
            recv_sem=self.sems[3].at[half, i, part],
            device_id={"dp_1": 1 - self.core},
            device_id_type=MESH,
        )

    def step(self, s, parts):
        for half in range(2):
            for part in parts:
                if s > 0:
                    self.round(s - 1, half, part, True).wait_recv()
                if s < 3:
                    self.round(s, half, part).start()
                self.across(s, half, part).start()

    def arrive(self, parts):
        for half in range(2):
            for part in parts:
                for i in range(4):
                    self.across(i, half, part, True).wait_recv()

    def drain(self):
        for half in range(2):
            for part in range(4):
                for s in range(3):
                    self.round(s, half, part).wait_send()
                for i in range(4):
                    self.across(i, half, part).wait_send()


class Exchange:
    def __init__(self, buffer, rows, count, me, device_of, send, recv, source=None, spread=False):
        self.buffer, self.rows, self.count, self.me = buffer, rows, count, me
        self.device_of, self.send, self.recv = device_of, send, recv
        self.source = buffer if source is None else source
        self.spread = spread

    def slot(self, i):
        return self.buffer.at[pl.ds(aligned(i * self.rows, 8), self.rows), :]

    def copy(self, delta):
        peer = lax.rem(self.me + delta, self.count)
        origin = peer if self.spread else self.me
        return pltpu.make_async_remote_copy(
            src_ref=self.source.at[pl.ds(aligned(origin * self.rows, 8), self.rows), :],
            dst_ref=self.slot(self.me),
            send_sem=self.send.at[delta],
            recv_sem=self.recv.at[delta],
            device_id=self.device_of(peer),
            device_id_type=MESH,
        )

    def start(self):
        for delta in range(1, self.count):
            self.copy(delta).start()

    def wait(self):
        for delta in range(1, self.count):
            arrived = self.slot(lax.rem(self.me - delta + self.count, self.count))
            pltpu.make_async_remote_copy(
                src_ref=arrived,
                dst_ref=arrived,
                send_sem=self.send.at[delta],
                recv_sem=self.recv.at[delta],
                device_id=self.device_of(lax.rem(self.me + delta, self.count)),
                device_id_type=MESH,
            ).wait_recv()

    def total(self):
        value = self.buffer[0 : self.rows, :].astype(F32)
        for i in range(1, self.count):
            value = value + self.buffer[self.rows * i : self.rows * i + self.rows, :].astype(F32)
        return value

    def drain(self):
        for delta in range(1, self.count):
            self.copy(delta).wait_send()


def in_tensor(i):
    return {"tensor_0": lax.div(i, 4), "tensor_1": lax.rem(i, 4)}


def in_data(i):
    return {"dp_0": lax.div(i, 2), "dp_1": lax.rem(i, 2)}


def greet(peers):
    barrier = pltpu.get_barrier_semaphore()
    for peer in peers:
        pl.semaphore_signal(barrier, inc=1, device_id=peer, device_id_type=MESH)
    pl.semaphore_wait(barrier, len(peers))


def pack_tail(tail):
    last = jnp.concatenate([tail[240:288], jnp.zeros((32, 32), tail.dtype)], axis=0)
    return jnp.concatenate([tail[0:80], tail[80:160], tail[160:240], last], axis=1)


GROUPS = ((0, 80), (80, 80), (160, 80), (240, 48))


def unpack_features(buffer, rows, offset, target, row_offset):
    def main(t, carry):
        base = aligned(t * rows + offset, 16)
        for half in range(2):
            target[pl.ds(row_offset, TOK), pl.ds(aligned(256 * t + 128 * half, 128), 128)] = buffer[
                pl.ds(aligned(base + TOK * half, 16), TOK), :
            ]
        return carry

    lax.fori_loop(0, 16, main, 0)

    def tail(q, carry):
        tails = [
            buffer[pl.ds(aligned((4 * q + j) * rows + offset + 2 * TOK, 16), GROUP), :] for j in range(4)
        ]
        for g, (start, size) in enumerate(GROUPS):
            joined = jnp.concatenate([t[:size, 32 * g : 32 * g + 32] for t in tails], axis=1)
            target[pl.ds(row_offset + start, size), pl.ds(aligned(MAIN + 128 * q, 128), 128)] = joined
        return carry

    lax.fori_loop(0, 4, tail, 0)


def unpack_result(packed, offset, target):
    for half in range(2):
        target[:, 128 * half : 128 * half + 128] = packed[offset + TOK * half : offset + TOK * half + TOK, :]
    for g, (start, size) in enumerate(GROUPS):
        base = offset + 2 * TOK
        target[start : start + size, 256:288] = packed[base : base + size, 32 * g : 32 * g + 32]


def pack_hidden(hidden, buffer, base):
    for half in range(2):
        buffer[pl.ds(aligned(base + TOK * half, 16), TOK), :] = hidden[:, 128 * half : 128 * half + 128].astype(
            BF16
        )
    buffer[pl.ds(aligned(base + 2 * TOK, 16), GROUP), :] = pack_tail(hidden[:, 256:288]).astype(BF16)


def gain_tile(gain, c):
    if c < 32:
        return gain[c // 2 : c // 2 + 1, 128 * (c % 2) : 128 * (c % 2) + 128]
    return jnp.concatenate([gain[4 * (c - 32) + j : 4 * (c - 32) + j + 1, 256:288] for j in range(4)], axis=1)


def normalize(normed, scale_ref, gain_ref, models):
    def rows(i, carry):
        at = pl.ds(aligned(96 * i, 96), 96)
        squares = jnp.zeros((96, 128), F32)
        for c in range(36):
            x = normed[at, 128 * c : 128 * c + 128].astype(F32)
            squares = squares + x * x
        scale = lax.rsqrt(jnp.sum(squares, axis=1, keepdims=True) / WIDTH + NORM_EPS)
        scale_ref[at, :] = jnp.broadcast_to(scale, (96, 128))
        for c in range(36):
            x = normed[at, 128 * c : 128 * c + 128].astype(F32)
            normed[at, 128 * c : 128 * c + 128] = (x * scale * gain_tile(gain_ref, c)).astype(BF16)
        return carry

    lax.fori_loop(0, 3 * models, rows, 0)


def rope(x, cosine, sine):
    return x * cosine + pltpu.roll(x, 64, 1) * sine


def allowed_here(length):
    query = lax.broadcasted_iota(jnp.int32, (LENGTH, LENGTH), 0)
    key = lax.broadcasted_iota(jnp.int32, (LENGTH, LENGTH), 1)
    return (key <= query) & (key < length)


def columns_to_rows(scratch, columns):
    lane = lax.broadcasted_iota(jnp.int32, (TOK, 128), 1)
    table = jnp.zeros((TOK, 128), F32)
    for k, column in enumerate(columns):
        table = jnp.where(lane == k, column, table)
    scratch[0:TOK, :] = table
    scratch[TOK:384, :] = jnp.zeros((384 - TOK, 128), F32)
    return jnp.transpose(scratch[...])[0:8, :]


def rows_to_columns(scratch, rows):
    missing = 128 - sum(row.shape[0] for row in rows)
    filled = jnp.concatenate(list(rows) + [jnp.zeros((missing, 384), F32)], axis=0)
    scratch[...] = jnp.transpose(filled)


SCRATCH = {
    "hidden_buf": ((32 * SHARD, 128), BF16),
    "w_in": ((WIDTH, 640), BF16),
    "w_back": ((WIDTH, 256), BF16),
    "normed": ((2 * TOK, WIDTH), BF16),
    "scale": ((2 * TOK, 128), F32),
    "acc": ((2 * TOK, 640), F32),
    "linear": ((TOK, 640), F32),
    "low": ((TOK, 128), BF16),
    "heads": ((2 * TOK, 512), BF16),
    "mixed": ((2 * TOK, 256), BF16),
    "probs": ((2 * TOK, 256), F32),
    "capped": ((2 * TOK, 256), F32),
    "partial": ((32 * SHARD, 128), BF16),
    "landing": ((30 * SHARD, 128), BF16),
    "result": ((2 * SHARD, 128), F32),
    "summed": ((2, TOK, TOK), F32),
    "table": ((384, 128), F32),
    "stats": ((16 * 8, 384), F32),
    "scores": ((8 * 8, 128), F32),
    "grad_buf": ((16 * SHARD, 128), BF16),
    "grad_mixed": ((TOK, 256), F32),
    "grads": ((TOK, 640), BF16),
    "partial_back": ((16 * SHARD, 128), BF16),
    "landing_back": ((15 * SHARD, 128), BF16),
    "hooks": ((384, 128), F32),
    "hook_parts": ((384, 128), F32),
    "hook_whole": ((384, 128), F32),
    "stats_back": ((16 * 8, 384), F32),
    "factors": ((8 * 64, 384), BF16),
    "a_terms": ((WIDTH, 128), BF16),
    "a_across": ((4 * 576, 128), BF16),
    "a_pairs": ((4 * 576, 128), BF16),
    "a_round": ((4 * 576, 128), BF16),
}
SEMAPHORES = {
    "gather": (4, 15),
    "scatter": (4, 15),
    "gather_back": (4, 15),
    "scatter_back": (4, 15),
    "y": (2, 3, 4),
    "d": (2, 4, 4),
    "stats": (16,),
    "scores": (8,),
    "hooks": (16,),
    "hook_whole": (16,),
    "stats_back": (16,),
    "factors": (8,),
    "across": (4,),
    "round": (4,),
}


class Refs:
    pass


def step_body(*refs):
    names = INPUTS + OUTPUTS + list(SCRATCH)
    r = Refs()
    for name, ref in zip(names, refs):
        setattr(r, name, ref)
    sems = refs[len(names) :]
    send = dict(zip(SEMAPHORES, sems[0::2]))
    recv = dict(zip(SEMAPHORES, sems[1::2]))

    x, z = lax.axis_index("tensor_0"), lax.axis_index("tensor_1")
    y, core = lax.axis_index("dp_0"), lax.axis_index("dp_1")
    mine, rank = 4 * x + z, 2 * y + core
    base = mine * 2 * SHARD
    pack_hidden(r.ref_hidden[...], r.hidden_buf, base)
    pack_hidden(r.pol_hidden[...], r.hidden_buf, base + SHARD)
    for half in range(2):
        tile = 2 * rank + half
        for start, size, to in ((0, 256, 256 * tile), (256, 32, MAIN + 32 * tile)):
            here, there = pl.ds(288 * half + start, size), pl.ds(aligned(to, 32), size)
            r.w_in[there, 0:256] = r.w_query[here, :]
            r.w_in[there, 256:384] = r.w_key[here, :]
            r.w_in[there, 384:512] = r.w_value[here, :]
            r.w_in[there, 512:640] = jnp.concatenate([r.a_query[here, :], r.a_value[here, :]], axis=1)
            r.w_back[there, :] = r.w_out[here, :]
    greet(
        [in_tensor(lax.rem(mine + i, 16)) for i in range(1, 16)]
        + [in_data(lax.rem(rank + i, 8)) for i in range(1, 8)]
    )

    gather = Gather(r.hidden_buf, 2 * SHARD, send["gather"], recv["gather"])
    weights = Weights(r.w_in, r.w_back, send["y"], recv["y"], send["d"], recv["d"])
    gather.wave(0)
    weights.step(0, (0, 1))
    gather.wave(1)
    gather.wave(2)
    weights.step(1, (0, 1))
    gather.wave(3)
    gather.wave(4)
    weights.step(2, (0, 1))
    weights.step(0, (2, 3))
    gather.wave(5)
    gather.wave(6)
    unpack_features(r.hidden_buf, 2 * SHARD, 0, r.normed, 0)
    unpack_features(r.hidden_buf, 2 * SHARD, SHARD, r.normed, TOK)
    normalize(r.normed, r.scale, r.pre_gain, 2)
    weights.step(3, (0, 1))
    weights.arrive((0, 1))

    acc = r.acc
    acc[...] = jnp.zeros_like(acc)

    def project(i, carry):
        at = pl.ds(aligned(512 * i, 512), 512)
        acc[...] += dot(r.normed[:, at], r.w_in[at, :])
        return carry

    lax.fori_loop(0, 9, project, 0)
    weights.step(1, (2, 3))

    r.linear[...] = acc[TOK : 2 * TOK, :]
    r.low[...] = acc[TOK : 2 * TOK, 512:640].astype(BF16)
    query_factor = jnp.concatenate([r.b_query[...], jnp.zeros((RANK, 256), BF16)], axis=0)
    value_factor = jnp.concatenate([jnp.zeros((RANK, 128), BF16), r.b_value[...]], axis=0)
    acc[TOK : 2 * TOK, 0:256] += ADAPTER_SCALE * dot(r.low[...], query_factor)
    acc[TOK : 2 * TOK, 384:512] += ADAPTER_SCALE * dot(r.low[...], value_factor)

    def attend(i, carry):
        at = pl.ds(aligned(96 * i, 96), 96)
        cos, sin = r.cosine[...], r.sine[...]
        key = rope(acc[at, 256:384], cos, sin).astype(BF16)
        value = acc[at, 384:512].astype(BF16)
        allowed = allowed_here(r.lengths[lax.rem(i, 3)])
        r.heads[at, 256:384] = key
        r.heads[at, 384:512] = value
        for g in range(2):
            query = rope(acc[at, 128 * g : 128 * g + 128], cos, sin).astype(BF16)
            r.heads[at, 128 * g : 128 * g + 128] = query
            scores = dot(query, key, NT) * QUERY_SCALE
            cap = SOFT_CAP * jnp.tanh(scores / SOFT_CAP)
            weight = jnp.where(allowed, jnp.exp(cap), 0.0)
            prob = weight / jnp.sum(weight, axis=1, keepdims=True)
            r.probs[at, 128 * g : 128 * g + 96] = prob
            r.capped[at, 128 * g : 128 * g + 96] = cap
            r.mixed[at, 128 * g : 128 * g + 128] = dot(prob.astype(BF16), value).astype(BF16)
        return carry

    lax.fori_loop(0, 6, attend, 0)
    weights.step(2, (2, 3))
    weights.step(3, (2, 3))
    weights.arrive((2, 3))
    partial_products(r.mixed, r.w_back, r.partial, 2)

    scatter = Scatter(r.partial, r.landing, 2 * SHARD, send["scatter"], recv["scatter"])
    scatter.begin()
    scatter.run(r.result)
    for m in range(2):
        unpack_result(r.result, m * SHARD, r.summed.at[m])

    post_gain = r.post_gain[pl.ds(mine, 1), :]
    pre_gain = r.pre_gain[pl.ds(mine, 1), :]
    columns = [[], [], []]
    for m, hidden in enumerate((r.ref_hidden, r.pol_hidden)):
        summed, readout = r.summed[m], r.readout[...].astype(F32)
        columns[0].append(jnp.sum(summed * summed, axis=1, keepdims=True))
        columns[1].append(jnp.sum(summed * post_gain * readout, axis=1, keepdims=True))
        columns[2].append(jnp.sum(hidden[...].astype(F32) * readout, axis=1, keepdims=True))
    stats = Exchange(r.stats, 8, 16, mine, in_tensor, send["stats"], recv["stats"])
    r.stats[pl.ds(aligned(8 * mine, 8), 8), :] = columns_to_rows(r.table, sum(columns, []))
    stats.start()
    stats.wait()
    totals = stats.total()
    post_scale = lax.rsqrt(totals[0:2] / WIDTH + NORM_EPS)
    lane = lax.broadcasted_iota(jnp.int32, (1, 384), 1)
    lengths = [r.lengths[s] for s in range(3)]
    living = jnp.zeros((1, 384), F32)
    for s in range(3):
        living = jnp.where((lane >= 96 * s) & (lane < 96 * s + lengths[s]), 1.0, living)
    token_scores = (totals[4:6] + post_scale * totals[2:4]) * living
    row8 = lax.broadcasted_iota(jnp.int32, (8, 128), 0)
    lane8 = lax.broadcasted_iota(jnp.int32, (8, 128), 1)
    tile = jnp.zeros((8, 128), F32)
    for m in range(2):
        for s in range(3):
            inside = (lane >= 96 * s) & (lane < 96 * s + 96)
            score = jnp.sum(jnp.where(inside, token_scores[m : m + 1], 0.0), axis=1, keepdims=True)
            tile = jnp.where((row8 == m) & (lane8 == 3 * rank + s), score, tile)
    scores = Exchange(r.scores, 8, 8, rank, in_data, send["scores"], recv["scores"])
    r.scores[pl.ds(aligned(8 * rank, 8), 8), :] = tile
    scores.start()
    scores.wait()
    everyone = scores.total()
    ratio = everyone[1:2] - everyone[0:1]
    row32 = lax.broadcasted_iota(jnp.int32, (32, 128), 0)
    lane32 = lax.broadcasted_iota(jnp.int32, (32, 128), 1)
    named = jnp.full((32, 128), -1, jnp.int32)
    for k in range(24):
        named = jnp.where(row32 == k, r.pairing[k], named)
    chosen = named == lane32
    even = lax.rem(row32, 2) == 0
    picked = jnp.broadcast_to(jnp.sum(jnp.where(chosen, ratio, 0.0), axis=1, keepdims=True), (32, 128))
    other = jnp.where(even, pltpu.roll(picked, 31, 0), pltpu.roll(picked, 1, 0))
    margin = DPO_BETA * jnp.where(even, picked - other, other - picked)
    loss = jnp.maximum(-margin, 0.0) + jnp.log1p(jnp.exp(-jnp.abs(margin)))
    counted = even & (row32 < 24) & (lane32 == 0)
    total_loss = jnp.sum(jnp.where(counted, loss, 0.0), axis=(0, 1), keepdims=True)
    r.loss[...] = jnp.broadcast_to(total_loss, (8, 128))
    pull = DPO_BETA * LOSS_SCALE / (1.0 + jnp.exp(margin))
    signed = jnp.where(even, -pull, pull)
    coefficients = jnp.sum(jnp.where(chosen, signed, 0.0), axis=0, keepdims=True)
    lane128 = lax.broadcasted_iota(jnp.int32, (1, 128), 1)
    coefficient = jnp.zeros((1, 384), F32)
    for s in range(3):
        own = jnp.sum(jnp.where(lane128 == 3 * rank + s, coefficients, 0.0), axis=1, keepdims=True)
        coefficient = jnp.where((lane >= 96 * s) & (lane < 96 * s + 96), own, coefficient)
    coefficient = coefficient * living
    scale_pol = post_scale[1:2]
    shrink = scale_pol * scale_pol * scale_pol * (coefficient * totals[3:4]) / WIDTH
    rows_to_columns(r.table, [post_scale, coefficient, shrink])
    grad_result = r.table[0:TOK, 2:3] * r.readout[...].astype(F32)
    grad_summed = r.table[0:TOK, 1:2] * post_gain * grad_result - r.summed[1] * r.table[0:TOK, 3:4]
    pack_hidden(grad_summed, r.grad_buf, mine * SHARD)

    back_gather = Gather(r.grad_buf, SHARD, send["gather_back"], recv["gather_back"])
    back_gather.wave(0)
    for m, (hidden, out) in enumerate(((r.ref_hidden, r.ref_out), (r.pol_hidden, r.pol_out))):
        out[...] = (hidden[...].astype(F32) + r.summed[m] * r.table[0:TOK, m : m + 1] * post_gain).astype(BF16)
    for w in range(1, 7):
        back_gather.wave(w)
    unpack_features(r.grad_buf, SHARD, 0, r.normed, 0)

    r.grad_mixed[...] = jnp.zeros_like(r.grad_mixed)

    def mix_back(i, carry):
        at = pl.ds(aligned(512 * i, 512), 512)
        r.grad_mixed[...] += dot(r.normed[0:TOK, at], r.w_back[at, :])
        return carry

    lax.fori_loop(0, 9, mix_back, 0)

    def attend_back(i, carry):
        here = pl.ds(aligned(96 * i, 96), 96)
        at = pl.ds(aligned(TOK + 96 * i, 96), 96)
        cos, sin = r.cosine[...], r.sine[...]
        key, value = r.heads[at, 256:384], r.heads[at, 384:512]
        key_grad = jnp.zeros((96, HEAD), F32)
        value_grad = jnp.zeros((96, HEAD), F32)
        for g in range(2):
            query = r.heads[at, 128 * g : 128 * g + 128]
            incoming = r.grad_mixed[here, 128 * g : 128 * g + 128].astype(BF16)
            prob = r.probs[at, 128 * g : 128 * g + 96]
            cap = r.capped[at, 128 * g : 128 * g + 96] / SOFT_CAP
            grad_probs = dot(incoming, value, NT)
            value_grad = value_grad + dot(prob.astype(BF16), incoming, TN)
            centered = grad_probs - jnp.sum(grad_probs * prob, axis=1, keepdims=True)
            grad_scores = (prob * centered * (1.0 - cap * cap) * QUERY_SCALE).astype(BF16)
            query_grad = dot(grad_scores, key)
            key_grad = key_grad + dot(grad_scores, query, TN)
            r.grads[here, 128 * g : 128 * g + 128] = rope(query_grad, cos, -sin).astype(BF16)
        r.grads[here, 256:384] = rope(key_grad, cos, -sin).astype(BF16)
        r.grads[here, 384:512] = value_grad.astype(BF16)
        return carry

    lax.fori_loop(0, 3, attend_back, 0)

    query_factor = jnp.concatenate([r.b_query[...], jnp.zeros((RANK, 256), BF16)], axis=0)
    value_factor = jnp.concatenate([jnp.zeros((RANK, 128), BF16), r.b_value[...]], axis=0)
    hook = dot(r.grads[:, 0:256], query_factor, NT) + dot(r.grads[:, 384:512], value_factor, NT)
    r.grads[:, 512:640] = (ADAPTER_SCALE * hook).astype(BF16)
    r.hooks[0:TOK, :] = r.grads[:, 512:640].astype(F32)
    r.hooks[TOK:384, :] = jnp.zeros((384 - TOK, 128), F32)
    hooks = Exchange(r.hook_parts, 24, 16, mine, in_tensor, send["hooks"], recv["hooks"], r.hooks, True)
    own_rows = pl.ds(aligned(24 * mine, 8), 24)
    r.hook_parts[own_rows, :] = r.hooks[own_rows, :]
    hooks.start()
    pull_back = jnp.sum(r.grads[...].astype(F32) * r.linear[...], axis=1, keepdims=True)
    stats_back = Exchange(r.stats_back, 8, 16, mine, in_tensor, send["stats_back"], recv["stats_back"])
    r.summed[0, :, 0:128] = r.table[0:TOK, :]
    r.stats_back[pl.ds(aligned(8 * mine, 8), 8), :] = columns_to_rows(r.table, [pull_back])
    stats_back.start()
    factor_terms = ADAPTER_SCALE * dot(r.low[...], r.grads[:, 0:512], TN)
    own_factor = pl.ds(aligned(64 * rank, 64), 64)
    r.factors[own_factor, 0:256] = factor_terms[0:64, 0:256].astype(BF16)
    r.factors[own_factor, 256:384] = factor_terms[64:128, 384:512].astype(BF16)
    factors = Exchange(r.factors, 64, 8, rank, in_data, send["factors"], recv["factors"])
    factors.start()
    partial_products(r.grads, r.w_in, r.partial_back, 1)
    back_scatter = Scatter(
        r.partial_back, r.landing_back, SHARD, send["scatter_back"], recv["scatter_back"]
    )
    back_scatter.begin()

    hooks.wait()
    r.hook_whole[own_rows, :] = hooks.total()
    hook_whole = Exchange(
        r.hook_whole, 24, 16, mine, in_tensor, send["hook_whole"], recv["hook_whole"]
    )
    hook_whole.start()
    back_scatter.turn(0, r.result)
    hook_whole.wait()
    hook_low = r.hook_whole[0:TOK, :].astype(BF16)

    def adapter_main(t, carry):
        term = dot(r.normed[TOK : 2 * TOK, pl.ds(aligned(256 * t, 256), 256)], hook_low, TN)
        r.a_terms[pl.ds(aligned(288 * t, 32), 256), :] = term.astype(BF16)
        return carry

    lax.fori_loop(0, 16, adapter_main, 0)

    def adapter_tail(q, carry):
        term = dot(r.normed[TOK : 2 * TOK, pl.ds(aligned(MAIN + 128 * q, 128), 128)], hook_low, TN)
        for j in range(4):
            at = aligned(288 * (4 * q + j) + 256, 32)
            r.a_terms[pl.ds(at, 32), :] = term[32 * j : 32 * j + 32, :].astype(BF16)
        return carry

    lax.fori_loop(0, 4, adapter_tail, 0)

    def across(i):
        return pltpu.make_async_remote_copy(
            src_ref=r.a_terms.at[pl.ds(aligned(576 * (2 * i + 1 - core), 64), 576), :],
            dst_ref=r.a_across.at[pl.ds(576 * i, 576), :],
            send_sem=send["across"].at[i],
            recv_sem=recv["across"].at[i],
            device_id={"dp_1": 1 - core},
            device_id_type=MESH,
        )

    def round_y(i):
        to = lax.rem(y + i, 4)
        return pltpu.make_async_remote_copy(
            src_ref=r.a_pairs.at[pl.ds(aligned(576 * to, 64), 576), :],
            dst_ref=r.a_round.at[pl.ds(576 * i, 576), :],
            send_sem=send["round"].at[i],
            recv_sem=recv["round"].at[i],
            device_id={"dp_0": to},
            device_id_type=MESH,
        )

    for i in range(4):
        across(i).start()
    back_scatter.turn(1, r.result)
    for i in range(4):
        across(i).wait_recv()
        own = r.a_terms[pl.ds(aligned(576 * (2 * i + core), 64), 576), :].astype(F32)
        pair = own + r.a_across[576 * i : 576 * i + 576, :].astype(F32)
        r.a_pairs[576 * i : 576 * i + 576, :] = pair.astype(BF16)
    for i in range(1, 4):
        round_y(i).start()
    back_scatter.turn(2, r.result)

    stats_back.wait()
    rows_to_columns(r.table, [stats_back.total()])
    unpack_result(r.result, 0, r.summed.at[1])
    pre_scale = r.scale[TOK : 2 * TOK, 0:1]
    shrink_back = pre_scale * pre_scale * r.table[0:TOK, 0:1] / WIDTH
    grad_result = r.summed[0, :, 2:3] * r.readout[...].astype(F32)
    hidden = r.pol_hidden[...].astype(F32)
    r.grad_hidden[...] = (
        grad_result + pre_scale * pre_gain * r.summed[1] - hidden * shrink_back
    ).astype(BF16)
    factors.wait()
    factor_total = factors.total()
    r.query_grad[...] = factor_total[:, 0:256]
    r.value_grad[...] = factor_total[:, 256:384]
    whole = r.a_pairs[pl.ds(aligned(576 * y, 64), 576), :].astype(F32)
    for i in range(1, 4):
        round_y(i).wait_recv()
        whole = whole + r.a_round[576 * i : 576 * i + 576, :].astype(F32)
    r.grad_a[...] = whole
    for ring in (gather, weights, scatter, back_gather, back_scatter):
        ring.drain()
    for exchange in (stats, scores, hooks, hook_whole, stats_back, factors):
        exchange.drain()
    for i in range(4):
        across(i).wait_send()
    for i in range(1, 4):
        round_y(i).wait_send()


def partial_products(rows, matrix, partial, models):
    def main(t, carry):
        product = dot(rows[...], matrix[pl.ds(aligned(256 * t, 256), 256), :], NT).astype(BF16)
        for m in range(models):
            for half in range(2):
                at = aligned((t * models + m) * SHARD + TOK * half, 16)
                partial[pl.ds(at, TOK), :] = product[m * TOK : m * TOK + TOK, 128 * half : 128 * half + 128]
        return carry

    lax.fori_loop(0, 16, main, 0)

    def tail(q, carry):
        product = dot(rows[...], matrix[pl.ds(aligned(MAIN + 128 * q, 128), 128), :], NT).astype(BF16)
        for m in range(models):
            for j in range(4):
                at = aligned(((4 * q + j) * models + m) * SHARD + 2 * TOK, 16)
                partial[pl.ds(at, GROUP), :] = pack_tail(product[m * TOK : m * TOK + TOK, 32 * j : 32 * j + 32])
        return carry

    lax.fori_loop(0, 4, tail, 0)


def rotation_tables():
    spacing = ROPE_BASE ** (-2.0 * np.arange(64, dtype=np.float32) / HEAD)
    angles = np.arange(LENGTH, dtype=np.float32)[:, None] * spacing.astype(np.float32)[None, :]
    cosine, sine = np.cos(angles), np.sin(angles)
    return (
        np.concatenate([cosine, cosine], axis=1).astype(np.float32),
        np.concatenate([-sine, sine], axis=1).astype(np.float32),
    )


INPUTS = [
    "lengths", "pairing", "ref_hidden", "pol_hidden", "readout", "w_query", "w_key", "w_value", "w_out", "a_query",
    "a_value", "b_query", "b_value", "pre_gain", "post_gain", "cosine", "sine",
]
OUTPUTS = ["pol_out", "ref_out", "loss", "grad_hidden", "grad_a", "query_grad", "value_grad"]


def body(
    ref_hidden,
    pol_hidden,
    readout,
    lengths,
    pairing,
    pre_gain,
    post_gain,
    w_query,
    w_key,
    value_projection,
    w_out,
    a_query,
    a_value,
    query_second_factor,
    value_second_factor,
):
    vmem, smem = pl.BlockSpec(memory_space=pltpu.VMEM), pl.BlockSpec(memory_space=pltpu.SMEM)
    cosine, sine = rotation_tables()
    semaphores = [pltpu.SemaphoreType.DMA(shape) for shape in SEMAPHORES.values() for _ in range(2)]
    tile = jax.ShapeDtypeStruct((TOK, TOK), BF16)
    results = pl.pallas_call(
        step_body,
        out_shape=(
            tile,
            tile,
            jax.ShapeDtypeStruct((8, 128), F32),
            tile,
            jax.ShapeDtypeStruct((576, 128), F32),
            jax.ShapeDtypeStruct((RANK, 256), F32),
            jax.ShapeDtypeStruct((RANK, 128), F32),
        ),
        in_specs=[smem, smem] + [vmem] * (len(INPUTS) - 2),
        out_specs=(vmem,) * len(OUTPUTS),
        scratch_shapes=[pltpu.VMEM(shape, kind) for shape, kind in SCRATCH.values()] + semaphores,
        compiler_params=pltpu.CompilerParams(
            collective_id=0, has_side_effects=True, vmem_limit_bytes=62 * 1024 * 1024
        ),
    )(
        lengths,
        pairing,
        ref_hidden,
        pol_hidden,
        readout,
        w_query,
        w_key,
        value_projection,
        w_out,
        a_query,
        a_value,
        query_second_factor,
        value_second_factor,
        pre_gain.reshape(16, TOK),
        post_gain.reshape(16, TOK),
        jnp.asarray(cosine),
        jnp.asarray(sine),
    )
    pol_out, ref_out, loss, grad_hidden, grad_a, query_grad, value_grad = results
    return (pol_out, ref_out, loss[0, 0], grad_hidden, grad_a, query_grad, value_grad)


def solution(mesh):
    torus = Mesh(mesh.devices.reshape(4, 2, 4, 4), ("dp_0", "dp_1", "tensor_0", "tensor_1"))
    split, rows, columns = P(DP, TENSOR), P(DP, None), P(None, TENSOR)
    return jax.shard_map(
        body,
        mesh=torus,
        in_specs=(split, split, split, P(DP), P(), P(), P(), split, split, split, split, rows, rows, columns, columns),
        out_specs=(split, split, P(), split, rows, columns, columns),
        check_vma=False,
    )
```

time: 573 us -> 198 us (0.35); the launches traced: 564 us -> 197 us
  blocking collectives: 191 us -> 0 us
  Pallas kernels: 0 us -> 185 us
  waiting for transfers between devices: 172 us -> 0 us
  local copies, waits for them, and re-layouts: 89.4 us -> 11.7 us
  matrix products: 45.7 us -> 0 us
  starting transfers between devices: 30.3 us -> 0 us
  other arithmetic: 20.1 us -> 0 us
  between operations: 15.2 us -> 0.66 us
    pallas_call x0 -> x1, Pallas kernels: none -> 185 us  [body(): pl.pallas_call(step_body, out_shape=(tile, tile, jax.ShapeDtypeStruct((8,...]
    psum x12 -> x0, blocking collectives: 108 us -> none  [one_axis_at_a_time(): return functools.reduce(lax.psum, axes, shard)]
    all_to_all x6 -> x0, waiting for transfers between devices: 104 us -> none  [the longest x3 71 us: summed_on_arrival(): lax.all_to_all(tiles, axis, split_axis=0, concat_axis=0, tiled=True)]
    all_to_all x2 -> x0, blocking collectives: 82.7 us -> none  [copy_for_each(): lax.all_to_all(jnp.broadcast_to(shard[None], (count, *shard.shape)), axis...]
    psum x1 -> x0, waiting for transfers between devices: 68 us -> none  [body(): lax.psum(input_terms.astype(jnp.bfloat16), TENSOR).astype(jnp.float32)]
    dot_general x30 -> x0, matrix products: 45.7 us -> none  [the longest x2 6 us: attention_layer(): query_rows = jnp.dot(normed, w_query, preferred_element_type=jnp.float32)]
    reshape x10 -> x2, local copies, waits for them, and re-layouts: 34.5 us -> 2.85 us  [the longest x1 1.44 us: body(): pre_gain.reshape(16, TOK)]
    all_to_all x6 -> x0, starting transfers between devices: 30.2 us -> none  [the longest x3 18.8 us: summed_on_arrival(): lax.all_to_all(tiles, axis, split_axis=0, concat_axis=0, tiled=True)]
  transfers between devices with their start and end apart: 8 -> 0, of which waited for: 7 -> 0; matrix products, arithmetic and copies ran while one was open for 14% -> 0% of each run, Pallas kernels for 0% -> 0%
where the time goes in v1:
time: 198 us; the launch traced here: 197 us
  Pallas kernels  185 us (93%)
  local copies, waits for them, and re-layouts  11.7 us (6%)
    pallas_call x1, Pallas kernels, body(): pl.pallas_call(step_body, out_shape=(tile, tile, jax.ShapeDtypeStruct((8,...  185 us
    unnamed x22, local copies, waits for them, and re-layouts  7.66 us

profile of v1, /device:TPU:0, one launch (start us, length us, event | category | flops | bytes accessed | tf_op | source)
XLA Modules:
  0.0 197.0 jit_solution(12678355078730246401)
XLA Ops:
  0.6 0.0 copy-start.3
  0.6 1.4 reshape.20.refs_13_
  2.1 1.4 reshape.21.refs_14_
  3.5 0.0 copy-done.3
  3.5 0.0 copy-start.4
  3.5 0.8 copy.24.refs_9_
  4.3 0.1 copy-done.4
  4.4 0.8 copy.25.refs_10_
  5.2 184.7 %shard_map.216 = (bf16[288,288]{1,0:T(8,128)(2,1)}, bf16[288,288]{1,0:T(8,128)(2,1)}, f32[8,128]{1,0:T(8,128)}, bf16[288,288]{1,0:T(8,128)(2,1)}, f32[576,128]{1...) custom-call(s32[3]{0:T(128)} %refs_0_.1, s32[24]{0:T(128)} %refs_1_.1, bf16[288,288]{1,0:T(8,128)(2,1)} %refs_2_.1, ...), custom_call_target="tpu_custom_call" | custom-call | tf_op jit(solution)/shard_map/pallas_call | solution.py:852
  189.9 1.2 slice.3
  191.1 0.0 copy-start.2
  191.1 1.7 copy.32
  192.7 0.0 copy-done.2
  192.8 0.0 copy-start.1
  192.8 0.7 copy.33
  193.4 0.3 copy-done.1
  193.8 0.0 copy-start
  193.8 0.7 copy.34
  194.5 0.4 copy-done
  194.8 0.0 copy-start.5
  194.8 0.7 copy.35
  195.5 0.1 copy-done.5
  195.7 0.0 copy-start.6
  195.7 0.6 copy.36
  196.3 0.1 copy-done.6
  196.4 0.6 copy.37
Async XLA Ops:
  0.6 2.9 %copy-start.3 = (bf16[576,64]{0,1:T(8,128)(2,1)S(1)}, bf16[576,64]{0,1:T(8,128)(2,1)}, u32[]{:S(2)}) copy-start(bf16[576,64]{0,1:T(8,128)(2,1)} %param.28) | copy-start | bytes 221188
  3.5 0.9 copy-start.4
  191.1 1.7 copy-start.2
  192.8 1.0 copy-start.1
  193.8 1.0 copy-start
  194.8 0.9 copy-start.5
  195.7 0.8 copy-start.6

commit v2 on v1

--- a/solution.py
+++ b/solution.py
@@ -29,6 +29,8 @@
 MAIN = 4096
 RINGS = ((0, 1), (0, -1), (1, 1), (1, -1))
 
+ORDER = (2, 1, 3, 0)
+
 F32 = jnp.float32
 BF16 = jnp.bfloat16
 NT = (((1,), (1,)), ((), ()))
@@ -67,10 +69,10 @@
         px, pz = (a, b) if primary == 0 else (b, a)
         return aligned((4 * px + pz) * self.rows + self.starts[k], 16)
 
-    def next_on(self, k, secondary):
+    def next_on(self, k, secondary, behind=False):
         primary, way = RINGS[k]
         axis = 1 - primary if secondary else primary
-        return {TENSOR[axis]: back(self.at[axis], -1, way)}
+        return {TENSOR[axis]: back(self.at[axis], 1 if behind else -1, way)}
 
     def remote(self, source, target, k, number, device):
         return pltpu.make_async_remote_copy(
@@ -91,47 +93,57 @@
     def piece(self, k, j, s):
         return self.buffer.at[pl.ds(self.place(k, j, s), self.sizes[k]), :]
 
-    def number(self, secondary, j, s):
-        return 3 + 3 * j + s if secondary else j
-
-    def copy(self, k, secondary, j, s):
+    def first(self, k, number):
+        piece = self.piece(k, 1 if number == 1 else 0, 0)
+        return self.remote(piece, piece, k, number, self.next_on(k, False, number == 2))
+
+    def second(self, k, j, s):
         piece = self.piece(k, j, s)
-        return self.remote(piece, piece, k, self.number(secondary, j, s), self.next_on(k, secondary))
-
-    def start(self, secondary, j, s):
+        return self.remote(piece, piece, k, 3 + 3 * j + s, self.next_on(k, True))
+
+    def begin(self):
         for k in range(4):
-            self.copy(k, secondary, j, s).start()
-
-    def wait(self, k, secondary, j, s):
-        piece = self.piece(k, j, s + 1) if secondary else self.piece(k, j + 1, s)
-        self.remote(piece, piece, k, self.number(secondary, j, s), self.next_on(k, secondary)).wait_recv()
-
-    def wave(self, w):
-        if w == 0:
-            self.start(False, 0, 0)
-            self.start(True, 0, 0)
-            return
-        if w <= 3:
-            for k in range(4):
-                self.wait(k, False, w - 1, 0)
-                if w < 3:
-                    self.copy(k, False, w, 0).start()
-                self.copy(k, True, w, 0).start()
-        for s in range(3):
-            j = w - 1 - s
-            if 0 <= j <= 3:
-                for k in range(4):
-                    self.wait(k, True, j, s)
-                    if s < 2:
-                        self.copy(k, True, j, s + 1).start()
+            self.first(k, 0).start()
+            self.first(k, 2).start()
+        for k in range(4):
+            self.second(k, 0, 0).start()
+
+    def await_first(self, number):
+        j = number + 1
+        for k in range(4):
+            piece = self.piece(k, j, 0)
+            self.remote(piece, piece, k, number, self.next_on(k, False)).wait_recv()
+            if number == 0:
+                self.first(k, 1).start()
+            self.second(k, j, 0).start()
+
+    def await_second(self, j, s):
+        for k in range(4):
+            piece = self.piece(k, j, s + 1)
+            self.remote(piece, piece, k, 3 + 3 * j + s, self.next_on(k, True)).wait_recv()
+            if s < 2:
+                self.second(k, j, s + 1).start()
+
+    def steps(self):
+        self.await_first(0)
+        yield
+        self.await_first(2)
+        yield
+        self.await_second(0, 0)
+        yield
+        self.await_first(1)
+        yield
+        for j, s in ((1, 0), (3, 0), (0, 1), (2, 0), (1, 1), (3, 1), (0, 2), (2, 1), (1, 2), (3, 2), (2, 2)):
+            self.await_second(j, s)
+            yield
 
     def drain(self):
         for k in range(4):
-            for j in range(3):
-                self.copy(k, False, j, 0).wait_send()
+            for number in range(3):
+                self.first(k, number).wait_send()
             for j in range(4):
                 for s in range(3):
-                    self.copy(k, True, j, s).wait_send()
+                    self.second(k, j, s).wait_send()
 
 
 class Scatter(Ring):
@@ -147,10 +159,11 @@
 
     def outer(self, k, j, s):
         number = 3 * j + s
-        return self.remote(self.piece(k, j + 1, s + 1), self.slot(k, number), k, number, self.next_on(k, True))
-
-    def inner(self, k, s):
-        return self.remote(self.piece(k, s + 1, 0), self.slot(k, 12 + s), k, 12 + s, self.next_on(k, False))
+        return self.remote(self.piece(k, ORDER[j], s + 1), self.slot(k, number), k, number, self.next_on(k, True))
+
+    def inner(self, k, number):
+        piece = self.piece(k, (2, 3, 1)[number - 12], 0)
+        return self.remote(piece, self.slot(k, number), k, number, self.next_on(k, False, number == 14))
 
     def add(self, k, number, first, second):
         piece, slot = self.piece(k, first, second), self.slot(k, number)
@@ -161,36 +174,38 @@
             for k in range(4):
                 self.outer(k, j, 0).start()
 
-    def run(self, result):
+    def steps(self, result):
         for s in range(3):
-            self.turn(s, result)
-
-    def turn(self, s, result):
-        for j in range(4):
-            for k in range(4):
-                self.outer(k, j, s).wait_recv()
-                self.add(k, 3 * j + s, j + 1, s + 2)
-                if s < 2:
-                    self.outer(k, j, s + 1).start()
-                    continue
-                if j == 0:
-                    self.inner(k, 0).start()
-                    continue
-                self.inner(k, j - 1).wait_recv()
-                if j < 3:
-                    self.add(k, 12 + j - 1, j + 1, 0)
-                    self.inner(k, j).start()
-                else:
-                    own = self.piece(k, 0, 0)[...].astype(F32) + self.slot(k, 14)[...].astype(F32)
-                    result[pl.ds(self.starts[k], self.sizes[k]), :] = own
+            for j in range(4):
+                for k in range(4):
+                    self.outer(k, j, s).wait_recv()
+                    self.add(k, 3 * j + s, ORDER[j], s + 2)
+                    if s < 2:
+                        self.outer(k, j, s + 1).start()
+                    elif j == 0:
+                        self.inner(k, 12).start()
+                    elif j == 1:
+                        self.inner(k, 14).start()
+                    elif j == 2:
+                        self.inner(k, 12).wait_recv()
+                        self.add(k, 12, 3, 0)
+                        self.inner(k, 13).start()
+                yield
+        for k in range(4):
+            own = self.piece(k, 0, 0)[...].astype(F32)
+            for number in (14, 13):
+                self.inner(k, number).wait_recv()
+                own = own + self.slot(k, number)[...].astype(F32)
+            result[pl.ds(self.starts[k], self.sizes[k]), :] = own
+        yield
 
     def drain(self):
         for k in range(4):
             for j in range(4):
                 for s in range(3):
                     self.outer(k, j, s).wait_send()
-            for s in range(3):
-                self.inner(k, s).wait_send()
+            for number in range(12, 15):
+                self.inner(k, number).wait_send()
 
 
 class Weights:
@@ -202,9 +217,11 @@
     def block(self, hops, half, part, core):
         way = 1 - 2 * half
         tile = 2 * (2 * back(self.y, hops, way) + core) + half
-        ref = self.w_in if part < 2 else self.w_back
-        if part % 2 == 0:
-            return ref.at[pl.ds(aligned(256 * tile, 256), 256), :]
+        if part < 2:
+            return self.w_in.at[pl.ds(aligned(256 * tile + 128 * part, 128), 128), :]
+        if part == 3:
+            return self.w_back.at[pl.ds(aligned(256 * tile, 256), 256), :]
+        ref = self.w_in if part == 2 else self.w_back
         return ref.at[pl.ds(aligned(MAIN + 32 * tile, 32), 32), :]
 
     def round(self, s, half, part, arriving=False):
@@ -230,8 +247,8 @@
         )
 
     def step(self, s, parts):
-        for half in range(2):
-            for part in parts:
+        for part in parts:
+            for half in range(2):
                 if s > 0:
                     self.round(s - 1, half, part, True).wait_recv()
                 if s < 3:
@@ -246,7 +263,7 @@
 
     def drain(self):
         for half in range(2):
-            for part in range(4):
+            for part in range(5):
                 for s in range(3):
                     self.round(s, half, part).wait_send()
                 for i in range(4):
@@ -310,6 +327,14 @@
     return {"dp_0": lax.div(i, 2), "dp_1": lax.rem(i, 2)}
 
 
+def together(main, filler, ratio):
+    for number, _ in enumerate(main):
+        for _ in range(ratio if isinstance(ratio, int) else ratio[number]):
+            next(filler, None)
+    for _ in filler:
+        pass
+
+
 def greet(peers):
     barrier = pltpu.get_barrier_semaphore()
     for peer in peers:
@@ -364,15 +389,35 @@
     buffer[pl.ds(aligned(base + 2 * TOK, 16), GROUP), :] = pack_tail(hidden[:, 256:288]).astype(BF16)
 
 
-def gain_tile(gain, c):
-    if c < 32:
-        return gain[c // 2 : c // 2 + 1, 128 * (c % 2) : 128 * (c % 2) + 128]
-    return jnp.concatenate([gain[4 * (c - 32) + j : 4 * (c - 32) + j + 1, 256:288] for j in range(4)], axis=1)
-
-
-def normalize(normed, scale_ref, gain_ref, models):
+def feature_lanes(gain, start, count):
+    pieces = []
+    while count:
+        row, lane = divmod(start, 128)
+        size = min(count, 128 - lane)
+        pieces.append(gain[row : row + 1, lane : lane + size])
+        start, count = start + size, count - size
+    return pieces[0] if len(pieces) == 1 else jnp.concatenate(pieces, axis=1)
+
+
+def order_gain(gain, target):
+    for c in range(32):
+        target[c : c + 1, :] = feature_lanes(gain, 288 * (c // 2) + 128 * (c % 2), 128)
+    for q in range(4):
+        tails = [feature_lanes(gain, 288 * (4 * q + j) + 256, 32) for j in range(4)]
+        target[32 + q : 33 + q, :] = jnp.concatenate(tails, axis=1)
+
+
+def own_gain(ordered, mine):
+    tail = ordered[pl.ds(32 + lax.div(mine, 4), 1), :]
+    picked = jnp.zeros((1, 32), F32)
+    for j in range(4):
+        picked = jnp.where(lax.rem(mine, 4) == j, tail[:, 32 * j : 32 * j + 32], picked)
+    return jnp.concatenate([ordered[pl.ds(2 * mine, 1), :], ordered[pl.ds(2 * mine + 1, 1), :], picked], axis=1)
+
+
+def normalize(normed, scale_ref, gain_ref, offset):
     def rows(i, carry):
-        at = pl.ds(aligned(96 * i, 96), 96)
+        at = pl.ds(aligned(offset + 96 * i, 96), 96)
         squares = jnp.zeros((96, 128), F32)
         for c in range(36):
             x = normed[at, 128 * c : 128 * c + 128].astype(F32)
@@ -381,10 +426,10 @@
         scale_ref[at, :] = jnp.broadcast_to(scale, (96, 128))
         for c in range(36):
             x = normed[at, 128 * c : 128 * c + 128].astype(F32)
-            normed[at, 128 * c : 128 * c + 128] = (x * scale * gain_tile(gain_ref, c)).astype(BF16)
+            normed[at, 128 * c : 128 * c + 128] = (x * scale * gain_ref[c : c + 1, :]).astype(BF16)
         return carry
 
-    lax.fori_loop(0, 3 * models, rows, 0)
+    lax.fori_loop(0, 3, rows, 0)
 
 
 def rope(x, cosine, sine):
@@ -426,12 +471,18 @@
     "mixed": ((2 * TOK, 256), BF16),
     "probs": ((2 * TOK, 256), F32),
     "capped": ((2 * TOK, 256), F32),
-    "partial": ((32 * SHARD, 128), BF16),
-    "landing": ((30 * SHARD, 128), BF16),
-    "result": ((2 * SHARD, 128), F32),
+    "partial": ((16 * SHARD, 128), BF16),
+    "partial_pol": ((16 * SHARD, 128), BF16),
+    "landing": ((15 * SHARD, 128), BF16),
+    "landing_pol": ((15 * SHARD, 128), BF16),
+    "result": ((2, SHARD, 128), F32),
     "summed": ((2, TOK, TOK), F32),
     "table": ((384, 128), F32),
-    "stats": ((16 * 8, 384), F32),
+    "coefficient": ((384, 128), F32),
+    "ref_stats": ((16 * 8, 384), F32),
+    "pol_stats": ((16 * 16, 128), F32),
+    "pre_ordered": ((40, 128), F32),
+    "post_ordered": ((40, 128), F32),
     "scores": ((8 * 8, 128), F32),
     "grad_buf": ((16 * SHARD, 128), BF16),
     "grad_mixed": ((TOK, 256), F32),
@@ -450,12 +501,14 @@
 }
 SEMAPHORES = {
     "gather": (4, 15),
-    "scatter": (4, 15),
+    "scatter_ref": (4, 15),
+    "scatter_pol": (4, 15),
     "gather_back": (4, 15),
     "scatter_back": (4, 15),
-    "y": (2, 3, 4),
-    "d": (2, 4, 4),
-    "stats": (16,),
+    "y": (2, 3, 5),
+    "d": (2, 4, 5),
+    "ref_stats": (16,),
+    "pol_stats": (16,),
     "scores": (8,),
     "hooks": (16,),
     "hook_whole": (16,),
@@ -482,9 +535,10 @@
     x, z = lax.axis_index("tensor_0"), lax.axis_index("tensor_1")
     y, core = lax.axis_index("dp_0"), lax.axis_index("dp_1")
     mine, rank = 4 * x + z, 2 * y + core
-    base = mine * 2 * SHARD
-    pack_hidden(r.ref_hidden[...], r.hidden_buf, base)
-    pack_hidden(r.pol_hidden[...], r.hidden_buf, base + SHARD)
+    pack_hidden(r.ref_hidden[...], r.hidden_buf, mine * 2 * SHARD)
+    pack_hidden(r.pol_hidden[...], r.hidden_buf, mine * 2 * SHARD + SHARD)
+    a_both = jnp.concatenate([r.a_query[...].astype(F32), r.a_value[...].astype(F32)], axis=0)
+    a_both = jnp.transpose(jnp.concatenate([a_both, jnp.zeros((128, 64), F32)], axis=1))
     for half in range(2):
         tile = 2 * rank + half
         for start, size, to in ((0, 256, 256 * tile), (256, 32, MAIN + 32 * tile)):
@@ -492,7 +546,7 @@
             r.w_in[there, 0:256] = r.w_query[here, :]
             r.w_in[there, 256:384] = r.w_key[here, :]
             r.w_in[there, 384:512] = r.w_value[here, :]
-            r.w_in[there, 512:640] = jnp.concatenate([r.a_query[here, :], r.a_value[here, :]], axis=1)
+            r.w_in[there, 512:640] = a_both[288 * half + start : 288 * half + start + size, :].astype(BF16)
             r.w_back[there, :] = r.w_out[here, :]
     greet(
         [in_tensor(lax.rem(mine + i, 16)) for i in range(1, 16)]
@@ -501,157 +555,231 @@
 
     gather = Gather(r.hidden_buf, 2 * SHARD, send["gather"], recv["gather"])
     weights = Weights(r.w_in, r.w_back, send["y"], recv["y"], send["d"], recv["d"])
-    gather.wave(0)
-    weights.step(0, (0, 1))
-    gather.wave(1)
-    gather.wave(2)
-    weights.step(1, (0, 1))
-    gather.wave(3)
-    gather.wave(4)
-    weights.step(2, (0, 1))
-    weights.step(0, (2, 3))
-    gather.wave(5)
-    gather.wave(6)
+
+    def weight_steps():
+        for s in range(1, 3):
+            weights.step(s, (0,))
+            yield
+            weights.step(s, (1,))
+            if s == 1:
+                weights.step(s, (2,))
+            yield
+        weights.step(2, (2,))
+        weights.step(0, (3, 4))
+        yield
+        for part in range(3):
+            weights.step(3, (part,))
+            yield
+        weights.step(1, (3, 4))
+        yield
+
+    gather.begin()
+    weights.step(0, (0, 1, 2))
+    gain = r.pre_ordered
+    order_gain(r.pre_gain, gain)
+    order_gain(r.post_gain, r.post_ordered)
+    pre_gain, post_gain = own_gain(gain, mine), own_gain(r.post_ordered, mine)
+    together(gather.steps(), weight_steps(), (0, 1, 1, 0, 1, 1, 0, 1, 1, 0, 1, 1, 0, 1, 0))
+
+    def project(m):
+        rows = slice(m * TOK, m * TOK + TOK)
+        for i in range(3):
+            total = None
+            for c in range(3 * i, 3 * i + 3):
+                term = dot(r.normed[rows, 512 * c : 512 * c + 512], r.w_in[512 * c : 512 * c + 512, :])
+                total = term if total is None else total + term
+            r.acc[rows, :] = total if i == 0 else r.acc[rows, :] + total
+            yield
+
+    def attend(m):
+        for i in range(3):
+            at = slice(m * TOK + 96 * i, m * TOK + 96 * i + 96)
+            cos, sin = r.cosine[...], r.sine[...]
+            key = rope(r.acc[at, 256:384], cos, sin).astype(BF16)
+            value = r.acc[at, 384:512].astype(BF16)
+            allowed = allowed_here(r.lengths[i])
+            r.heads[at, 256:384] = key
+            r.heads[at, 384:512] = value
+            for g in range(2):
+                query = rope(r.acc[at, 128 * g : 128 * g + 128], cos, sin).astype(BF16)
+                r.heads[at, 128 * g : 128 * g + 128] = query
+                scores = dot(query, key, NT) * QUERY_SCALE
+                cap = SOFT_CAP * jnp.tanh(scores / SOFT_CAP)
+                weight = jnp.where(allowed, jnp.exp(cap), 0.0)
+                prob = weight / jnp.sum(weight, axis=1, keepdims=True)
+                r.probs[at, 128 * g : 128 * g + 96] = prob
+                r.capped[at, 128 * g : 128 * g + 96] = cap
+                r.mixed[at, 128 * g : 128 * g + 128] = dot(prob.astype(BF16), value).astype(BF16)
+            yield
+
     unpack_features(r.hidden_buf, 2 * SHARD, 0, r.normed, 0)
-    unpack_features(r.hidden_buf, 2 * SHARD, SHARD, r.normed, TOK)
-    normalize(r.normed, r.scale, r.pre_gain, 2)
-    weights.step(3, (0, 1))
-    weights.arrive((0, 1))
-
-    acc = r.acc
-    acc[...] = jnp.zeros_like(acc)
-
-    def project(i, carry):
-        at = pl.ds(aligned(512 * i, 512), 512)
-        acc[...] += dot(r.normed[:, at], r.w_in[at, :])
-        return carry
-
-    lax.fori_loop(0, 9, project, 0)
-    weights.step(1, (2, 3))
-
-    r.linear[...] = acc[TOK : 2 * TOK, :]
-    r.low[...] = acc[TOK : 2 * TOK, 512:640].astype(BF16)
-    query_factor = jnp.concatenate([r.b_query[...], jnp.zeros((RANK, 256), BF16)], axis=0)
-    value_factor = jnp.concatenate([jnp.zeros((RANK, 128), BF16), r.b_value[...]], axis=0)
-    acc[TOK : 2 * TOK, 0:256] += ADAPTER_SCALE * dot(r.low[...], query_factor)
-    acc[TOK : 2 * TOK, 384:512] += ADAPTER_SCALE * dot(r.low[...], value_factor)
-
-    def attend(i, carry):
-        at = pl.ds(aligned(96 * i, 96), 96)
-        cos, sin = r.cosine[...], r.sine[...]
-        key = rope(acc[at, 256:384], cos, sin).astype(BF16)
-        value = acc[at, 384:512].astype(BF16)
-        allowed = allowed_here(r.lengths[lax.rem(i, 3)])
-        r.heads[at, 256:384] = key
-        r.heads[at, 384:512] = value
-        for g in range(2):
-            query = rope(acc[at, 128 * g : 128 * g + 128], cos, sin).astype(BF16)
-            r.heads[at, 128 * g : 128 * g + 128] = query
-            scores = dot(query, key, NT) * QUERY_SCALE
-            cap = SOFT_CAP * jnp.tanh(scores / SOFT_CAP)
-            weight = jnp.where(allowed, jnp.exp(cap), 0.0)
-            prob = weight / jnp.sum(weight, axis=1, keepdims=True)
-            r.probs[at, 128 * g : 128 * g + 96] = prob
-            r.capped[at, 128 * g : 128 * g + 96] = cap
-            r.mixed[at, 128 * g : 128 * g + 128] = dot(prob.astype(BF16), value).astype(BF16)
-        return carry
-
-    lax.fori_loop(0, 6, attend, 0)
-    weights.step(2, (2, 3))
-    weights.step(3, (2, 3))
-    weights.arrive((2, 3))
-    partial_products(r.mixed, r.w_back, r.partial, 2)
-
-    scatter = Scatter(r.partial, r.landing, 2 * SHARD, send["scatter"], recv["scatter"])
-    scatter.begin()
-    scatter.run(r.result)
-    for m in range(2):
-        unpack_result(r.result, m * SHARD, r.summed.at[m])
-
-    post_gain = r.post_gain[pl.ds(mine, 1), :]
-    pre_gain = r.pre_gain[pl.ds(mine, 1), :]
-    columns = [[], [], []]
-    for m, hidden in enumerate((r.ref_hidden, r.pol_hidden)):
+    normalize(r.normed, r.scale, gain, 0)
+    weights.arrive((0, 1, 2))
+    weights.step(2, (3, 4))
+    for _ in project(0):
+        pass
+    for _ in attend(0):
+        pass
+    weights.step(3, (3, 4))
+    weights.arrive((3, 4))
+    for _ in partial_products(r.mixed.at[0:TOK], r.w_back, r.partial):
+        pass
+    ref_scatter = Scatter(r.partial, r.landing, SHARD, send["scatter_ref"], recv["scatter_ref"])
+    ref_scatter.begin()
+    pol_scatter = Scatter(r.partial_pol, r.landing_pol, SHARD, send["scatter_pol"], recv["scatter_pol"])
+
+    def policy():
+        unpack_features(r.hidden_buf, 2 * SHARD, SHARD, r.normed, TOK)
+        yield
+        normalize(r.normed, r.scale, gain, TOK)
+        yield
+        yield from project(1)
+        r.linear[...] = r.acc[TOK : 2 * TOK, :]
+        r.low[...] = r.acc[TOK : 2 * TOK, 512:640].astype(BF16)
+        query_factor = jnp.concatenate([r.b_query[...], jnp.zeros((RANK, 256), BF16)], axis=0)
+        value_factor = jnp.concatenate([jnp.zeros((RANK, 128), BF16), r.b_value[...]], axis=0)
+        r.acc[TOK : 2 * TOK, 0:256] += ADAPTER_SCALE * dot(r.low[...], query_factor)
+        r.acc[TOK : 2 * TOK, 384:512] += ADAPTER_SCALE * dot(r.low[...], value_factor)
+        yield
+        yield from attend(1)
+        yield from partial_products(r.mixed.at[TOK : 2 * TOK], r.w_back, r.partial_pol)
+        pol_scatter.begin()
+        yield
+
+    def token_sums(m, hidden):
+        unpack_result(r.result.at[m], 0, r.summed.at[m])
         summed, readout = r.summed[m], r.readout[...].astype(F32)
-        columns[0].append(jnp.sum(summed * summed, axis=1, keepdims=True))
-        columns[1].append(jnp.sum(summed * post_gain * readout, axis=1, keepdims=True))
-        columns[2].append(jnp.sum(hidden[...].astype(F32) * readout, axis=1, keepdims=True))
-    stats = Exchange(r.stats, 8, 16, mine, in_tensor, send["stats"], recv["stats"])
-    r.stats[pl.ds(aligned(8 * mine, 8), 8), :] = columns_to_rows(r.table, sum(columns, []))
-    stats.start()
-    stats.wait()
-    totals = stats.total()
-    post_scale = lax.rsqrt(totals[0:2] / WIDTH + NORM_EPS)
+        return [
+            jnp.sum(summed * summed, axis=1, keepdims=True),
+            jnp.sum(summed * post_gain * readout, axis=1, keepdims=True),
+            jnp.sum(hidden[...].astype(F32) * readout, axis=1, keepdims=True),
+        ]
+
+    ref_stats = Exchange(r.ref_stats, 8, 16, mine, in_tensor, send["ref_stats"], recv["ref_stats"])
+    pol_stats = Exchange(r.pol_stats, 16, 16, mine, in_tensor, send["pol_stats"], recv["pol_stats"])
+
+    def policy_ring():
+        yield from pol_scatter.steps(r.result.at[1])
+
+    def after_ref():
+        columns = columns_to_rows(r.table, token_sums(0, r.ref_hidden))
+        r.ref_stats[pl.ds(aligned(8 * mine, 8), 8), :] = columns
+        ref_stats.start()
+        yield
+
+    def fill(steps, count):
+        for _ in range(count):
+            next(steps, None)
+
+    ref_ring, policy_work, policy_steps = ref_scatter.steps(r.result.at[0]), policy(), policy_ring()
+    fill(policy_work, 3)
+    for count in (2, 2, 2, 2, 4):
+        fill(ref_ring, 1)
+        fill(policy_work, count)
+    for _ in policy_work:
+        pass
+    fill(ref_ring, 3)
+    for _ in range(5):
+        fill(ref_ring, 1)
+        fill(policy_steps, 1)
+    together(policy_steps, after_ref(), (1,) + (0,) * 12)
+    columns = columns_to_rows(r.table, token_sums(1, r.pol_hidden))
+    packed = [columns[k : k + 1, 128 * c : 128 * c + 128] for k in range(3) for c in range(3)]
+    packed = jnp.concatenate(packed + [jnp.zeros((7, 128), F32)], axis=0)
+    r.pol_stats[pl.ds(aligned(16 * mine, 8), 16), :] = packed
+    pol_stats.start()
+    pol_stats.wait()
+    packed = pol_stats.total()
+    pol_total = [
+        jnp.concatenate([packed[3 * k + c : 3 * k + c + 1] for c in range(3)], axis=1) for k in range(3)
+    ]
+    scale_pol = lax.rsqrt(pol_total[0] / WIDTH + NORM_EPS)
+    rows_to_columns(r.table, [scale_pol, scale_pol * scale_pol * scale_pol * pol_total[1] / WIDTH])
+    readout = r.readout[...].astype(F32)
+    bare = r.table[0:TOK, 0:1] * post_gain * readout - r.summed[1] * r.table[0:TOK, 1:2]
+    pack_hidden(bare, r.grad_buf, mine * SHARD)
+    back_gather = Gather(r.grad_buf, SHARD, send["gather_back"], recv["gather_back"])
+    back_gather.begin()
+
     lane = lax.broadcasted_iota(jnp.int32, (1, 384), 1)
     lengths = [r.lengths[s] for s in range(3)]
     living = jnp.zeros((1, 384), F32)
     for s in range(3):
         living = jnp.where((lane >= 96 * s) & (lane < 96 * s + lengths[s]), 1.0, living)
-    token_scores = (totals[4:6] + post_scale * totals[2:4]) * living
+    ref_stats.wait()
+    ref_total = ref_stats.total()
+    scale_ref = lax.rsqrt(ref_total[0:1] / WIDTH + NORM_EPS)
+    token_scores = (
+        (ref_total[2:3] + scale_ref * ref_total[1:2]) * living,
+        (pol_total[2] + scale_pol * pol_total[1]) * living,
+    )
     row8 = lax.broadcasted_iota(jnp.int32, (8, 128), 0)
     lane8 = lax.broadcasted_iota(jnp.int32, (8, 128), 1)
     tile = jnp.zeros((8, 128), F32)
     for m in range(2):
         for s in range(3):
             inside = (lane >= 96 * s) & (lane < 96 * s + 96)
-            score = jnp.sum(jnp.where(inside, token_scores[m : m + 1], 0.0), axis=1, keepdims=True)
+            score = jnp.sum(jnp.where(inside, token_scores[m], 0.0), axis=1, keepdims=True)
             tile = jnp.where((row8 == m) & (lane8 == 3 * rank + s), score, tile)
     scores = Exchange(r.scores, 8, 8, rank, in_data, send["scores"], recv["scores"])
     r.scores[pl.ds(aligned(8 * rank, 8), 8), :] = tile
     scores.start()
-    scores.wait()
-    everyone = scores.total()
-    ratio = everyone[1:2] - everyone[0:1]
-    row32 = lax.broadcasted_iota(jnp.int32, (32, 128), 0)
-    lane32 = lax.broadcasted_iota(jnp.int32, (32, 128), 1)
-    named = jnp.full((32, 128), -1, jnp.int32)
-    for k in range(24):
-        named = jnp.where(row32 == k, r.pairing[k], named)
-    chosen = named == lane32
-    even = lax.rem(row32, 2) == 0
-    picked = jnp.broadcast_to(jnp.sum(jnp.where(chosen, ratio, 0.0), axis=1, keepdims=True), (32, 128))
-    other = jnp.where(even, pltpu.roll(picked, 31, 0), pltpu.roll(picked, 1, 0))
-    margin = DPO_BETA * jnp.where(even, picked - other, other - picked)
-    loss = jnp.maximum(-margin, 0.0) + jnp.log1p(jnp.exp(-jnp.abs(margin)))
-    counted = even & (row32 < 24) & (lane32 == 0)
-    total_loss = jnp.sum(jnp.where(counted, loss, 0.0), axis=(0, 1), keepdims=True)
-    r.loss[...] = jnp.broadcast_to(total_loss, (8, 128))
-    pull = DPO_BETA * LOSS_SCALE / (1.0 + jnp.exp(margin))
-    signed = jnp.where(even, -pull, pull)
-    coefficients = jnp.sum(jnp.where(chosen, signed, 0.0), axis=0, keepdims=True)
-    lane128 = lax.broadcasted_iota(jnp.int32, (1, 128), 1)
-    coefficient = jnp.zeros((1, 384), F32)
-    for s in range(3):
-        own = jnp.sum(jnp.where(lane128 == 3 * rank + s, coefficients, 0.0), axis=1, keepdims=True)
-        coefficient = jnp.where((lane >= 96 * s) & (lane < 96 * s + 96), own, coefficient)
-    coefficient = coefficient * living
-    scale_pol = post_scale[1:2]
-    shrink = scale_pol * scale_pol * scale_pol * (coefficient * totals[3:4]) / WIDTH
-    rows_to_columns(r.table, [post_scale, coefficient, shrink])
-    grad_result = r.table[0:TOK, 2:3] * r.readout[...].astype(F32)
-    grad_summed = r.table[0:TOK, 1:2] * post_gain * grad_result - r.summed[1] * r.table[0:TOK, 3:4]
-    pack_hidden(grad_summed, r.grad_buf, mine * SHARD)
-
-    back_gather = Gather(r.grad_buf, SHARD, send["gather_back"], recv["gather_back"])
-    back_gather.wave(0)
-    for m, (hidden, out) in enumerate(((r.ref_hidden, r.ref_out), (r.pol_hidden, r.pol_out))):
-        out[...] = (hidden[...].astype(F32) + r.summed[m] * r.table[0:TOK, m : m + 1] * post_gain).astype(BF16)
-    for w in range(1, 7):
-        back_gather.wave(w)
+
+    def outputs():
+        rows_to_columns(r.coefficient, [scale_ref, scale_pol])
+        for m, (hidden, out) in enumerate(((r.ref_hidden, r.ref_out), (r.pol_hidden, r.pol_out))):
+            scale = r.coefficient[0:TOK, m : m + 1]
+            out[...] = (hidden[...].astype(F32) + r.summed[m] * scale * post_gain).astype(BF16)
+            yield
+
+    def preference():
+        scores.wait()
+        everyone = scores.total()
+        ratio = everyone[1:2] - everyone[0:1]
+        row32 = lax.broadcasted_iota(jnp.int32, (32, 128), 0)
+        lane32 = lax.broadcasted_iota(jnp.int32, (32, 128), 1)
+        named = jnp.full((32, 128), -1, jnp.int32)
+        for k in range(24):
+            named = jnp.where(row32 == k, r.pairing[k], named)
+        chosen = named == lane32
+        even = lax.rem(row32, 2) == 0
+        picked = jnp.sum(jnp.where(chosen, ratio, 0.0), axis=1, keepdims=True)
+        picked = jnp.broadcast_to(picked, (32, 128))
+        other = jnp.where(even, pltpu.roll(picked, 31, 0), pltpu.roll(picked, 1, 0))
+        margin = DPO_BETA * jnp.where(even, picked - other, other - picked)
+        loss = jnp.maximum(-margin, 0.0) + jnp.log1p(jnp.exp(-jnp.abs(margin)))
+        counted = even & (row32 < 24) & (lane32 == 0)
+        total_loss = jnp.sum(jnp.where(counted, loss, 0.0), axis=(0, 1), keepdims=True)
+        r.loss[...] = jnp.broadcast_to(total_loss, (8, 128))
+        pull = DPO_BETA * LOSS_SCALE / (1.0 + jnp.exp(margin))
+        signed = jnp.where(even, -pull, pull)
+        coefficients = jnp.sum(jnp.where(chosen, signed, 0.0), axis=0, keepdims=True)
+        lane128 = lax.broadcasted_iota(jnp.int32, (1, 128), 1)
+        coefficient = jnp.zeros((1, 384), F32)
+        for s in range(3):
+            own = jnp.sum(jnp.where(lane128 == 3 * rank + s, coefficients, 0.0), axis=1, keepdims=True)
+            coefficient = jnp.where((lane >= 96 * s) & (lane < 96 * s + 96), own, coefficient)
+        rows_to_columns(r.coefficient, [coefficient * living])
+        yield
+
+    def meanwhile():
+        yield from outputs()
+        yield from preference()
+
+    together(back_gather.steps(), meanwhile(), (1, 1, 0, 0, 0, 0, 0, 1, 0, 0, 0, 0, 0, 0, 0))
     unpack_features(r.grad_buf, SHARD, 0, r.normed, 0)
 
-    r.grad_mixed[...] = jnp.zeros_like(r.grad_mixed)
-
-    def mix_back(i, carry):
-        at = pl.ds(aligned(512 * i, 512), 512)
-        r.grad_mixed[...] += dot(r.normed[0:TOK, at], r.w_back[at, :])
-        return carry
-
-    lax.fori_loop(0, 9, mix_back, 0)
-
-    def attend_back(i, carry):
-        here = pl.ds(aligned(96 * i, 96), 96)
-        at = pl.ds(aligned(TOK + 96 * i, 96), 96)
+    for i in range(3):
+        total = None
+        for c in range(3 * i, 3 * i + 3):
+            term = dot(r.normed[0:TOK, 512 * c : 512 * c + 512], r.w_back[512 * c : 512 * c + 512, :])
+            total = term if total is None else total + term
+        r.grad_mixed[...] = total if i == 0 else r.grad_mixed[...] + total
+    r.grad_mixed[...] *= r.coefficient[0:TOK, 0:1]
+
+    for i in range(3):
+        here = slice(96 * i, 96 * i + 96)
+        at = slice(TOK + 96 * i, TOK + 96 * i + 96)
         cos, sin = r.cosine[...], r.sine[...]
         key, value = r.heads[at, 256:384], r.heads[at, 384:512]
         key_grad = jnp.zeros((96, HEAD), F32)
@@ -670,9 +798,6 @@
             r.grads[here, 128 * g : 128 * g + 128] = rope(query_grad, cos, -sin).astype(BF16)
         r.grads[here, 256:384] = rope(key_grad, cos, -sin).astype(BF16)
         r.grads[here, 384:512] = value_grad.astype(BF16)
-        return carry
-
-    lax.fori_loop(0, 3, attend_back, 0)
 
     query_factor = jnp.concatenate([r.b_query[...], jnp.zeros((RANK, 256), BF16)], axis=0)
     value_factor = jnp.concatenate([jnp.zeros((RANK, 128), BF16), r.b_value[...]], axis=0)
@@ -686,7 +811,6 @@
     hooks.start()
     pull_back = jnp.sum(r.grads[...].astype(F32) * r.linear[...], axis=1, keepdims=True)
     stats_back = Exchange(r.stats_back, 8, 16, mine, in_tensor, send["stats_back"], recv["stats_back"])
-    r.summed[0, :, 0:128] = r.table[0:TOK, :]
     r.stats_back[pl.ds(aligned(8 * mine, 8), 8), :] = columns_to_rows(r.table, [pull_back])
     stats_back.start()
     factor_terms = ADAPTER_SCALE * dot(r.low[...], r.grads[:, 0:512], TN)
@@ -695,37 +819,18 @@
     r.factors[own_factor, 256:384] = factor_terms[64:128, 384:512].astype(BF16)
     factors = Exchange(r.factors, 64, 8, rank, in_data, send["factors"], recv["factors"])
     factors.start()
-    partial_products(r.grads, r.w_in, r.partial_back, 1)
+    for _ in partial_products(r.grads, r.w_in, r.partial_back):
+        pass
     back_scatter = Scatter(
         r.partial_back, r.landing_back, SHARD, send["scatter_back"], recv["scatter_back"]
     )
-    back_scatter.begin()
-
-    hooks.wait()
-    r.hook_whole[own_rows, :] = hooks.total()
     hook_whole = Exchange(
         r.hook_whole, 24, 16, mine, in_tensor, send["hook_whole"], recv["hook_whole"]
     )
+    hooks.wait()
+    r.hook_whole[own_rows, :] = hooks.total()
     hook_whole.start()
-    back_scatter.turn(0, r.result)
-    hook_whole.wait()
-    hook_low = r.hook_whole[0:TOK, :].astype(BF16)
-
-    def adapter_main(t, carry):
-        term = dot(r.normed[TOK : 2 * TOK, pl.ds(aligned(256 * t, 256), 256)], hook_low, TN)
-        r.a_terms[pl.ds(aligned(288 * t, 32), 256), :] = term.astype(BF16)
-        return carry
-
-    lax.fori_loop(0, 16, adapter_main, 0)
-
-    def adapter_tail(q, carry):
-        term = dot(r.normed[TOK : 2 * TOK, pl.ds(aligned(MAIN + 128 * q, 128), 128)], hook_low, TN)
-        for j in range(4):
-            at = aligned(288 * (4 * q + j) + 256, 32)
-            r.a_terms[pl.ds(at, 32), :] = term[32 * j : 32 * j + 32, :].astype(BF16)
-        return carry
-
-    lax.fori_loop(0, 4, adapter_tail, 0)
+    back_scatter.begin()
 
     def across(i):
         return pltpu.make_async_remote_copy(
@@ -748,24 +853,36 @@
             device_id_type=MESH,
         )
 
-    for i in range(4):
-        across(i).start()
-    back_scatter.turn(1, r.result)
-    for i in range(4):
-        across(i).wait_recv()
-        own = r.a_terms[pl.ds(aligned(576 * (2 * i + core), 64), 576), :].astype(F32)
-        pair = own + r.a_across[576 * i : 576 * i + 576, :].astype(F32)
-        r.a_pairs[576 * i : 576 * i + 576, :] = pair.astype(BF16)
-    for i in range(1, 4):
-        round_y(i).start()
-    back_scatter.turn(2, r.result)
+    def adapters_back():
+        hook_whole.wait()
+        hook_low = r.hook_whole[0:TOK, :].astype(BF16)
+        for q in range(4):
+            at = MAIN + 128 * q
+            tail = dot(r.normed[TOK : 2 * TOK, at : at + 128], hook_low, TN).astype(BF16)
+            for t in range(4 * q, 4 * q + 4):
+                term = dot(r.normed[TOK : 2 * TOK, 256 * t : 256 * t + 256], hook_low, TN)
+                r.a_terms[288 * t : 288 * t + 256, :] = term.astype(BF16)
+                j = t - 4 * q
+                r.a_terms[288 * t + 256 : 288 * t + 288, :] = tail[32 * j : 32 * j + 32, :]
+            across(q).start()
+            yield
+        for i in range(4):
+            across(i).wait_recv()
+            own = r.a_terms[pl.ds(aligned(576 * (2 * i + core), 64), 576), :].astype(F32)
+            pair = own + r.a_across[576 * i : 576 * i + 576, :].astype(F32)
+            r.a_pairs[576 * i : 576 * i + 576, :] = pair.astype(BF16)
+        for i in range(1, 4):
+            round_y(i).start()
+        yield
+
+    together(back_scatter.steps(r.result.at[0]), adapters_back(), (0, 0, 1, 1, 1, 1, 0, 1, 0, 0, 0, 0, 0))
 
     stats_back.wait()
     rows_to_columns(r.table, [stats_back.total()])
-    unpack_result(r.result, 0, r.summed.at[1])
+    unpack_result(r.result.at[0], 0, r.summed.at[1])
     pre_scale = r.scale[TOK : 2 * TOK, 0:1]
     shrink_back = pre_scale * pre_scale * r.table[0:TOK, 0:1] / WIDTH
-    grad_result = r.summed[0, :, 2:3] * r.readout[...].astype(F32)
+    grad_result = r.coefficient[0:TOK, 0:1] * r.readout[...].astype(F32)
     hidden = r.pol_hidden[...].astype(F32)
     r.grad_hidden[...] = (
         grad_result + pre_scale * pre_gain * r.summed[1] - hidden * shrink_back
@@ -779,9 +896,9 @@
         round_y(i).wait_recv()
         whole = whole + r.a_round[576 * i : 576 * i + 576, :].astype(F32)
     r.grad_a[...] = whole
-    for ring in (gather, weights, scatter, back_gather, back_scatter):
+    for ring in (gather, weights, ref_scatter, pol_scatter, back_gather, back_scatter):
         ring.drain()
-    for exchange in (stats, scores, hooks, hook_whole, stats_back, factors):
+    for exchange in (ref_stats, pol_stats, scores, hooks, hook_whole, stats_back, factors):
         exchange.drain()
     for i in range(4):
         across(i).wait_send()
@@ -789,26 +906,20 @@
         round_y(i).wait_send()
 
 
-def partial_products(rows, matrix, partial, models):
-    def main(t, carry):
-        product = dot(rows[...], matrix[pl.ds(aligned(256 * t, 256), 256), :], NT).astype(BF16)
-        for m in range(models):
+def partial_products(rows, matrix, partial):
+    for block in range(4):
+        left = rows[...]
+        for t in range(4 * block, 4 * block + 4):
+            product = dot(left, matrix[256 * t : 256 * t + 256, :], NT).astype(BF16)
             for half in range(2):
-                at = aligned((t * models + m) * SHARD + TOK * half, 16)
-                partial[pl.ds(at, TOK), :] = product[m * TOK : m * TOK + TOK, 128 * half : 128 * half + 128]
-        return carry
-
-    lax.fori_loop(0, 16, main, 0)
-
-    def tail(q, carry):
-        product = dot(rows[...], matrix[pl.ds(aligned(MAIN + 128 * q, 128), 128), :], NT).astype(BF16)
-        for m in range(models):
-            for j in range(4):
-                at = aligned(((4 * q + j) * models + m) * SHARD + 2 * TOK, 16)
-                partial[pl.ds(at, GROUP), :] = pack_tail(product[m * TOK : m * TOK + TOK, 32 * j : 32 * j + 32])
-        return carry
-
-    lax.fori_loop(0, 4, tail, 0)
+                at = t * SHARD + TOK * half
+                partial[at : at + TOK, :] = product[:, 128 * half : 128 * half + 128]
+        at = MAIN + 128 * block
+        product = dot(left, matrix[at : at + 128, :], NT).astype(BF16)
+        for j in range(4):
+            at = (4 * block + j) * SHARD + 2 * TOK
+            partial[at : at + GROUP, :] = pack_tail(product[:, 32 * j : 32 * j + 32])
+        yield
 
 
 def rotation_tables():
@@ -826,6 +937,11 @@
     "a_value", "b_query", "b_value", "pre_gain", "post_gain", "cosine", "sine",
 ]
 OUTPUTS = ["pol_out", "ref_out", "loss", "grad_hidden", "grad_a", "query_grad", "value_grad"]
+
+
+def hand_out(*refs):
+    for source, target in zip(refs[: len(OUTPUTS)], refs[len(OUTPUTS) :]):
+        target[...] = source[0 : target.shape[0], 0 : target.shape[1]]
 
 
 def body(
@@ -876,17 +992,24 @@
         w_key,
         value_projection,
         w_out,
-        a_query,
-        a_value,
+        a_query.T,
+        a_value.T,
         query_second_factor,
         value_second_factor,
-        pre_gain.reshape(16, TOK),
-        post_gain.reshape(16, TOK),
+        pre_gain.reshape(36, 128),
+        post_gain.reshape(36, 128),
         jnp.asarray(cosine),
         jnp.asarray(sine),
     )
-    pol_out, ref_out, loss, grad_hidden, grad_a, query_grad, value_grad = results
-    return (pol_out, ref_out, loss[0, 0], grad_hidden, grad_a, query_grad, value_grad)
+    shapes = [jax.ShapeDtypeStruct(a.shape, a.dtype) for a in results]
+    shapes[2] = jax.ShapeDtypeStruct((1, 1), F32)
+    pol_out, ref_out, loss, grad_hidden, grad_a, query_grad, value_grad = pl.pallas_call(
+        hand_out,
+        out_shape=tuple(shapes),
+        in_specs=[vmem] * len(OUTPUTS),
+        out_specs=(vmem,) * len(OUTPUTS),
+    )(*results)
+    return (pol_out, ref_out, loss.reshape(()), grad_hidden, grad_a, query_grad, value_grad)
 
 
 def solution(mesh):

time: 198 us -> 158 us (0.80)
  Pallas kernels: 185 us -> 156 us
  local copies, waits for them, and re-layouts: 11.7 us -> 0 us
    pallas_call x1, Pallas kernels: 185 us -> 154 us  [body(): pl.pallas_call(step_body, out_shape=(tile, tile, jax.ShapeDtypeStruct((8,...]
    unnamed x22 -> x0, local copies, waits for them, and re-layouts: 7.66 us -> none
    reshape x2 -> x0, local copies, waits for them, and re-layouts: 2.85 us -> none  [the longest x1 1.44 us: body(): pre_gain.reshape(16, TOK)]
    pallas_call x0 -> x1, Pallas kernels: none -> 2.32 us  [body(): pl.pallas_call(hand_out, out_shape=tuple(shapes), in_specs=[vmem] * len(O...]
where the time goes in v2:
time: 158 us; the launch traced here: 157 us
  Pallas kernels  156 us (99%)
    pallas_call x1, Pallas kernels, body(): pl.pallas_call(step_body, out_shape=(tile, tile, jax.ShapeDtypeStruct((8,...  154 us

profile of v2, /device:TPU:0, one launch (start us, length us, event | category | flops | bytes accessed | tf_op | source)
XLA Modules:
  0.0 157.1 jit_solution(6292699135653964549)
XLA Ops:
  0.6 154.1 %shard_map.216 = (bf16[288,288]{1,0:T(8,128)(2,1)}, bf16[288,288]{1,0:T(8,128)(2,1)}, f32[8,128]{1,0:T(8,128)}, bf16[288,288]{1,0:T(8,128)(2,1)}, f32[576,128]{1...) custom-call(s32[3]{0:T(128)} %refs_0_.1, s32[24]{0:T(128)} %refs_1_.1, bf16[288,288]{1,0:T(8,128)(2,1)} %refs_2_.1, ...), custom_call_target="tpu_custom_call" | custom-call | tf_op jit(solution)/shard_map/pallas_call | solution.py:968
  154.8 2.3 %shard_map.217 = (bf16[288,288]{1,0:T(8,128)(2,1)}, bf16[288,288]{1,0:T(8,128)(2,1)}, f32[1,1]{1,0:T(1,128)}, bf16[288,288]{1,0:T(8,128)(2,1)}, f32[576,128]{1,0...) custom-call(bf16[288,288]{1,0:T(8,128)(2,1)} %get-tuple-element.21.refs_0_, bf16[288,288]{1,0:T(8,128)(2,1)} %get-tuple-element.22.refs_1_, ...), custom_call_target="tpu_custom_call" | custom-call | tf_op jit(solution)/shard_map/pallas_call | solution.py:1006

commit v3 on v2

--- a/solution.py
+++ b/solution.py
@@ -7,8 +7,8 @@
 from jax.sharding import Mesh
 from jax.sharding import PartitionSpec as P
 
-DP = ("dp_0", "dp_1")
-TENSOR = ("tensor_0", "tensor_1")
+Y, CORE, X, Z = "dp_0", "dp_1", "tensor_0", "tensor_1"
+DP, TENSOR = (Y, CORE), (X, Z)
 MESH = pl.DeviceIdType.MESH
 
 WIDTH = 4608
@@ -60,7 +60,7 @@
         self.rows = rows
         self.sizes, self.starts = chunks_of(rows)
         self.send, self.recv = send, recv
-        self.at = (lax.axis_index("tensor_0"), lax.axis_index("tensor_1"))
+        self.at = (lax.axis_index(X), lax.axis_index(Z))
 
     def place(self, k, first, second):
         primary, way = RINGS[k]
@@ -74,32 +74,40 @@
         axis = 1 - primary if secondary else primary
         return {TENSOR[axis]: back(self.at[axis], 1 if behind else -1, way)}
 
-    def remote(self, source, target, k, number, device):
+    def remote(self, source, target, number, device):
         return pltpu.make_async_remote_copy(
             src_ref=source,
             dst_ref=target,
-            send_sem=self.send.at[k, number],
-            recv_sem=self.recv.at[k, number],
+            send_sem=self.send.at[0],
+            recv_sem=self.recv.at[number],
             device_id=device,
             device_id_type=MESH,
         )
 
+    def arrived(self, number):
+        whole = self.memory.at[pl.ds(0, self.rows), :]
+        self.remote(whole, whole, number, self.next_on(0, False)).wait_recv()
+
+    def drain(self):
+        whole = self.memory.at[pl.ds(0, 15 * self.rows), :]
+        self.remote(whole, whole, 0, self.next_on(0, False)).wait_send()
+
 
 class Gather(Ring):
     def __init__(self, buffer, rows, send, recv):
         super().__init__(rows, send, recv)
-        self.buffer = buffer
+        self.memory = buffer
 
     def piece(self, k, j, s):
-        return self.buffer.at[pl.ds(self.place(k, j, s), self.sizes[k]), :]
+        return self.memory.at[pl.ds(self.place(k, j, s), self.sizes[k]), :]
 
     def first(self, k, number):
         piece = self.piece(k, 1 if number == 1 else 0, 0)
-        return self.remote(piece, piece, k, number, self.next_on(k, False, number == 2))
+        return self.remote(piece, piece, number, self.next_on(k, False, number == 2))
 
     def second(self, k, j, s):
         piece = self.piece(k, j, s)
-        return self.remote(piece, piece, k, 3 + 3 * j + s, self.next_on(k, True))
+        return self.remote(piece, piece, 3 + 3 * j + s, self.next_on(k, True))
 
     def begin(self):
         for k in range(4):
@@ -109,19 +117,16 @@
             self.second(k, 0, 0).start()
 
     def await_first(self, number):
-        j = number + 1
+        self.arrived(number)
         for k in range(4):
-            piece = self.piece(k, j, 0)
-            self.remote(piece, piece, k, number, self.next_on(k, False)).wait_recv()
             if number == 0:
                 self.first(k, 1).start()
-            self.second(k, j, 0).start()
+            self.second(k, number + 1, 0).start()
 
     def await_second(self, j, s):
-        for k in range(4):
-            piece = self.piece(k, j, s + 1)
-            self.remote(piece, piece, k, 3 + 3 * j + s, self.next_on(k, True)).wait_recv()
-            if s < 2:
+        self.arrived(3 + 3 * j + s)
+        if s < 2:
+            for k in range(4):
                 self.second(k, j, s + 1).start()
 
     def steps(self):
@@ -137,19 +142,11 @@
             self.await_second(j, s)
             yield
 
-    def drain(self):
-        for k in range(4):
-            for number in range(3):
-                self.first(k, number).wait_send()
-            for j in range(4):
-                for s in range(3):
-                    self.second(k, j, s).wait_send()
-
 
 class Scatter(Ring):
     def __init__(self, partial, landing, rows, send, recv):
         super().__init__(rows, send, recv)
-        self.partial, self.landing = partial, landing
+        self.partial, self.landing, self.memory = partial, landing, landing
 
     def piece(self, k, first, second):
         return self.partial.at[pl.ds(self.place(k, first, second), self.sizes[k]), :]
@@ -159,26 +156,28 @@
 
     def outer(self, k, j, s):
         number = 3 * j + s
-        return self.remote(self.piece(k, ORDER[j], s + 1), self.slot(k, number), k, number, self.next_on(k, True))
+        return self.remote(self.piece(k, ORDER[j], s + 1), self.slot(k, number), number, self.next_on(k, True))
 
     def inner(self, k, number):
         piece = self.piece(k, (2, 3, 1)[number - 12], 0)
-        return self.remote(piece, self.slot(k, number), k, number, self.next_on(k, False, number == 14))
+        return self.remote(piece, self.slot(k, number), number, self.next_on(k, False, number == 14))
 
     def add(self, k, number, first, second):
         piece, slot = self.piece(k, first, second), self.slot(k, number)
         piece[...] = (piece[...].astype(F32) + slot[...].astype(F32)).astype(BF16)
 
-    def begin(self):
-        for j in range(4):
+    def begin(self, parts=range(4)):
+        for j in parts:
             for k in range(4):
                 self.outer(k, j, 0).start()
 
     def steps(self, result):
         for s in range(3):
             for j in range(4):
+                self.arrived(3 * j + s)
+                if s == 2 and j == 2:
+                    self.arrived(12)
                 for k in range(4):
-                    self.outer(k, j, s).wait_recv()
                     self.add(k, 3 * j + s, ORDER[j], s + 2)
                     if s < 2:
                         self.outer(k, j, s + 1).start()
@@ -187,32 +186,24 @@
                     elif j == 1:
                         self.inner(k, 14).start()
                     elif j == 2:
-                        self.inner(k, 12).wait_recv()
                         self.add(k, 12, 3, 0)
                         self.inner(k, 13).start()
                 yield
+        self.arrived(14)
+        self.arrived(13)
         for k in range(4):
             own = self.piece(k, 0, 0)[...].astype(F32)
             for number in (14, 13):
-                self.inner(k, number).wait_recv()
                 own = own + self.slot(k, number)[...].astype(F32)
             result[pl.ds(self.starts[k], self.sizes[k]), :] = own
         yield
-
-    def drain(self):
-        for k in range(4):
-            for j in range(4):
-                for s in range(3):
-                    self.outer(k, j, s).wait_send()
-            for number in range(12, 15):
-                self.inner(k, number).wait_send()
 
 
 class Weights:
     def __init__(self, w_in, w_back, y_send, y_recv, d_send, d_recv):
         self.w_in, self.w_back = w_in, w_back
         self.sems = (y_send, y_recv, d_send, d_recv)
-        self.y, self.core = lax.axis_index("dp_0"), lax.axis_index("dp_1")
+        self.y, self.core = lax.axis_index(Y), lax.axis_index(CORE)
 
     def block(self, hops, half, part, core):
         way = 1 - 2 * half
@@ -224,89 +215,74 @@
         ref = self.w_in if part == 2 else self.w_back
         return ref.at[pl.ds(aligned(MAIN + 32 * tile, 32), 32), :]
 
-    def round(self, s, half, part, arriving=False):
-        ref = self.block(s + 1 if arriving else s, half, part, self.core)
+    def round(self, s, half, part):
+        ref = self.block(s, half, part, self.core)
+        return self.copy(ref, 0, part, 5 * s + part, {Y: back(self.y, -1, 1 - 2 * half)})
+
+    def across(self, i, half, part):
+        return self.copy(self.block(i, half, part, self.core), 2, part, part // 3, {CORE: 1 - self.core})
+
+    def copy(self, ref, way, part, number, device):
         return pltpu.make_async_remote_copy(
             src_ref=ref,
             dst_ref=ref,
-            send_sem=self.sems[0].at[half, s, part],
-            recv_sem=self.sems[1].at[half, s, part],
-            device_id={"dp_0": back(self.y, -1, 1 - 2 * half)},
+            send_sem=self.sems[way].at[part // 3],
+            recv_sem=self.sems[way + 1].at[number],
+            device_id=device,
             device_id_type=MESH,
         )
 
-    def across(self, i, half, part, arriving=False):
-        ref = self.block(i, half, part, 1 - self.core if arriving else self.core)
-        return pltpu.make_async_remote_copy(
-            src_ref=ref,
-            dst_ref=ref,
-            send_sem=self.sems[2].at[half, i, part],
-            recv_sem=self.sems[3].at[half, i, part],
-            device_id={"dp_1": 1 - self.core},
-            device_id_type=MESH,
-        )
+    def rows(self, part, count):
+        return (self.w_in if part < 3 else self.w_back).at[pl.ds(0, count), :]
 
     def step(self, s, parts):
         for part in parts:
+            if s > 0:
+                both = self.rows(part, 2 * (128, 128, 32, 256, 32)[part])
+                self.copy(both, 0, part, 5 * (s - 1) + part, {CORE: 1 - self.core}).wait_recv()
             for half in range(2):
-                if s > 0:
-                    self.round(s - 1, half, part, True).wait_recv()
                 if s < 3:
                     self.round(s, half, part).start()
                 self.across(s, half, part).start()
 
-    def arrive(self, parts):
-        for half in range(2):
-            for part in parts:
-                for i in range(4):
-                    self.across(i, half, part, True).wait_recv()
+    def arrive(self, part):
+        self.copy(self.rows(part, 8 * TOK), 2, part, part // 3, {CORE: 1 - self.core}).wait_recv()
 
     def drain(self):
-        for half in range(2):
-            for part in range(5):
-                for s in range(3):
-                    self.round(s, half, part).wait_send()
-                for i in range(4):
-                    self.across(i, half, part).wait_send()
+        for part in (0, 3):
+            self.copy(self.rows(part, 6 * TOK), 0, part, 0, {CORE: 1 - self.core}).wait_send()
+            self.copy(self.rows(part, 8 * TOK), 2, part, 0, {CORE: 1 - self.core}).wait_send()
 
 
 class Exchange:
-    def __init__(self, buffer, rows, count, me, device_of, send, recv, source=None, spread=False):
+    def __init__(self, buffer, rows, count, me, device_of, send, recv):
         self.buffer, self.rows, self.count, self.me = buffer, rows, count, me
         self.device_of, self.send, self.recv = device_of, send, recv
-        self.source = buffer if source is None else source
-        self.spread = spread
-
-    def slot(self, i):
-        return self.buffer.at[pl.ds(aligned(i * self.rows, 8), self.rows), :]
-
-    def copy(self, delta):
-        peer = lax.rem(self.me + delta, self.count)
-        origin = peer if self.spread else self.me
+
+    def part(self, buffer, i):
+        return buffer.at[pl.ds(aligned(i * self.rows, self.rows), self.rows), :]
+
+    def copy(self, source, target, peer):
         return pltpu.make_async_remote_copy(
-            src_ref=self.source.at[pl.ds(aligned(origin * self.rows, 8), self.rows), :],
-            dst_ref=self.slot(self.me),
-            send_sem=self.send.at[delta],
-            recv_sem=self.recv.at[delta],
+            src_ref=source,
+            dst_ref=target,
+            send_sem=self.send.at[0],
+            recv_sem=self.recv.at[0],
             device_id=self.device_of(peer),
             device_id_type=MESH,
         )
 
     def start(self):
+        own = self.part(self.buffer, self.me)
         for delta in range(1, self.count):
-            self.copy(delta).start()
+            self.copy(own, own, lax.rem(self.me + delta, self.count)).start()
+
+    def slots(self, count):
+        whole = self.buffer.at[pl.ds(0, count * self.rows), :]
+        return self.copy(whole, whole, lax.rem(self.me + 1, self.count))
 
     def wait(self):
-        for delta in range(1, self.count):
-            arrived = self.slot(lax.rem(self.me - delta + self.count, self.count))
-            pltpu.make_async_remote_copy(
-                src_ref=arrived,
-                dst_ref=arrived,
-                send_sem=self.send.at[delta],
-                recv_sem=self.recv.at[delta],
-                device_id=self.device_of(lax.rem(self.me + delta, self.count)),
-                device_id_type=MESH,
-            ).wait_recv()
+        self.slots(self.count - 1).wait_recv()
 
     def total(self):
         value = self.buffer[0 : self.rows, :].astype(F32)
@@ -315,16 +291,67 @@
         return value
 
     def drain(self):
-        for delta in range(1, self.count):
-            self.copy(delta).wait_send()
+        self.slots(self.count - 1).wait_send()
+
+
+OWNERS = 9
+
+
+class HookSum:
+    def __init__(self, terms, parts, sums, me, send_parts, recv_parts, send_sums, recv_sums):
+        self.terms, self.parts, self.sums, self.me = terms, parts, sums, me
+        self.there = Exchange(parts, 32, 16, me, in_tensor, send_parts, recv_parts)
+        self.home = Exchange(parts, 32, 16, me, in_tensor, send_sums, recv_sums)
+        self.owner = me < OWNERS
+
+    def start(self):
+        @pl.when(self.owner)
+        def _():
+            own = pl.ds(aligned(32 * self.me, 32), 32)
+            self.parts[own, :] = self.terms[own, :]
+
+        for delta in range(1, 16):
+            peer = lax.rem(self.me + delta, 16)
+
+            @pl.when(peer < OWNERS)
+            def _():
+                self.there.copy(self.there.part(self.terms, peer), self.there.part(self.parts, self.me), peer).start()
+
+    def reduce(self):
+        @pl.when(self.owner)
+        def _():
+            self.there.wait()
+            self.sums[pl.ds(aligned(32 * self.me, 32), 32), :] = self.there.total().astype(BF16)
+            own = self.home.part(self.sums, self.me)
+            for delta in range(1, 16):
+                self.home.copy(own, own, lax.rem(self.me + delta, 16)).start()
+
+    def wait(self):
+        @pl.when(self.owner)
+        def _():
+            self.home.slots(OWNERS - 1).wait_recv()
+
+        @pl.when(jnp.logical_not(self.owner))
+        def _():
+            self.home.slots(OWNERS).wait_recv()
+
+    def drain(self):
+        @pl.when(self.owner)
+        def _():
+            self.there.slots(OWNERS - 1).wait_send()
+            self.home.slots(15).wait_send()
+
+        @pl.when(jnp.logical_not(self.owner))
+        def _():
+            self.there.slots(OWNERS).wait_send()
 
 
 def in_tensor(i):
-    return {"tensor_0": lax.div(i, 4), "tensor_1": lax.rem(i, 4)}
+    return {X: lax.div(i, 4), Z: lax.rem(i, 4)}
 
 
 def in_data(i):
-    return {"dp_0": lax.div(i, 2), "dp_1": lax.rem(i, 2)}
+    return {Y: lax.div(i, 2), CORE: lax.rem(i, 2)}
 
 
 def together(main, filler, ratio):
@@ -335,11 +362,10 @@
         pass
 
 
-def greet(peers):
+def signal(peers):
     barrier = pltpu.get_barrier_semaphore()
     for peer in peers:
         pl.semaphore_signal(barrier, inc=1, device_id=peer, device_id_type=MESH)
-    pl.semaphore_wait(barrier, len(peers))
 
 
 def pack_tail(tail):
@@ -458,65 +484,65 @@
     scratch[...] = jnp.transpose(filled)
 
 
-SCRATCH = {
-    "hidden_buf": ((32 * SHARD, 128), BF16),
-    "w_in": ((WIDTH, 640), BF16),
-    "w_back": ((WIDTH, 256), BF16),
-    "normed": ((2 * TOK, WIDTH), BF16),
-    "scale": ((2 * TOK, 128), F32),
-    "acc": ((2 * TOK, 640), F32),
-    "linear": ((TOK, 640), F32),
-    "low": ((TOK, 128), BF16),
-    "heads": ((2 * TOK, 512), BF16),
-    "mixed": ((2 * TOK, 256), BF16),
-    "probs": ((2 * TOK, 256), F32),
-    "capped": ((2 * TOK, 256), F32),
-    "partial": ((16 * SHARD, 128), BF16),
-    "partial_pol": ((16 * SHARD, 128), BF16),
-    "landing": ((15 * SHARD, 128), BF16),
-    "landing_pol": ((15 * SHARD, 128), BF16),
-    "result": ((2, SHARD, 128), F32),
-    "summed": ((2, TOK, TOK), F32),
-    "table": ((384, 128), F32),
-    "coefficient": ((384, 128), F32),
-    "ref_stats": ((16 * 8, 384), F32),
-    "pol_stats": ((16 * 16, 128), F32),
-    "pre_ordered": ((40, 128), F32),
-    "post_ordered": ((40, 128), F32),
-    "scores": ((8 * 8, 128), F32),
-    "grad_buf": ((16 * SHARD, 128), BF16),
-    "grad_mixed": ((TOK, 256), F32),
-    "grads": ((TOK, 640), BF16),
-    "partial_back": ((16 * SHARD, 128), BF16),
-    "landing_back": ((15 * SHARD, 128), BF16),
-    "hooks": ((384, 128), F32),
-    "hook_parts": ((384, 128), F32),
-    "hook_whole": ((384, 128), F32),
-    "stats_back": ((16 * 8, 384), F32),
-    "factors": ((8 * 64, 384), BF16),
-    "a_terms": ((WIDTH, 128), BF16),
-    "a_across": ((4 * 576, 128), BF16),
-    "a_pairs": ((4 * 576, 128), BF16),
-    "a_round": ((4 * 576, 128), BF16),
-}
-SEMAPHORES = {
-    "gather": (4, 15),
-    "scatter_ref": (4, 15),
-    "scatter_pol": (4, 15),
-    "gather_back": (4, 15),
-    "scatter_back": (4, 15),
-    "y": (2, 3, 5),
-    "d": (2, 4, 5),
-    "ref_stats": (16,),
-    "pol_stats": (16,),
-    "scores": (8,),
-    "hooks": (16,),
-    "hook_whole": (16,),
-    "stats_back": (16,),
-    "factors": (8,),
-    "across": (4,),
-    "round": (4,),
-}
+SCRATCH = dict(
+    hidden_buf=((32 * SHARD, 128), BF16),
+    w_in=((WIDTH, 640), BF16),
+    w_back=((WIDTH, 256), BF16),
+    normed=((2 * TOK, WIDTH), BF16),
+    scale=((2 * TOK, 128), F32),
+    acc=((2 * TOK, 640), F32),
+    linear=((TOK, 640), F32),
+    low=((TOK, 128), BF16),
+    heads=((2 * TOK, 512), BF16),
+    mixed=((2 * TOK, 256), BF16),
+    probs=((2 * TOK, 256), F32),
+    capped=((2 * TOK, 256), F32),
+    partial=((16 * SHARD, 128), BF16),
+    partial_pol=((16 * SHARD, 128), BF16),
+    landing=((15 * SHARD, 128), BF16),
+    landing_pol=((15 * SHARD, 128), BF16),
+    result=((2, SHARD, 128), F32),
+    summed=((2, TOK, TOK), F32),
+    table=((384, 128), F32),
+    coefficient=((384, 128), F32),
+    ref_stats=((16 * 8, 384), F32),
+    pol_stats=((16 * 16, 128), F32),
+    pre_ordered=((40, 128), F32),
+    post_ordered=((40, 128), F32),
+    scores=((8 * 8, 128), F32),
+    grad_buf=((16 * SHARD, 128), BF16),
+    grad_mixed=((TOK, 256), F32),
+    grads=((TOK, 640), BF16),
+    partial_back=((16 * SHARD, 128), BF16),
+    landing_back=((15 * SHARD, 128), BF16),
+    hooks=((TOK, 128), BF16),
+    hook_parts=((16 * 32, 128), BF16),
+    hook_sums=((TOK, 128), BF16),
+    stats_back=((16 * 8, 128), F32),
+    factors=((8 * 64, 384), BF16),
+    a_terms=((WIDTH, 128), BF16),
+    a_across=((4 * 576, 128), BF16),
+    a_pairs=((4 * 576, 128), BF16),
+    a_round=((4 * 576, 128), BF16),
+)
+SEMAPHORES = dict(
+    gather=(1, 15),
+    scatter_ref=(1, 15),
+    scatter_pol=(1, 15),
+    gather_back=(1, 15),
+    scatter_back=(1, 15),
+    y=(2, 15),
+    d=(2, 2),
+    ref_stats=(1, 1),
+    pol_stats=(1, 1),
+    scores=(1, 1),
+    hooks=(1, 1),
+    hook_sums=(1, 1),
+    stats_back=(1, 1),
+    factors=(1, 1),
+    across=(1, 1),
+    round=(1, 1),
+)
 
 
 class Refs:
@@ -524,17 +550,35 @@
 
 
 def step_body(*refs):
-    names = INPUTS + OUTPUTS + list(SCRATCH)
-    r = Refs()
+    inputs, outputs = list(INPUTS), list(OUTPUTS)
+    outside, refs = refs[: len(inputs + outputs)], refs[len(inputs + outputs) :]
+    names = inputs + outputs + list(SCRATCH)
+    r, send, recv = Refs(), Refs(), Refs()
     for name, ref in zip(names, refs):
         setattr(r, name, ref)
-    sems = refs[len(names) :]
-    send = dict(zip(SEMAPHORES, sems[0::2]))
-    recv = dict(zip(SEMAPHORES, sems[1::2]))
-
-    x, z = lax.axis_index("tensor_0"), lax.axis_index("tensor_1")
-    y, core = lax.axis_index("dp_0"), lax.axis_index("dp_1")
+    load_sems, store_sems, *sems = refs[len(names) :]
+    for number, name in enumerate(SEMAPHORES):
+        setattr(send, name, sems[2 * number])
+        setattr(recv, name, sems[2 * number + 1])
+
+    x, z = lax.axis_index(X), lax.axis_index(Z)
+    y, core = lax.axis_index(Y), lax.axis_index(CORE)
     mine, rank = 4 * x + z, 2 * y + core
+    def load(number):
+        return pltpu.make_async_copy(outside[number], refs[number], load_sems.at[number])
+
+    def store(number):
+        at = len(inputs) + number
+        return pltpu.make_async_copy(refs[at], outside[at], store_sems.at[number])
+
+    signal(
+        [in_tensor(lax.rem(mine + i, 16)) for i in range(1, 16)]
+        + [in_data(lax.rem(rank + i, 8)) for i in range(1, 8)]
+    )
+    for number in range(len(inputs)):
+        load(number).start()
+    for number in range(10):
+        load(number).wait()
     pack_hidden(r.ref_hidden[...], r.hidden_buf, mine * 2 * SHARD)
     pack_hidden(r.pol_hidden[...], r.hidden_buf, mine * 2 * SHARD + SHARD)
     a_both = jnp.concatenate([r.a_query[...].astype(F32), r.a_value[...].astype(F32)], axis=0)
@@ -548,13 +592,10 @@
             r.w_in[there, 384:512] = r.w_value[here, :]
             r.w_in[there, 512:640] = a_both[288 * half + start : 288 * half + start + size, :].astype(BF16)
             r.w_back[there, :] = r.w_out[here, :]
-    greet(
-        [in_tensor(lax.rem(mine + i, 16)) for i in range(1, 16)]
-        + [in_data(lax.rem(rank + i, 8)) for i in range(1, 8)]
-    )
-
-    gather = Gather(r.hidden_buf, 2 * SHARD, send["gather"], recv["gather"])
-    weights = Weights(r.w_in, r.w_back, send["y"], recv["y"], send["d"], recv["d"])
+    pl.semaphore_wait(pltpu.get_barrier_semaphore(), 22)
+
+    gather = Gather(r.hidden_buf, 2 * SHARD, send.gather, recv.gather)
+    weights = Weights(r.w_in, r.w_back, send.y, recv.y, send.d, recv.d)
 
     def weight_steps():
         for s in range(1, 3):
@@ -575,6 +616,8 @@
 
     gather.begin()
     weights.step(0, (0, 1, 2))
+    for number in range(10, len(inputs)):
+        load(number).wait()
     gain = r.pre_ordered
     order_gain(r.pre_gain, gain)
     order_gain(r.post_gain, r.post_ordered)
@@ -614,19 +657,19 @@
 
     unpack_features(r.hidden_buf, 2 * SHARD, 0, r.normed, 0)
     normalize(r.normed, r.scale, gain, 0)
-    weights.arrive((0, 1, 2))
+    weights.arrive(0)
     weights.step(2, (3, 4))
     for _ in project(0):
         pass
     for _ in attend(0):
         pass
     weights.step(3, (3, 4))
-    weights.arrive((3, 4))
+    weights.arrive(3)
     for _ in partial_products(r.mixed.at[0:TOK], r.w_back, r.partial):
         pass
-    ref_scatter = Scatter(r.partial, r.landing, SHARD, send["scatter_ref"], recv["scatter_ref"])
+    ref_scatter = Scatter(r.partial, r.landing, SHARD, send.scatter_ref, recv.scatter_ref)
     ref_scatter.begin()
-    pol_scatter = Scatter(r.partial_pol, r.landing_pol, SHARD, send["scatter_pol"], recv["scatter_pol"])
+    pol_scatter = Scatter(r.partial_pol, r.landing_pol, SHARD, send.scatter_pol, recv.scatter_pol)
 
     def policy():
         unpack_features(r.hidden_buf, 2 * SHARD, SHARD, r.normed, TOK)
@@ -643,8 +686,6 @@
         yield
         yield from attend(1)
         yield from partial_products(r.mixed.at[TOK : 2 * TOK], r.w_back, r.partial_pol)
-        pol_scatter.begin()
-        yield
 
     def token_sums(m, hidden):
         unpack_result(r.result.at[m], 0, r.summed.at[m])
@@ -655,8 +696,8 @@
             jnp.sum(hidden[...].astype(F32) * readout, axis=1, keepdims=True),
         ]
 
-    ref_stats = Exchange(r.ref_stats, 8, 16, mine, in_tensor, send["ref_stats"], recv["ref_stats"])
-    pol_stats = Exchange(r.pol_stats, 16, 16, mine, in_tensor, send["pol_stats"], recv["pol_stats"])
+    ref_stats = Exchange(r.ref_stats, 8, 16, mine, in_tensor, send.ref_stats, recv.ref_stats)
+    pol_stats = Exchange(r.pol_stats, 16, 16, mine, in_tensor, send.pol_stats, recv.pol_stats)
 
     def policy_ring():
         yield from pol_scatter.steps(r.result.at[1])
@@ -673,15 +714,20 @@
 
     ref_ring, policy_work, policy_steps = ref_scatter.steps(r.result.at[0]), policy(), policy_ring()
     fill(policy_work, 3)
-    for count in (2, 2, 2, 2, 4):
+    for count in (2, 2, 2, 2, 2):
         fill(ref_ring, 1)
         fill(policy_work, count)
     for _ in policy_work:
         pass
     fill(ref_ring, 3)
-    for _ in range(5):
+    pol_scatter.begin((0,))
+    fill(ref_ring, 1)
+    pol_scatter.begin((1,))
+    fill(ref_ring, 1)
+    pol_scatter.begin((2, 3))
+    for count in (2, 2, 1):
         fill(ref_ring, 1)
-        fill(policy_steps, 1)
+        fill(policy_steps, count)
     together(policy_steps, after_ref(), (1,) + (0,) * 12)
     columns = columns_to_rows(r.table, token_sums(1, r.pol_hidden))
     packed = [columns[k : k + 1, 128 * c : 128 * c + 128] for k in range(3) for c in range(3)]
@@ -698,7 +744,7 @@
     readout = r.readout[...].astype(F32)
     bare = r.table[0:TOK, 0:1] * post_gain * readout - r.summed[1] * r.table[0:TOK, 1:2]
     pack_hidden(bare, r.grad_buf, mine * SHARD)
-    back_gather = Gather(r.grad_buf, SHARD, send["gather_back"], recv["gather_back"])
+    back_gather = Gather(r.grad_buf, SHARD, send.gather_back, recv.gather_back)
     back_gather.begin()
 
     lane = lax.broadcasted_iota(jnp.int32, (1, 384), 1)
@@ -721,16 +767,17 @@
             inside = (lane >= 96 * s) & (lane < 96 * s + 96)
             score = jnp.sum(jnp.where(inside, token_scores[m], 0.0), axis=1, keepdims=True)
             tile = jnp.where((row8 == m) & (lane8 == 3 * rank + s), score, tile)
-    scores = Exchange(r.scores, 8, 8, rank, in_data, send["scores"], recv["scores"])
+    scores = Exchange(r.scores, 8, 8, rank, in_data, send.scores, recv.scores)
     r.scores[pl.ds(aligned(8 * rank, 8), 8), :] = tile
     scores.start()
 
-    def outputs():
+    def layer_outputs():
         rows_to_columns(r.coefficient, [scale_ref, scale_pol])
         for m, (hidden, out) in enumerate(((r.ref_hidden, r.ref_out), (r.pol_hidden, r.pol_out))):
             scale = r.coefficient[0:TOK, m : m + 1]
             out[...] = (hidden[...].astype(F32) + r.summed[m] * scale * post_gain).astype(BF16)
             yield
+            store(1 - m).start()
 
     def preference():
         scores.wait()
@@ -751,6 +798,7 @@
         counted = even & (row32 < 24) & (lane32 == 0)
         total_loss = jnp.sum(jnp.where(counted, loss, 0.0), axis=(0, 1), keepdims=True)
         r.loss[...] = jnp.broadcast_to(total_loss, (8, 128))
+        store(2).start()
         pull = DPO_BETA * LOSS_SCALE / (1.0 + jnp.exp(margin))
         signed = jnp.where(even, -pull, pull)
         coefficients = jnp.sum(jnp.where(chosen, signed, 0.0), axis=0, keepdims=True)
@@ -763,7 +811,7 @@
         yield
 
     def meanwhile():
-        yield from outputs()
+        yield from layer_outputs()
         yield from preference()
 
     together(back_gather.steps(), meanwhile(), (1, 1, 0, 0, 0, 0, 0, 1, 0, 0, 0, 0, 0, 0, 0))
@@ -803,42 +851,36 @@
     value_factor = jnp.concatenate([jnp.zeros((RANK, 128), BF16), r.b_value[...]], axis=0)
     hook = dot(r.grads[:, 0:256], query_factor, NT) + dot(r.grads[:, 384:512], value_factor, NT)
     r.grads[:, 512:640] = (ADAPTER_SCALE * hook).astype(BF16)
-    r.hooks[0:TOK, :] = r.grads[:, 512:640].astype(F32)
-    r.hooks[TOK:384, :] = jnp.zeros((384 - TOK, 128), F32)
-    hooks = Exchange(r.hook_parts, 24, 16, mine, in_tensor, send["hooks"], recv["hooks"], r.hooks, True)
-    own_rows = pl.ds(aligned(24 * mine, 8), 24)
-    r.hook_parts[own_rows, :] = r.hooks[own_rows, :]
+    r.hooks[...] = r.grads[:, 512:640]
+    hooks = HookSum(
+        r.hooks,
+        r.hook_parts,
+        r.hook_sums,
+        mine,
+        send.hooks,
+        recv.hooks,
+        send.hook_sums,
+        recv.hook_sums,
+    )
     hooks.start()
-    pull_back = jnp.sum(r.grads[...].astype(F32) * r.linear[...], axis=1, keepdims=True)
-    stats_back = Exchange(r.stats_back, 8, 16, mine, in_tensor, send["stats_back"], recv["stats_back"])
-    r.stats_back[pl.ds(aligned(8 * mine, 8), 8), :] = columns_to_rows(r.table, [pull_back])
-    stats_back.start()
-    factor_terms = ADAPTER_SCALE * dot(r.low[...], r.grads[:, 0:512], TN)
-    own_factor = pl.ds(aligned(64 * rank, 64), 64)
-    r.factors[own_factor, 0:256] = factor_terms[0:64, 0:256].astype(BF16)
-    r.factors[own_factor, 256:384] = factor_terms[64:128, 384:512].astype(BF16)
-    factors = Exchange(r.factors, 64, 8, rank, in_data, send["factors"], recv["factors"])
-    factors.start()
+    stats_back = Exchange(r.stats_back, 8, 16, mine, in_tensor, send.stats_back, recv.stats_back)
+    factors = Exchange(r.factors, 64, 8, rank, in_data, send.factors, recv.factors)
     for _ in partial_products(r.grads, r.w_in, r.partial_back):
         pass
     back_scatter = Scatter(
-        r.partial_back, r.landing_back, SHARD, send["scatter_back"], recv["scatter_back"]
+        r.partial_back, r.landing_back, SHARD, send.scatter_back, recv.scatter_back
     )
-    hook_whole = Exchange(
-        r.hook_whole, 24, 16, mine, in_tensor, send["hook_whole"], recv["hook_whole"]
-    )
-    hooks.wait()
-    r.hook_whole[own_rows, :] = hooks.total()
-    hook_whole.start()
-    back_scatter.begin()
+    back_scatter.begin((0,))
+    hooks.reduce()
+    back_scatter.begin((1, 2, 3))
 
     def across(i):
         return pltpu.make_async_remote_copy(
             src_ref=r.a_terms.at[pl.ds(aligned(576 * (2 * i + 1 - core), 64), 576), :],
             dst_ref=r.a_across.at[pl.ds(576 * i, 576), :],
-            send_sem=send["across"].at[i],
-            recv_sem=recv["across"].at[i],
-            device_id={"dp_1": 1 - core},
+            send_sem=send.across.at[0],
+            recv_sem=recv.across.at[0],
+            device_id={CORE: 1 - core},
             device_id_type=MESH,
         )
 
@@ -847,15 +889,37 @@
         return pltpu.make_async_remote_copy(
             src_ref=r.a_pairs.at[pl.ds(aligned(576 * to, 64), 576), :],
             dst_ref=r.a_round.at[pl.ds(576 * i, 576), :],
-            send_sem=send["round"].at[i],
-            recv_sem=recv["round"].at[i],
-            device_id={"dp_0": to},
+            send_sem=send.round.at[0],
+            recv_sem=recv.round.at[0],
+            device_id={Y: to},
             device_id_type=MESH,
         )
 
+    def all_bytes(sent, arrived, buffer, count):
+        whole = buffer.at[pl.ds(0, 576 * count), :]
+        return pltpu.make_async_remote_copy(
+            src_ref=whole,
+            dst_ref=whole,
+            send_sem=sent.at[0],
+            recv_sem=arrived.at[0],
+            device_id={CORE: 1 - core},
+            device_id_type=MESH,
+        )
+
     def adapters_back():
-        hook_whole.wait()
-        hook_low = r.hook_whole[0:TOK, :].astype(BF16)
+        pull_back = jnp.sum(r.grads[...].astype(F32) * r.linear[...], axis=1, keepdims=True)
+        row = columns_to_rows(r.table, [pull_back])[0:1]
+        row = [row[:, 128 * c : 128 * c + 128] for c in range(3)] + [jnp.zeros((5, 128), F32)]
+        r.stats_back[pl.ds(aligned(8 * mine, 8), 8), :] = jnp.concatenate(row, axis=0)
+        stats_back.start()
+        factor_terms = ADAPTER_SCALE * dot(r.low[...], r.grads[:, 0:512], TN)
+        own_factor = pl.ds(aligned(64 * rank, 64), 64)
+        r.factors[own_factor, 0:256] = factor_terms[0:64, 0:256].astype(BF16)
+        r.factors[own_factor, 256:384] = factor_terms[64:128, 384:512].astype(BF16)
+        factors.start()
+        yield
+        hooks.wait()
+        hook_low = r.hook_sums[...]
         for q in range(4):
             at = MAIN + 128 * q
             tail = dot(r.normed[TOK : 2 * TOK, at : at + 128], hook_low, TN).astype(BF16)
@@ -866,8 +930,8 @@
                 r.a_terms[288 * t + 256 : 288 * t + 288, :] = tail[32 * j : 32 * j + 32, :]
             across(q).start()
             yield
+        all_bytes(send.across, recv.across, r.a_across, 4).wait_recv()
         for i in range(4):
-            across(i).wait_recv()
             own = r.a_terms[pl.ds(aligned(576 * (2 * i + core), 64), 576), :].astype(F32)
             pair = own + r.a_across[576 * i : 576 * i + 576, :].astype(F32)
             r.a_pairs[576 * i : 576 * i + 576, :] = pair.astype(BF16)
@@ -875,10 +939,13 @@
             round_y(i).start()
         yield
 
-    together(back_scatter.steps(r.result.at[0]), adapters_back(), (0, 0, 1, 1, 1, 1, 0, 1, 0, 0, 0, 0, 0))
+    adapters = adapters_back()
+    fill(adapters, 1)
+    together(back_scatter.steps(r.result.at[0]), adapters, (0, 0, 1, 1, 1, 1, 0, 1, 0, 0, 0, 0, 0))
 
     stats_back.wait()
-    rows_to_columns(r.table, [stats_back.total()])
+    row = stats_back.total()
+    rows_to_columns(r.table, [jnp.concatenate([row[c : c + 1] for c in range(3)], axis=1)])
     unpack_result(r.result.at[0], 0, r.summed.at[1])
     pre_scale = r.scale[TOK : 2 * TOK, 0:1]
     shrink_back = pre_scale * pre_scale * r.table[0:TOK, 0:1] / WIDTH
@@ -887,23 +954,27 @@
     r.grad_hidden[...] = (
         grad_result + pre_scale * pre_gain * r.summed[1] - hidden * shrink_back
     ).astype(BF16)
+    store(3).start()
     factors.wait()
     factor_total = factors.total()
     r.query_grad[...] = factor_total[:, 0:256]
     r.value_grad[...] = factor_total[:, 256:384]
+    store(5).start()
+    store(6).start()
     whole = r.a_pairs[pl.ds(aligned(576 * y, 64), 576), :].astype(F32)
+    all_bytes(send.round, recv.round, r.a_round, 3).wait_recv()
     for i in range(1, 4):
-        round_y(i).wait_recv()
         whole = whole + r.a_round[576 * i : 576 * i + 576, :].astype(F32)
     r.grad_a[...] = whole
+    store(4).start()
     for ring in (gather, weights, ref_scatter, pol_scatter, back_gather, back_scatter):
         ring.drain()
-    for exchange in (ref_stats, pol_stats, scores, hooks, hook_whole, stats_back, factors):
+    for exchange in (ref_stats, pol_stats, scores, hooks, stats_back, factors):
         exchange.drain()
-    for i in range(4):
-        across(i).wait_send()
-    for i in range(1, 4):
-        round_y(i).wait_send()
+    all_bytes(send.across, recv.across, r.a_across, 4).wait_send()
+    all_bytes(send.round, recv.round, r.a_round, 3).wait_send()
+    for number in range(len(outputs)):
+        store(number).wait()
 
 
 def partial_products(rows, matrix, partial):
@@ -932,11 +1003,34 @@
     )
 
 
-INPUTS = [
-    "lengths", "pairing", "ref_hidden", "pol_hidden", "readout", "w_query", "w_key", "w_value", "w_out", "a_query",
-    "a_value", "b_query", "b_value", "pre_gain", "post_gain", "cosine", "sine",
-]
-OUTPUTS = ["pol_out", "ref_out", "loss", "grad_hidden", "grad_a", "query_grad", "value_grad"]
+INPUTS = dict(
+    lengths=None,
+    pairing=None,
+    ref_hidden=((TOK, TOK), BF16),
+    pol_hidden=((TOK, TOK), BF16),
+    w_query=((576, 256), BF16),
+    w_key=((576, 128), BF16),
+    w_value=((576, 128), BF16),
+    w_out=((576, 256), BF16),
+    a_query=((RANK, 576), BF16),
+    a_value=((RANK, 576), BF16),
+    readout=((TOK, TOK), BF16),
+    b_query=((RANK, 256), BF16),
+    b_value=((RANK, 128), BF16),
+    pre_gain=((36, 128), F32),
+    post_gain=((36, 128), F32),
+    cosine=((LENGTH, HEAD), F32),
+    sine=((LENGTH, HEAD), F32),
+)
+OUTPUTS = dict(
+    pol_out=((TOK, TOK), BF16),
+    ref_out=((TOK, TOK), BF16),
+    loss=((8, 128), F32),
+    grad_hidden=((TOK, TOK), BF16),
+    grad_a=((576, 128), F32),
+    query_grad=((RANK, 256), F32),
+    value_grad=((RANK, 128), F32),
+)
 
 
 def hand_out(*refs):
@@ -961,24 +1055,20 @@
     query_second_factor,
     value_second_factor,
 ):
-    vmem, smem = pl.BlockSpec(memory_space=pltpu.VMEM), pl.BlockSpec(memory_space=pltpu.SMEM)
+    vmem, whole = pl.BlockSpec(memory_space=pltpu.VMEM), pl.BlockSpec(memory_space=pl.ANY)
     cosine, sine = rotation_tables()
-    semaphores = [pltpu.SemaphoreType.DMA(shape) for shape in SEMAPHORES.values() for _ in range(2)]
-    tile = jax.ShapeDtypeStruct((TOK, TOK), BF16)
+    dma = pltpu.SemaphoreType.DMA
+    staged = [pltpu.VMEM(*kind) if kind else None for kind in list(INPUTS.values()) + list(OUTPUTS.values())]
+    staged[0:2] = [pltpu.SMEM((3,), jnp.int32), pltpu.SMEM((24,), jnp.int32)]
     results = pl.pallas_call(
         step_body,
-        out_shape=(
-            tile,
-            tile,
-            jax.ShapeDtypeStruct((8, 128), F32),
-            tile,
-            jax.ShapeDtypeStruct((576, 128), F32),
-            jax.ShapeDtypeStruct((RANK, 256), F32),
-            jax.ShapeDtypeStruct((RANK, 128), F32),
-        ),
-        in_specs=[smem, smem] + [vmem] * (len(INPUTS) - 2),
-        out_specs=(vmem,) * len(OUTPUTS),
-        scratch_shapes=[pltpu.VMEM(shape, kind) for shape, kind in SCRATCH.values()] + semaphores,
+        out_shape=tuple(jax.ShapeDtypeStruct(*kind) for kind in OUTPUTS.values()),
+        in_specs=[whole] * len(INPUTS),
+        out_specs=(whole,) * len(OUTPUTS),
+        scratch_shapes=staged
+        + [pltpu.VMEM(shape, kind) for shape, kind in SCRATCH.values()]
+        + [dma((len(INPUTS),)), dma((len(OUTPUTS),))]
+        + [dma((count,)) for pair in SEMAPHORES.values() for count in pair],
         compiler_params=pltpu.CompilerParams(
             collective_id=0, has_side_effects=True, vmem_limit_bytes=62 * 1024 * 1024
         ),
@@ -987,13 +1077,13 @@
         pairing,
         ref_hidden,
         pol_hidden,
-        readout,
         w_query,
         w_key,
         value_projection,
         w_out,
         a_query.T,
         a_value.T,
+        readout,
         query_second_factor,
         value_second_factor,
         pre_gain.reshape(36, 128),
@@ -1013,7 +1103,7 @@
 
 
 def solution(mesh):
-    torus = Mesh(mesh.devices.reshape(4, 2, 4, 4), ("dp_0", "dp_1", "tensor_0", "tensor_1"))
+    torus = Mesh(mesh.devices.reshape(4, 2, 4, 4), (Y, CORE, X, Z))
     split, rows, columns = P(DP, TENSOR), P(DP, None), P(None, TENSOR)
     return jax.shard_map(
         body,

time: 158 us -> 145 us (0.918)
  Pallas kernels: 156 us -> 144 us
    pallas_call x1, Pallas kernels: 154 us -> 141 us  [body(): pl.pallas_call(step_body, out_shape=tuple((jax.ShapeDtypeStruct(*kind) fo...]
where the time goes in v3:
time: 145 us; the launch traced here: 144 us
  Pallas kernels  144 us (99%)
    pallas_call x1, Pallas kernels, body(): pl.pallas_call(step_body, out_shape=tuple((jax.ShapeDtypeStruct(*kind) fo...  141 us

profile of v3, /device:TPU:0, one launch (start us, length us, event | category | flops | bytes accessed | tf_op | source)
XLA Modules:
  0.0 144.3 jit_solution(4383935555531099519)
XLA Ops:
  0.6 141.4 %shard_map.216 = (bf16[288,288]{1,0:T(8,128)(2,1)}, bf16[288,288]{1,0:T(8,128)(2,1)}, f32[8,128]{1,0:T(8,128)}, bf16[288,288]{1,0:T(8,128)(2,1)}, f32[576,128]{1...) custom-call(s32[3]{0:T(128)} %refs_0_.1, s32[24]{0:T(128)} %refs_1_.1, bf16[288,288]{1,0:T(8,128)(2,1)} %refs_2_.1, ...), custom_call_target="tpu_custom_call" | custom-call | tf_op jit(solution)/shard_map/pallas_call | solution.py:1063
  142.0 2.3 %shard_map.217 = (bf16[288,288]{1,0:T(8,128)(2,1)}, bf16[288,288]{1,0:T(8,128)(2,1)}, f32[1,1]{1,0:T(1,128)}, bf16[288,288]{1,0:T(8,128)(2,1)}, f32[576,128]{1,0...) custom-call(bf16[288,288]{1,0:T(8,128)(2,1)} %get-tuple-element.21.refs_0_, bf16[288,288]{1,0:T(8,128)(2,1)} %get-tuple-element.22.refs_1_, ...), custom_call_target="tpu_custom_call" | custom-call | tf_op jit(solution)/shard_map/pallas_call | solution.py:1096

commit v4 on v3

--- a/solution.py
+++ b/solution.py
@@ -478,6 +478,15 @@
     return jnp.transpose(scratch[...])[0:8, :]
 
 
+def as_tile(row):
+    pieces = [row[:, 128 * c : 128 * c + 128] for c in range(3)]
+    return jnp.concatenate(pieces + [jnp.zeros((5, 128), F32)], axis=0)
+
+
+def as_row(tile):
+    return jnp.concatenate([tile[c : c + 1] for c in range(3)], axis=1)
+
+
 def rows_to_columns(scratch, rows):
     missing = 128 - sum(row.shape[0] for row in rows)
     filled = jnp.concatenate(list(rows) + [jnp.zeros((missing, 384), F32)], axis=0)
@@ -485,13 +494,20 @@
 
 
 SCRATCH = dict(
-    hidden_buf=((32 * SHARD, 128), BF16),
-    w_in=((WIDTH, 640), BF16),
+    ref_gathered=((16 * SHARD, 128), BF16),
+    pol_gathered=((16 * SHARD, 128), BF16),
+    w_in=((WIDTH, 512), BF16),
+    a_all=((640, 128), BF16),
+    a_own=((TOK, 128), BF16),
     w_back=((WIDTH, 256), BF16),
     normed=((2 * TOK, WIDTH), BF16),
     scale=((2 * TOK, 128), F32),
-    acc=((2 * TOK, 640), F32),
-    linear=((TOK, 640), F32),
+    acc=((2 * TOK, 512), F32),
+    linear=((TOK, 512), F32),
+    pre_stats=((16 * 8, 128), F32),
+    own_normed=((TOK, TOK), BF16),
+    low_terms=((TOK, 128), BF16),
+    low_parts=((16 * 32, 128), BF16),
     low=((TOK, 128), BF16),
     heads=((2 * TOK, 512), BF16),
     mixed=((2 * TOK, 256), BF16),
@@ -512,7 +528,7 @@
     scores=((8 * 8, 128), F32),
     grad_buf=((16 * SHARD, 128), BF16),
     grad_mixed=((TOK, 256), F32),
-    grads=((TOK, 640), BF16),
+    grads=((TOK, 512), BF16),
     partial_back=((16 * SHARD, 128), BF16),
     landing_back=((15 * SHARD, 128), BF16),
     hooks=((TOK, 128), BF16),
@@ -526,7 +542,12 @@
     a_round=((4 * 576, 128), BF16),
 )
 SEMAPHORES = dict(
-    gather=(1, 15),
+    gather_ref=(1, 15),
+    gather_pol=(1, 15),
+    a=(1, 1),
+    pre_stats=(1, 1),
+    low_terms=(1, 1),
+    low=(1, 1),
     scatter_ref=(1, 15),
     scatter_pol=(1, 15),
     gather_back=(1, 15),
@@ -540,7 +561,7 @@
     hook_sums=(1, 1),
     stats_back=(1, 1),
     factors=(1, 1),
-    across=(1, 1),
+    across=(4, 4),
     round=(1, 1),
 )
 
@@ -579,10 +600,60 @@
         load(number).start()
     for number in range(10):
         load(number).wait()
-    pack_hidden(r.ref_hidden[...], r.hidden_buf, mine * 2 * SHARD)
-    pack_hidden(r.pol_hidden[...], r.hidden_buf, mine * 2 * SHARD + SHARD)
+    pack_hidden(r.ref_hidden[...], r.ref_gathered, mine * SHARD)
+    pack_hidden(r.pol_hidden[...], r.pol_gathered, mine * SHARD)
     a_both = jnp.concatenate([r.a_query[...].astype(F32), r.a_value[...].astype(F32)], axis=0)
-    a_both = jnp.transpose(jnp.concatenate([a_both, jnp.zeros((128, 64), F32)], axis=1))
+    r.a_all[...] = jnp.transpose(jnp.concatenate([a_both, jnp.zeros((128, 64), F32)], axis=1)).astype(BF16)
+    a_rank = lax.div(mine, 2)
+    a_here, a_core = rank == a_rank, core == lax.rem(a_rank, 2)
+    a_relay = a_core & (y != lax.div(a_rank, 2))
+    a_rows = pl.ds(aligned(TOK * lax.rem(mine, 2), 32), TOK)
+
+    @pl.when(a_here)
+    def _():
+        r.a_own[...] = r.a_all[a_rows, :]
+
+    def a_copy(source, target, device):
+        return pltpu.make_async_remote_copy(
+            src_ref=source,
+            dst_ref=target,
+            send_sem=send.a.at[0],
+            recv_sem=recv.a.at[0],
+            device_id=device,
+            device_id_type=MESH,
+        )
+
+    def send_a():
+        @pl.when(a_here)
+        def _():
+            for device in [{Y: lax.rem(y + i, 4)} for i in (1, 3, 2)] + [{CORE: 1 - core}]:
+                a_copy(r.a_all.at[a_rows, :], r.a_own, device).start()
+
+    def relay_a():
+        @pl.when(a_relay)
+        def _():
+            a_copy(r.a_own, r.a_own, {CORE: 1 - core}).wait_recv()
+            a_copy(r.a_own, r.a_own, {CORE: 1 - core}).start()
+
+    def await_a():
+        @pl.when(jnp.logical_not(a_core))
+        def _():
+            a_copy(r.a_own, r.a_own, {CORE: 1 - core}).wait_recv()
+
+    def drain_a():
+        @pl.when(a_here)
+        def _():
+            whole = r.ref_gathered.at[pl.ds(0, 4 * TOK), :]
+            a_copy(whole, whole, {CORE: 1 - core}).wait_send()
+
+        @pl.when(a_relay)
+        def _():
+            a_copy(r.a_own, r.a_own, {CORE: 1 - core}).wait_send()
+
+    pre_stats = Exchange(r.pre_stats, 8, 16, mine, in_tensor, send.pre_stats, recv.pre_stats)
+    own_hidden = r.pol_hidden[...].astype(F32)
+    row = columns_to_rows(r.table, [jnp.sum(own_hidden * own_hidden, axis=1, keepdims=True)])[0:1]
+    r.pre_stats[pl.ds(aligned(8 * mine, 8), 8), :] = as_tile(row)
     for half in range(2):
         tile = 2 * rank + half
         for start, size, to in ((0, 256, 256 * tile), (256, 32, MAIN + 32 * tile)):
@@ -590,11 +661,11 @@
             r.w_in[there, 0:256] = r.w_query[here, :]
             r.w_in[there, 256:384] = r.w_key[here, :]
             r.w_in[there, 384:512] = r.w_value[here, :]
-            r.w_in[there, 512:640] = a_both[288 * half + start : 288 * half + start + size, :].astype(BF16)
             r.w_back[there, :] = r.w_out[here, :]
     pl.semaphore_wait(pltpu.get_barrier_semaphore(), 22)
 
-    gather = Gather(r.hidden_buf, 2 * SHARD, send.gather, recv.gather)
+    ref_gather = Gather(r.ref_gathered, SHARD, send.gather_ref, recv.gather_ref)
+    pol_gather = Gather(r.pol_gathered, SHARD, send.gather_pol, recv.gather_pol)
     weights = Weights(r.w_in, r.w_back, send.y, recv.y, send.d, recv.d)
 
     def weight_steps():
@@ -611,10 +682,12 @@
         for part in range(3):
             weights.step(3, (part,))
             yield
-        weights.step(1, (3, 4))
-        yield
-
-    gather.begin()
+        for s in range(1, 4):
+            weights.step(s, (3, 4))
+            yield
+
+    pre_stats.start()
+    ref_gather.begin()
     weights.step(0, (0, 1, 2))
     for number in range(10, len(inputs)):
         load(number).wait()
@@ -622,8 +695,6 @@
     order_gain(r.pre_gain, gain)
     order_gain(r.post_gain, r.post_ordered)
     pre_gain, post_gain = own_gain(gain, mine), own_gain(r.post_ordered, mine)
-    together(gather.steps(), weight_steps(), (0, 1, 1, 0, 1, 1, 0, 1, 1, 0, 1, 1, 0, 1, 0))
-
     def project(m):
         rows = slice(m * TOK, m * TOK + TOK)
         for i in range(3):
@@ -655,15 +726,47 @@
                 r.mixed[at, 128 * g : 128 * g + 128] = dot(prob.astype(BF16), value).astype(BF16)
             yield
 
-    unpack_features(r.hidden_buf, 2 * SHARD, 0, r.normed, 0)
-    normalize(r.normed, r.scale, gain, 0)
-    weights.arrive(0)
-    weights.step(2, (3, 4))
-    for _ in project(0):
-        pass
-    for _ in attend(0):
-        pass
-    weights.step(3, (3, 4))
+    def fill(steps, count):
+        for _ in range(count):
+            next(steps, None)
+
+    def ref_work():
+        unpack_features(r.ref_gathered, SHARD, 0, r.normed, 0)
+        yield
+        normalize(r.normed, r.scale, gain, 0)
+        yield
+        weights.arrive(0)
+        yield from project(0)
+        yield from attend(0)
+
+    lows = HookSum(
+        r.low_terms, r.low_parts, r.low, mine, send.low_terms, recv.low_terms, send.low, recv.low
+    )
+
+    def low_work():
+        send_a()
+        pre_stats.wait()
+        rows_to_columns(r.table, [lax.rsqrt(as_row(pre_stats.total()) / WIDTH + NORM_EPS)])
+        own = r.pol_hidden[...].astype(F32) * r.table[0:TOK, 0:1] * pre_gain
+        r.own_normed[...] = own.astype(BF16)
+        yield
+        relay_a()
+        yield
+        await_a()
+        r.low_terms[...] = dot(r.own_normed[...], r.a_own[...]).astype(BF16)
+        lows.start()
+        yield
+        lows.reduce()
+        yield
+
+    low = low_work()
+    first, second, passing, work = ref_gather.steps(), pol_gather.steps(), weight_steps(), ref_work()
+    arrivals = dict(G=first, Q=second, V=passing, C=work, X=low)
+    for letter in "GGGVPGGGVQGVQGVXQGVQGVXQGQGVXQVGQGVQGCQVCQCQCCQCQXCQCV":
+        if letter == "P":
+            pol_gather.begin()
+        else:
+            fill(arrivals[letter], 1)
     weights.arrive(3)
     for _ in partial_products(r.mixed.at[0:TOK], r.w_back, r.partial):
         pass
@@ -672,13 +775,13 @@
     pol_scatter = Scatter(r.partial_pol, r.landing_pol, SHARD, send.scatter_pol, recv.scatter_pol)
 
     def policy():
-        unpack_features(r.hidden_buf, 2 * SHARD, SHARD, r.normed, TOK)
+        unpack_features(r.pol_gathered, SHARD, 0, r.normed, TOK)
         yield
         normalize(r.normed, r.scale, gain, TOK)
         yield
         yield from project(1)
         r.linear[...] = r.acc[TOK : 2 * TOK, :]
-        r.low[...] = r.acc[TOK : 2 * TOK, 512:640].astype(BF16)
+        lows.wait()
         query_factor = jnp.concatenate([r.b_query[...], jnp.zeros((RANK, 256), BF16)], axis=0)
         value_factor = jnp.concatenate([jnp.zeros((RANK, 128), BF16), r.b_value[...]], axis=0)
         r.acc[TOK : 2 * TOK, 0:256] += ADAPTER_SCALE * dot(r.low[...], query_factor)
@@ -708,18 +811,13 @@
         ref_stats.start()
         yield
 
-    def fill(steps, count):
-        for _ in range(count):
-            next(steps, None)
-
     ref_ring, policy_work, policy_steps = ref_scatter.steps(r.result.at[0]), policy(), policy_ring()
     fill(policy_work, 3)
-    for count in (2, 2, 2, 2, 2):
+    for count in (2, 2, 2, 2, 2, 0, 0, 0):
         fill(ref_ring, 1)
         fill(policy_work, count)
     for _ in policy_work:
         pass
-    fill(ref_ring, 3)
     pol_scatter.begin((0,))
     fill(ref_ring, 1)
     pol_scatter.begin((1,))
@@ -850,8 +948,7 @@
     query_factor = jnp.concatenate([r.b_query[...], jnp.zeros((RANK, 256), BF16)], axis=0)
     value_factor = jnp.concatenate([jnp.zeros((RANK, 128), BF16), r.b_value[...]], axis=0)
     hook = dot(r.grads[:, 0:256], query_factor, NT) + dot(r.grads[:, 384:512], value_factor, NT)
-    r.grads[:, 512:640] = (ADAPTER_SCALE * hook).astype(BF16)
-    r.hooks[...] = r.grads[:, 512:640]
+    r.hooks[...] = (ADAPTER_SCALE * hook).astype(BF16)
     hooks = HookSum(
         r.hooks,
         r.hook_parts,
@@ -870,47 +967,47 @@
     back_scatter = Scatter(
         r.partial_back, r.landing_back, SHARD, send.scatter_back, recv.scatter_back
     )
-    back_scatter.begin((0,))
-    hooks.reduce()
-    back_scatter.begin((1, 2, 3))
+    back_scatter.begin((0, 1))
 
     def across(i):
         return pltpu.make_async_remote_copy(
             src_ref=r.a_terms.at[pl.ds(aligned(576 * (2 * i + 1 - core), 64), 576), :],
             dst_ref=r.a_across.at[pl.ds(576 * i, 576), :],
-            send_sem=send.across.at[0],
-            recv_sem=recv.across.at[0],
+            send_sem=send.across.at[i],
+            recv_sem=recv.across.at[i],
             device_id={CORE: 1 - core},
             device_id_type=MESH,
         )
 
-    def round_y(i):
-        to = lax.rem(y + i, 4)
+    def round_y(source, target, to):
         return pltpu.make_async_remote_copy(
-            src_ref=r.a_pairs.at[pl.ds(aligned(576 * to, 64), 576), :],
-            dst_ref=r.a_round.at[pl.ds(576 * i, 576), :],
+            src_ref=source,
+            dst_ref=target,
             send_sem=send.round.at[0],
             recv_sem=recv.round.at[0],
             device_id={Y: to},
             device_id_type=MESH,
         )
 
-    def all_bytes(sent, arrived, buffer, count):
-        whole = buffer.at[pl.ds(0, 576 * count), :]
-        return pltpu.make_async_remote_copy(
-            src_ref=whole,
-            dst_ref=whole,
-            send_sem=sent.at[0],
-            recv_sem=arrived.at[0],
-            device_id={CORE: 1 - core},
-            device_id_type=MESH,
-        )
+    three = r.a_round.at[pl.ds(0, 3 * 576), :]
+    rounds = round_y(three, three, lax.rem(y + 1, 4))
+
+    def pair_up(i):
+        across(i).wait_recv()
+        rows = slice(576 * i, 576 * i + 576)
+        own = r.a_terms[pl.ds(aligned(576 * (2 * i + core), 64), 576), :].astype(F32)
+        r.a_pairs[rows, :] = (own + r.a_across[rows, :].astype(F32)).astype(BF16)
+
+        @pl.when(y != i)
+        def _():
+            place = pl.ds(aligned(576 * lax.rem(i - y + 4, 4), 64), 576)
+            round_y(r.a_pairs.at[pl.ds(576 * i, 576), :], r.a_round.at[place, :], i).start()
 
     def adapters_back():
         pull_back = jnp.sum(r.grads[...].astype(F32) * r.linear[...], axis=1, keepdims=True)
+        pull_back += jnp.sum(r.hooks[...].astype(F32) * r.low[...].astype(F32), axis=1, keepdims=True)
         row = columns_to_rows(r.table, [pull_back])[0:1]
-        row = [row[:, 128 * c : 128 * c + 128] for c in range(3)] + [jnp.zeros((5, 128), F32)]
-        r.stats_back[pl.ds(aligned(8 * mine, 8), 8), :] = jnp.concatenate(row, axis=0)
+        r.stats_back[pl.ds(aligned(8 * mine, 8), 8), :] = as_tile(row)
         stats_back.start()
         factor_terms = ADAPTER_SCALE * dot(r.low[...], r.grads[:, 0:512], TN)
         own_factor = pl.ds(aligned(64 * rank, 64), 64)
@@ -920,6 +1017,7 @@
         yield
         hooks.wait()
         hook_low = r.hook_sums[...]
+        r.summed[0] = dot(hook_low, r.a_own[...], NT)
         for q in range(4):
             at = MAIN + 128 * q
             tail = dot(r.normed[TOK : 2 * TOK, at : at + 128], hook_low, TN).astype(BF16)
@@ -929,30 +1027,28 @@
                 j = t - 4 * q
                 r.a_terms[288 * t + 256 : 288 * t + 288, :] = tail[32 * j : 32 * j + 32, :]
             across(q).start()
+            if q:
+                pair_up(q - 1)
             yield
-        all_bytes(send.across, recv.across, r.a_across, 4).wait_recv()
-        for i in range(4):
-            own = r.a_terms[pl.ds(aligned(576 * (2 * i + core), 64), 576), :].astype(F32)
-            pair = own + r.a_across[576 * i : 576 * i + 576, :].astype(F32)
-            r.a_pairs[576 * i : 576 * i + 576, :] = pair.astype(BF16)
-        for i in range(1, 4):
-            round_y(i).start()
+        pair_up(3)
         yield
 
     adapters = adapters_back()
     fill(adapters, 1)
-    together(back_scatter.steps(r.result.at[0]), adapters, (0, 0, 1, 1, 1, 1, 0, 1, 0, 0, 0, 0, 0))
+    back_scatter.begin((2,))
+    hooks.reduce()
+    back_scatter.begin((3,))
+    together(back_scatter.steps(r.result.at[0]), adapters, (0, 0, 0, 1, 1, 1, 1, 1, 0, 0, 0, 0, 0))
 
     stats_back.wait()
-    row = stats_back.total()
-    rows_to_columns(r.table, [jnp.concatenate([row[c : c + 1] for c in range(3)], axis=1)])
+    rows_to_columns(r.table, [as_row(stats_back.total())])
     unpack_result(r.result.at[0], 0, r.summed.at[1])
     pre_scale = r.scale[TOK : 2 * TOK, 0:1]
     shrink_back = pre_scale * pre_scale * r.table[0:TOK, 0:1] / WIDTH
     grad_result = r.coefficient[0:TOK, 0:1] * r.readout[...].astype(F32)
     hidden = r.pol_hidden[...].astype(F32)
     r.grad_hidden[...] = (
-        grad_result + pre_scale * pre_gain * r.summed[1] - hidden * shrink_back
+        grad_result + pre_scale * pre_gain * (r.summed[1] + r.summed[0]) - hidden * shrink_back
     ).astype(BF16)
     store(3).start()
     factors.wait()
@@ -962,17 +1058,19 @@
     store(5).start()
     store(6).start()
     whole = r.a_pairs[pl.ds(aligned(576 * y, 64), 576), :].astype(F32)
-    all_bytes(send.round, recv.round, r.a_round, 3).wait_recv()
+    rounds.wait_recv()
     for i in range(1, 4):
         whole = whole + r.a_round[576 * i : 576 * i + 576, :].astype(F32)
     r.grad_a[...] = whole
     store(4).start()
-    for ring in (gather, weights, ref_scatter, pol_scatter, back_gather, back_scatter):
+    drain_a()
+    for ring in (ref_gather, pol_gather, weights, ref_scatter, pol_scatter, back_gather, back_scatter):
         ring.drain()
-    for exchange in (ref_stats, pol_stats, scores, hooks, stats_back, factors):
+    for exchange in (pre_stats, ref_stats, pol_stats, scores, lows, hooks, stats_back, factors):
         exchange.drain()
-    all_bytes(send.across, recv.across, r.a_across, 4).wait_send()
-    all_bytes(send.round, recv.round, r.a_round, 3).wait_send()
+    for i in range(4):
+        across(i).wait_send()
+    rounds.wait_send()
     for number in range(len(outputs)):
         store(number).wait()
 

time: 145 us -> 140 us (0.966)
  Pallas kernels: 144 us -> 139 us
    pallas_call x1, Pallas kernels: 141 us -> 137 us  [body(): pl.pallas_call(step_body, out_shape=tuple((jax.ShapeDtypeStruct(*kind) fo...]
where the time goes in v4:
time: 140 us
  Pallas kernels  139 us (99%)
    pallas_call x1, Pallas kernels, body(): pl.pallas_call(step_body, out_shape=tuple((jax.ShapeDtypeStruct(*kind) fo...  137 us

profile of v4, /device:TPU:0, one launch (start us, length us, event | category | flops | bytes accessed | tf_op | source)
XLA Modules:
  0.0 140.1 jit_solution(15471478997073044421)
XLA Ops:
  0.6 137.1 %shard_map.216 = (bf16[288,288]{1,0:T(8,128)(2,1)}, bf16[288,288]{1,0:T(8,128)(2,1)}, f32[8,128]{1,0:T(8,128)}, bf16[288,288]{1,0:T(8,128)(2,1)}, f32[576,128]{1...) custom-call(s32[3]{0:T(128)} %refs_0_.1, s32[24]{0:T(128)} %refs_1_.1, bf16[288,288]{1,0:T(8,128)(2,1)} %refs_2_.1, ...), custom_call_target="tpu_custom_call" | custom-call | tf_op jit(solution)/shard_map/pallas_call | solution.py:1161
  137.8 2.3 %shard_map.217 = (bf16[288,288]{1,0:T(8,128)(2,1)}, bf16[288,288]{1,0:T(8,128)(2,1)}, f32[1,1]{1,0:T(1,128)}, bf16[288,288]{1,0:T(8,128)(2,1)}, f32[576,128]{1,0...) custom-call(bf16[288,288]{1,0:T(8,128)(2,1)} %get-tuple-element.21.refs_0_, bf16[288,288]{1,0:T(8,128)(2,1)} %get-tuple-element.22.refs_1_, ...), custom_call_target="tpu_custom_call" | custom-call | tf_op jit(solution)/shard_map/pallas_call | solution.py:1194

commit v5 on v4

--- a/solution.py
+++ b/solution.py
@@ -140,6 +140,49 @@
         yield
         for j, s in ((1, 0), (3, 0), (0, 1), (2, 0), (1, 1), (3, 1), (0, 2), (2, 1), (1, 2), (3, 2), (2, 2)):
             self.await_second(j, s)
+            yield
+
+
+class ShortGather(Gather):
+    def second(self, k, j, number):
+        piece = self.piece(k, j, 1 if number == 1 else 0)
+        return self.remote(piece, piece, 3 + 3 * j + number, self.next_on(k, True, number == 2))
+
+    def begin(self):
+        for k in range(4):
+            self.first(k, 0).start()
+            self.first(k, 2).start()
+        for k in range(4):
+            self.second(k, 0, 0).start()
+            self.second(k, 0, 2).start()
+
+    def await_first(self, number):
+        self.arrived(number)
+        for k in range(4):
+            if number == 0:
+                self.first(k, 1).start()
+            self.second(k, number + 1, 0).start()
+            self.second(k, number + 1, 2).start()
+
+    def await_second(self, j, number):
+        self.arrived(3 + 3 * j + number)
+        if number == 0:
+            for k in range(4):
+                self.second(k, j, 1).start()
+
+    def steps(self):
+        self.await_first(0)
+        yield
+        self.await_first(2)
+        yield
+        self.await_second(0, 0)
+        yield
+        self.await_first(1)
+        yield
+        for j, number in (
+            (0, 2), (1, 0), (3, 0), (2, 0), (1, 2), (3, 2), (0, 1), (1, 1), (2, 2), (3, 1), (2, 1)
+        ):
+            self.await_second(j, number)
             yield
 
 
@@ -199,6 +242,63 @@
         yield
 
 
+class ShortScatter(Scatter):
+    def outer(self, k, j, number):
+        piece = self.piece(k, ORDER[j], (2, 3, 1)[number])
+        slot = self.slot(k, 3 * j + number)
+        return self.remote(piece, slot, 3 * j + number, self.next_on(k, True, number == 2))
+
+    def hand_on(self, j, number):
+        for k in range(4):
+            self.outer(k, j, number).start()
+
+    def close(self, j):
+        self.arrived(3 * j + 1)
+        self.arrived(3 * j + 2)
+        for k in range(4):
+            piece = self.piece(k, ORDER[j], 0)
+            value = piece[...].astype(F32)
+            for number in (1, 2):
+                value = value + self.slot(k, 3 * j + number)[...].astype(F32)
+            piece[...] = value.astype(BF16)
+
+    def steps(self, result):
+        for j in range(4):
+            self.arrived(3 * j)
+            for k in range(4):
+                self.add(k, 3 * j, ORDER[j], 3)
+                self.outer(k, j, 1).start()
+            if j < 2:
+                self.hand_on(j, 2)
+            yield
+        self.close(0)
+        for k in range(4):
+            self.inner(k, 12).start()
+        self.hand_on(2, 2)
+        self.hand_on(3, 2)
+        yield
+        self.close(1)
+        for k in range(4):
+            self.inner(k, 14).start()
+        yield
+        self.close(2)
+        self.arrived(12)
+        for k in range(4):
+            self.add(k, 12, 3, 0)
+            self.inner(k, 13).start()
+        yield
+        self.close(3)
+        yield
+        self.arrived(14)
+        self.arrived(13)
+        for k in range(4):
+            own = self.piece(k, 0, 0)[...].astype(F32)
+            for number in (14, 13):
+                own = own + self.slot(k, number)[...].astype(F32)
+            result[pl.ds(self.starts[k], self.sizes[k]), :] = own
+        yield
+
+
 class Weights:
     def __init__(self, w_in, w_back, y_send, y_recv, d_send, d_recv):
         self.w_in, self.w_back = w_in, w_back
@@ -298,10 +398,10 @@
 
 
 class HookSum:
-    def __init__(self, terms, parts, sums, me, send_parts, recv_parts, send_sums, recv_sums):
+    def __init__(self, terms, parts, sums, me, send_parts, recv_parts, send_sums, recv_sums, narrow):
         self.terms, self.parts, self.sums, self.me = terms, parts, sums, me
         self.there = Exchange(parts, 32, 16, me, in_tensor, send_parts, recv_parts)
-        self.home = Exchange(parts, 32, 16, me, in_tensor, send_sums, recv_sums)
+        self.home = Exchange(narrow, 32, 16, me, in_tensor, send_sums, recv_sums)
         self.owner = me < OWNERS
 
     def start(self):
@@ -740,7 +840,7 @@
         yield from attend(0)
 
     lows = HookSum(
-        r.low_terms, r.low_parts, r.low, mine, send.low_terms, recv.low_terms, send.low, recv.low
+        r.low_terms, r.low_parts, r.low, mine, send.low_terms, recv.low_terms, send.low, recv.low, r.hook_parts
     )
 
     def low_work():
@@ -772,7 +872,7 @@
         pass
     ref_scatter = Scatter(r.partial, r.landing, SHARD, send.scatter_ref, recv.scatter_ref)
     ref_scatter.begin()
-    pol_scatter = Scatter(r.partial_pol, r.landing_pol, SHARD, send.scatter_pol, recv.scatter_pol)
+    pol_scatter = ShortScatter(r.partial_pol, r.landing_pol, SHARD, send.scatter_pol, recv.scatter_pol)
 
     def policy():
         unpack_features(r.pol_gathered, SHARD, 0, r.normed, TOK)
@@ -826,7 +926,7 @@
     for count in (2, 2, 1):
         fill(ref_ring, 1)
         fill(policy_steps, count)
-    together(policy_steps, after_ref(), (1,) + (0,) * 12)
+    together(policy_steps, after_ref(), (1,) + (0,) * 8)
     columns = columns_to_rows(r.table, token_sums(1, r.pol_hidden))
     packed = [columns[k : k + 1, 128 * c : 128 * c + 128] for k in range(3) for c in range(3)]
     packed = jnp.concatenate(packed + [jnp.zeros((7, 128), F32)], axis=0)
@@ -842,7 +942,7 @@
     readout = r.readout[...].astype(F32)
     bare = r.table[0:TOK, 0:1] * post_gain * readout - r.summed[1] * r.table[0:TOK, 1:2]
     pack_hidden(bare, r.grad_buf, mine * SHARD)
-    back_gather = Gather(r.grad_buf, SHARD, send.gather_back, recv.gather_back)
+    back_gather = ShortGather(r.grad_buf, SHARD, send.gather_back, recv.gather_back)
     back_gather.begin()
 
     lane = lax.broadcasted_iota(jnp.int32, (1, 384), 1)
@@ -958,13 +1058,14 @@
         recv.hooks,
         send.hook_sums,
         recv.hook_sums,
+        r.hook_parts,
     )
     hooks.start()
     stats_back = Exchange(r.stats_back, 8, 16, mine, in_tensor, send.stats_back, recv.stats_back)
     factors = Exchange(r.factors, 64, 8, rank, in_data, send.factors, recv.factors)
     for _ in partial_products(r.grads, r.w_in, r.partial_back):
         pass
-    back_scatter = Scatter(
+    back_scatter = ShortScatter(
         r.partial_back, r.landing_back, SHARD, send.scatter_back, recv.scatter_back
     )
     back_scatter.begin((0, 1))
@@ -1038,7 +1139,7 @@
     back_scatter.begin((2,))
     hooks.reduce()
     back_scatter.begin((3,))
-    together(back_scatter.steps(r.result.at[0]), adapters, (0, 0, 0, 1, 1, 1, 1, 1, 0, 0, 0, 0, 0))
+    together(back_scatter.steps(r.result.at[0]), adapters, (0, 0, 0, 2, 2, 1, 0, 0, 0))
 
     stats_back.wait()
     rows_to_columns(r.table, [as_row(stats_back.total())])

time: 140 us -> 136 us (0.971)
  Pallas kernels: 139 us -> 135 us
    pallas_call x1, Pallas kernels: 137 us -> 132 us  [body(): pl.pallas_call(step_body, out_shape=tuple((jax.ShapeDtypeStruct(*kind) fo...]
where the time goes in v5:
time: 136 us; the launch traced here: 135 us
  Pallas kernels  135 us (99%)
    pallas_call x1, Pallas kernels, body(): pl.pallas_call(step_body, out_shape=tuple((jax.ShapeDtypeStruct(*kind) fo...  132 us

profile of v5, /device:TPU:0, one launch (start us, length us, event | category | flops | bytes accessed | tf_op | source)
XLA Modules:
  0.0 135.4 jit_solution(6349416218742509420)
XLA Ops:
  0.6 132.5 %shard_map.216 = (bf16[288,288]{1,0:T(8,128)(2,1)}, bf16[288,288]{1,0:T(8,128)(2,1)}, f32[8,128]{1,0:T(8,128)}, bf16[288,288]{1,0:T(8,128)(2,1)}, f32[576,128]{1...) custom-call(s32[3]{0:T(128)} %refs_0_.1, s32[24]{0:T(128)} %refs_1_.1, bf16[288,288]{1,0:T(8,128)(2,1)} %refs_2_.1, ...), custom_call_target="tpu_custom_call" | custom-call | tf_op jit(solution)/shard_map/pallas_call | solution.py:1262
  133.1 2.3 %shard_map.217 = (bf16[288,288]{1,0:T(8,128)(2,1)}, bf16[288,288]{1,0:T(8,128)(2,1)}, f32[1,1]{1,0:T(1,128)}, bf16[288,288]{1,0:T(8,128)(2,1)}, f32[576,128]{1,0...) custom-call(bf16[288,288]{1,0:T(8,128)(2,1)} %get-tuple-element.21.refs_0_, bf16[288,288]{1,0:T(8,128)(2,1)} %get-tuple-element.22.refs_1_, ...), custom_call_target="tpu_custom_call" | custom-call | tf_op jit(solution)/shard_map/pallas_call | solution.py:1295

commit v6 on v5

--- a/solution.py
+++ b/solution.py
@@ -870,7 +870,7 @@
     weights.arrive(3)
     for _ in partial_products(r.mixed.at[0:TOK], r.w_back, r.partial):
         pass
-    ref_scatter = Scatter(r.partial, r.landing, SHARD, send.scatter_ref, recv.scatter_ref)
+    ref_scatter = ShortScatter(r.partial, r.landing, SHARD, send.scatter_ref, recv.scatter_ref)
     ref_scatter.begin()
     pol_scatter = ShortScatter(r.partial_pol, r.landing_pol, SHARD, send.scatter_pol, recv.scatter_pol)
 
@@ -913,7 +913,7 @@
 
     ref_ring, policy_work, policy_steps = ref_scatter.steps(r.result.at[0]), policy(), policy_ring()
     fill(policy_work, 3)
-    for count in (2, 2, 2, 2, 2, 0, 0, 0):
+    for count in (2, 2, 2, 2, 2):
         fill(ref_ring, 1)
         fill(policy_work, count)
     for _ in policy_work:
@@ -923,7 +923,7 @@
     pol_scatter.begin((1,))
     fill(ref_ring, 1)
     pol_scatter.begin((2, 3))
-    for count in (2, 2, 1):
+    for count in (2, 2):
         fill(ref_ring, 1)
         fill(policy_steps, count)
     together(policy_steps, after_ref(), (1,) + (0,) * 8)

time: 136 us -> 136 us (level)
  no operation moved by 1% of the time
where the time goes in v6:
time: 136 us; the launch traced here: 135 us
  Pallas kernels  134 us (99%)
    pallas_call x1, Pallas kernels, body(): pl.pallas_call(step_body, out_shape=tuple((jax.ShapeDtypeStruct(*kind) fo...  132 us

profile of v6, /device:TPU:0, one launch (start us, length us, event | category | flops | bytes accessed | tf_op | source)
XLA Modules:
  0.0 134.9 jit_solution(3914855765850755293)
XLA Ops:
  0.6 132.0 %shard_map.216 = (bf16[288,288]{1,0:T(8,128)(2,1)}, bf16[288,288]{1,0:T(8,128)(2,1)}, f32[8,128]{1,0:T(8,128)}, bf16[288,288]{1,0:T(8,128)(2,1)}, f32[576,128]{1...) custom-call(s32[3]{0:T(128)} %refs_0_.1, s32[24]{0:T(128)} %refs_1_.1, bf16[288,288]{1,0:T(8,128)(2,1)} %refs_2_.1, ...), custom_call_target="tpu_custom_call" | custom-call | tf_op jit(solution)/shard_map/pallas_call | solution.py:1262
  132.6 2.3 %shard_map.217 = (bf16[288,288]{1,0:T(8,128)(2,1)}, bf16[288,288]{1,0:T(8,128)(2,1)}, f32[1,1]{1,0:T(1,128)}, bf16[288,288]{1,0:T(8,128)(2,1)}, f32[576,128]{1,0...) custom-call(bf16[288,288]{1,0:T(8,128)(2,1)} %get-tuple-element.21.refs_0_, bf16[288,288]{1,0:T(8,128)(2,1)} %get-tuple-element.22.refs_1_, ...), custom_call_target="tpu_custom_call" | custom-call | tf_op jit(solution)/shard_map/pallas_call | solution.py:1295
